TPU v7x, 16 devices: a 4x2x1 block of a 4x4x8 slice. The times are simulated.
16 devices in a mesh: dp: 2 (over y, z), sp: 8 (over x, core).
Axes of the slice: x: 4, y: 2, z: 1, core: 2. Of those that a mesh axis runs over, the one named last changes fastest.
The devices are a block of a 4x4x8 slice.
Arguments:
- x_in: bfloat16 [4, 3072, 2048], P('dp', 'sp'), parts along dimension 0
- d_out: bfloat16 [4, 3072, 2048], P('dp', 'sp'), parts along dimension 0
- gain: float32 [2048], replicated
- w_q: bfloat16 [2048, 32, 64], replicated
- w_k: bfloat16 [2048, 8, 64], replicated
- w_v: bfloat16 [2048, 8, 64], replicated
- w_o: bfloat16 [32, 64, 2048], replicated
Outputs:
- output 1: bfloat16 [4, 3072, 2048], P('dp', 'sp'), parts along dimension 0
- output 2: bfloat16 [4, 3072, 2048], P('dp', 'sp'), parts along dimension 0
- output 3: float32 [4096, 32, 64], P('dp'), parts along dimension 0
- output 4: float32 [4096, 8, 64], P('dp'), parts along dimension 0
- output 5: float32 [4096, 8, 64], P('dp'), parts along dimension 0
- output 6: float32 [64, 64, 2048], P('dp'), parts along dimension 0
- output 7: float32 [4096], P('dp'), parts along dimension 0
There are 2 independent parts. A program takes and returns all parts, laid end to end along the dimension named above; an argument that names none is the same for every part.
All inputs are finite; a program needn't handle non-finite values.
Results may differ from a plain program's by a relative error of at most 0.0124358.
Values are sent between devices in bfloat16 or wider.
A program may use at most 768 MiB of HBM per device.

v0:
```python
import math
import jax
import jax.numpy as jnp
from jax import lax
from jax.sharding import PartitionSpec as P

ROPE_BASE = 1000000.0
NORM_EPS = 1e-5


def rope_tables(positions, head_dim):
    half = head_dim // 2
    inv_freq = ROPE_BASE ** (-2.0 * jnp.arange(half, dtype=jnp.float32) / head_dim)
    angle = positions[:, None] * inv_freq[None, :]
    return jnp.cos(angle), jnp.sin(angle)


def rotate(t_val, cos_t, sin_t):
    half = t_val.shape[-1] // 2
    first = t_val[..., :half]
    second = t_val[..., half:]
    cos_b = cos_t[:, None, :]
    sin_b = sin_t[:, None, :]
    return jnp.concatenate([first * cos_b - second * sin_b, second * cos_b + first * sin_b], axis=-1)


def rotate_back(grad_val, cos_t, sin_t):
    half = grad_val.shape[-1] // 2
    first = grad_val[..., :half]
    second = grad_val[..., half:]
    cos_b = cos_t[:, None, :]
    sin_b = sin_t[:, None, :]
    return jnp.concatenate([first * cos_b + second * sin_b, second * cos_b - first * sin_b], axis=-1)


def norm_forward(x_local, gain):
    x_f32 = x_local.astype(jnp.float32)
    inv_rms = lax.rsqrt(jnp.mean(x_f32 * x_f32, axis=-1, keepdims=True) + NORM_EPS)
    x_hat = x_f32 * inv_rms
    return x_hat, inv_rms, (x_hat * gain).astype(jnp.bfloat16)


def norm_backward(d_normed, x_hat, inv_rms, gain):
    d_hat = d_normed * gain
    return inv_rms * (d_hat - x_hat * jnp.mean(d_hat * x_hat, axis=-1, keepdims=True))


def project(normed, w_q, w_k, w_v, cos_t, sin_t):
    q_lin = jnp.einsum('bsd,dhe->bshe', normed, w_q, preferred_element_type=jnp.float32)
    k_lin = jnp.einsum('bsd,dhe->bshe', normed, w_k, preferred_element_type=jnp.float32)
    v_lin = jnp.einsum('bsd,dhe->bshe', normed, w_v, preferred_element_type=jnp.float32)
    return rotate(q_lin, cos_t, sin_t).astype(jnp.bfloat16), rotate(k_lin, cos_t, sin_t).astype(jnp.bfloat16), v_lin.astype(jnp.bfloat16)


def project_back(dq_lin, dk_lin, dv_val, w_q, w_k, w_v):
    d_q = jnp.einsum('bshe,dhe->bsd', dq_lin, w_q, preferred_element_type=jnp.float32)
    d_k = jnp.einsum('bshe,dhe->bsd', dk_lin, w_k, preferred_element_type=jnp.float32)
    d_v = jnp.einsum('bshe,dhe->bsd', dv_val, w_v, preferred_element_type=jnp.float32)
    return (d_q + d_k + d_v).astype(jnp.bfloat16)


def block_length(seq_q, num_q):
    return math.gcd(seq_q, max(64, 8192 // num_q))


def attention_forward(q_heads, k_heads, v_heads, q_offset):
    batch, seq_q, num_q, head_dim = q_heads.shape
    seq_k, num_kv = k_heads.shape[1], k_heads.shape[2]
    group = num_q // num_kv
    block_len = block_length(seq_q, num_q)
    scale = head_dim ** -0.5
    q_grouped = q_heads.reshape(batch, seq_q, num_kv, group, head_dim)
    key_pos = jnp.arange(seq_k)

    def one_block(block_idx):
        start = block_idx * block_len
        q_rows = lax.dynamic_slice_in_dim(q_grouped, start, block_len, axis=1)
        scores = jnp.einsum('bqkgd,btkd->bkgqt', q_rows, k_heads, preferred_element_type=jnp.float32) * scale
        q_pos = q_offset + start + jnp.arange(block_len)
        scores = jnp.where(key_pos[None, :] <= q_pos[:, None], scores, -1e30)
        row_max = jnp.max(scores, axis=-1, keepdims=True)
        exp_scores = jnp.exp(scores - row_max)
        row_sum = jnp.sum(exp_scores, axis=-1, keepdims=True)
        attn_weights = (exp_scores / row_sum).astype(jnp.bfloat16)
        out_rows = jnp.einsum('bkgqt,btkd->bqkgd', attn_weights, v_heads, preferred_element_type=jnp.float32)
        return out_rows.astype(jnp.bfloat16), row_max + jnp.log(row_sum)

    out_blocks, log_sum = lax.map(one_block, jnp.arange(seq_q // block_len))
    return jnp.moveaxis(out_blocks, 0, 1).reshape(batch, seq_q, num_q, head_dim), log_sum


def attention_backward(q_heads, k_heads, v_heads, d_heads, log_sum, q_offset):
    batch, seq_q, num_q, head_dim = q_heads.shape
    seq_k, num_kv = k_heads.shape[1], k_heads.shape[2]
    group = num_q // num_kv
    block_len = block_length(seq_q, num_q)
    num_blocks = seq_q // block_len
    scale = head_dim ** -0.5
    q_grouped = q_heads.reshape(batch, seq_q, num_kv, group, head_dim)
    d_grouped = d_heads.reshape(batch, seq_q, num_kv, group, head_dim)
    key_pos = jnp.arange(seq_k)

    def one_block(carry, inputs):
        dk_acc, dv_acc = carry
        block_idx, lse_rows = inputs
        start = block_idx * block_len
        q_rows = lax.dynamic_slice_in_dim(q_grouped, start, block_len, axis=1)
        d_rows = lax.dynamic_slice_in_dim(d_grouped, start, block_len, axis=1)
        scores = jnp.einsum('bqkgd,btkd->bkgqt', q_rows, k_heads, preferred_element_type=jnp.float32) * scale
        q_pos = q_offset + start + jnp.arange(block_len)
        scores = jnp.where(key_pos[None, :] <= q_pos[:, None], scores, -1e30)
        attn_weights = jnp.exp(scores - lse_rows)
        d_weights = jnp.einsum('bqkgd,btkd->bkgqt', d_rows, v_heads, preferred_element_type=jnp.float32).astype(jnp.bfloat16)
        delta = jnp.sum(attn_weights * d_weights, axis=-1, keepdims=True)
        d_scores = (attn_weights * (d_weights - delta) * scale).astype(jnp.bfloat16)
        dq_rows = jnp.einsum('bkgqt,btkd->bqkgd', d_scores, k_heads, preferred_element_type=jnp.float32).astype(jnp.bfloat16)
        dk_acc = dk_acc + jnp.einsum('bkgqt,bqkgd->btkd', d_scores, q_rows, preferred_element_type=jnp.float32)
        dv_acc = dv_acc + jnp.einsum('bkgqt,bqkgd->btkd', attn_weights.astype(jnp.bfloat16), d_rows, preferred_element_type=jnp.float32)
        return (dk_acc, dv_acc), dq_rows

    zeros = jnp.zeros(k_heads.shape, jnp.float32)
    (dk_acc, dv_acc), dq_blocks = lax.scan(one_block, (zeros, zeros), (jnp.arange(num_blocks), log_sum))
    return jnp.moveaxis(dq_blocks, 0, 1).reshape(batch, seq_q, num_q, head_dim), dk_acc, dv_acc


def solution(mesh):
    seq_par = mesh.shape['sp']

    def local_step(x_local, dy_local, gain, w_q, w_k, w_v, w_o):
        batch, seq_loc, d_model = x_local.shape
        num_kv, head_dim = w_k.shape[1], w_k.shape[2]
        spread = max(num_kv, seq_par) // num_kv
        offset = lax.axis_index('sp') * seq_loc
        cos_t, sin_t = rope_tables((offset + jnp.arange(seq_loc)).astype(jnp.float32), head_dim)
        x_hat, inv_rms, normed = norm_forward(x_local, gain)
        q_rot, k_rot, v_val = project(normed, w_q, w_k, w_v, cos_t, sin_t)
        k_send = k_rot
        v_send = v_val
        if spread > 1:
            k_send = jnp.repeat(k_rot, spread, axis=2)
            v_send = jnp.repeat(v_val, spread, axis=2)
        q_heads = lax.all_to_all(q_rot, 'sp', 2, 1, tiled=True)
        k_heads = lax.all_to_all(k_send, 'sp', 2, 1, tiled=True)
        v_heads = lax.all_to_all(v_send, 'sp', 2, 1, tiled=True)
        o_heads, log_sum = attention_forward(q_heads, k_heads, v_heads, 0)
        o_local = lax.all_to_all(o_heads, 'sp', 1, 2, tiled=True)
        y_proj = jnp.einsum('bshe,hed->bsd', o_local, w_o, preferred_element_type=jnp.float32)
        y_out = (x_local.astype(jnp.float32) + y_proj).astype(jnp.bfloat16)
        d_o = jnp.einsum('bsd,hed->bshe', dy_local, w_o, preferred_element_type=jnp.float32).astype(jnp.bfloat16)
        d_wo = jnp.einsum('bshe,bsd->hed', o_local, dy_local, preferred_element_type=jnp.float32)
        d_o_heads = lax.all_to_all(d_o, 'sp', 2, 1, tiled=True)
        dq_heads, dk_heads, dv_heads = attention_backward(q_heads, k_heads, v_heads, d_o_heads, log_sum, 0)
        dq_local = lax.all_to_all(dq_heads, 'sp', 1, 2, tiled=True)
        dk_local = lax.all_to_all(dk_heads.astype(jnp.bfloat16), 'sp', 1, 2, tiled=True)
        dv_local = lax.all_to_all(dv_heads.astype(jnp.bfloat16), 'sp', 1, 2, tiled=True)
        if spread > 1:
            dk_local = dk_local.reshape(batch, seq_loc, num_kv, spread, head_dim).sum(axis=3, dtype=jnp.float32).astype(jnp.bfloat16)
            dv_local = dv_local.reshape(batch, seq_loc, num_kv, spread, head_dim).sum(axis=3, dtype=jnp.float32).astype(jnp.bfloat16)
        dq_lin = rotate_back(dq_local, cos_t, sin_t).astype(jnp.bfloat16)
        dk_lin = rotate_back(dk_local, cos_t, sin_t).astype(jnp.bfloat16)
        d_normed = project_back(dq_lin, dk_lin, dv_local, w_q, w_k, w_v)
        d_wq = jnp.einsum('bsd,bshe->dhe', normed, dq_lin, preferred_element_type=jnp.float32)
        d_wk = jnp.einsum('bsd,bshe->dhe', normed, dk_lin, preferred_element_type=jnp.float32)
        d_wv = jnp.einsum('bsd,bshe->dhe', normed, dv_local, preferred_element_type=jnp.float32)
        d_x_norm = norm_backward(d_normed, x_hat, inv_rms, gain)
        d_gain = jnp.sum(d_normed * x_hat, axis=(0, 1))
        d_x = (dy_local.astype(jnp.float32) + d_x_norm).astype(jnp.bfloat16)
        d_wq, d_wk, d_wv, d_wo, d_gain = lax.psum((d_wq, d_wk, d_wv, d_wo, d_gain), 'sp')
        return y_out, d_x, d_wq, d_wk, d_wv, d_wo, d_gain

    specs_in = (P('dp', 'sp', None), P('dp', 'sp', None), P(None), P(None, None, None), P(None, None, None), P(None, None, None), P(None, None, None))
    specs_out = (P('dp', 'sp', None), P('dp', 'sp', None), P('dp', None, None), P('dp', None, None), P('dp', None, None), P('dp', None, None), P('dp'))
    return jax.shard_map(local_step, mesh=mesh, in_specs=specs_in, out_specs=specs_out, check_vma=False)
```

profile of v0, /device:TPU:113, one launch (start us, length us, event | category | flops | bytes accessed | tf_op | source)
XLA Modules:
  0.0 1756.9 jit_solution(18406644570952059800)
XLA Ops:
  72.9 22.7 %all-to-all-done = bf16[2,384,32,64]{1,3,0,2:T(8,128)(2,1)} async-done(((bf16[2,384,32,64]{1,3,0,2:T(8,128)(2,1)}), bf16[2,384,32,64]{1,3,0,2:T(8,128)(2,1)}, u32[]{:S(2)}, u32[]{:S(2)}) %all-to-all-start) | async-done | bytes 3145760 | tf_op jit(solution)/shard_map/all_to_all | solution.py:142
  115.0 338.5 %while.28 = (s32[]{:T(128)}, bf16[3,2,1024,1,4,64]{2,5,4,1,3,0:T(8,128)(2,1)}, f32[3,2,1,4,1024,1]{4,3,1,5,2,0:T(4,128)}, s32[3]{0:T(128)}, bf16[2,3072,1,4,64]{...) while((s32[]{:T(128)}, ...), condition=%wide.region_4.5_spmd.clone, body=%wide.region_1.4_spmd.clone.sunk | while | flops 6748103680 | bytes 324805856 | solution.py:88
  121.3 36.3 %fusion.156 = (f32[2,4,1024]{2,1,0:T(4,128)S(1)}, f32[2,1024,4,3072]{3,1,2,0:T(8,128)}) fusion(pred[1024,3072]{1,0:T(8,128)(4,1)} %iota_compare_fusion.4, bf16[2,3072,1,64]{1,3,0,2:T(8,128)(2,1)S(1)} %get-tuple-element.359, bf16[2,3072,1,4,64]{1,4,3,0,2:T(8,128)(2,1)} %get-tuple-element.358, s32[]{:T(128)S(6)} %select_n.47), kind=kOutput, calls=%fused_computation.6.clone.1 | convolution fusion | flops 3296714752 | bytes 105676800 | tf_op jit(solution)/shard_map/while/body/eval_jaxpr/bqkgd,btkd->bkgqt/dot_general | solution.py:78
  157.6 32.4 %fusion.157 = f32[2,4,1024]{2,1,0:T(4,128)S(1)} fusion(f32[2,1024,4,3072]{3,1,2,0:T(8,128)} %get-tuple-element.318, f32[2,4,1024]{2,1,0:T(4,128)S(1)} %get-tuple-element.319, pred[1024,3072]{1,0:T(8,128)(4,1)} %iota_compare_fusion.4), kind=kLoop, calls=%fused_computation.5.clone.1 | loop fusion | flops 100655104 | bytes 103874560 | tf_op jit(solution)/shard_map/while/body/eval_jaxpr/reduce_sum | solution.py:83
  190.6 37.3 %fusion.158 = bf16[3,2,1024,1,4,64]{2,5,4,1,3,0:T(8,128)(2,1)} fusion(bf16[3,2,1024,1,4,64]{2,5,4,1,3,0:T(8,128)(2,1)} %get-tuple-element.344, s32[]{:T(128)} %get-tuple-element.343, f32[2,4,1024]{2,1,0:T(4,128)S(1)} %fusion.157, f32[2,4,1024]{2,1,0:T(4,128)S(1)} %get-tuple-element.319, f32[2,1024,4,3072]{3,1,2,0:T(8,128)} %get-tuple-element.318, ...), kind=kOutput, calls=%fused_computation.12.clone.1 | convolution fusion | flops 3347578880 | bytes 105710080 | tf_op jit(solution)/shard_map/while/body/eval_jaxpr/bkgqt,btkd->bqkgd/dot_general | solution.py:85
  234.0 36.3 %fusion.156 = (f32[2,4,1024]{2,1,0:T(4,128)S(1)}, f32[2,1024,4,3072]{3,1,2,0:T(8,128)}) fusion(pred[1024,3072]{1,0:T(8,128)(4,1)} %iota_compare_fusion.4, bf16[2,3072,1,64]{1,3,0,2:T(8,128)(2,1)S(1)} %get-tuple-element.359, bf16[2,3072,1,4,64]{1,4,3,0,2:T(8,128)(2,1)} %get-tuple-element.358, s32[]{:T(128)S(6)} %select_n.47), kind=kOutput, calls=%fused_computation.6.clone.1 | convolution fusion | flops 3296714752 | bytes 105676800 | tf_op jit(solution)/shard_map/while/body/eval_jaxpr/bqkgd,btkd->bkgqt/dot_general | solution.py:78
  270.4 32.4 %fusion.157 = f32[2,4,1024]{2,1,0:T(4,128)S(1)} fusion(f32[2,1024,4,3072]{3,1,2,0:T(8,128)} %get-tuple-element.318, f32[2,4,1024]{2,1,0:T(4,128)S(1)} %get-tuple-element.319, pred[1024,3072]{1,0:T(8,128)(4,1)} %iota_compare_fusion.4), kind=kLoop, calls=%fused_computation.5.clone.1 | loop fusion | flops 100655104 | bytes 103874560 | tf_op jit(solution)/shard_map/while/body/eval_jaxpr/reduce_sum | solution.py:83
  303.4 37.3 %fusion.158 = bf16[3,2,1024,1,4,64]{2,5,4,1,3,0:T(8,128)(2,1)} fusion(bf16[3,2,1024,1,4,64]{2,5,4,1,3,0:T(8,128)(2,1)} %get-tuple-element.344, s32[]{:T(128)} %get-tuple-element.343, f32[2,4,1024]{2,1,0:T(4,128)S(1)} %fusion.157, f32[2,4,1024]{2,1,0:T(4,128)S(1)} %get-tuple-element.319, f32[2,1024,4,3072]{3,1,2,0:T(8,128)} %get-tuple-element.318, ...), kind=kOutput, calls=%fused_computation.12.clone.1 | convolution fusion | flops 3347578880 | bytes 105710080 | tf_op jit(solution)/shard_map/while/body/eval_jaxpr/bkgqt,btkd->bqkgd/dot_general | solution.py:85
  346.8 36.3 %fusion.156 = (f32[2,4,1024]{2,1,0:T(4,128)S(1)}, f32[2,1024,4,3072]{3,1,2,0:T(8,128)}) fusion(pred[1024,3072]{1,0:T(8,128)(4,1)} %iota_compare_fusion.4, bf16[2,3072,1,64]{1,3,0,2:T(8,128)(2,1)S(1)} %get-tuple-element.359, bf16[2,3072,1,4,64]{1,4,3,0,2:T(8,128)(2,1)} %get-tuple-element.358, s32[]{:T(128)S(6)} %select_n.47), kind=kOutput, calls=%fused_computation.6.clone.1 | convolution fusion | flops 3296714752 | bytes 105676800 | tf_op jit(solution)/shard_map/while/body/eval_jaxpr/bqkgd,btkd->bkgqt/dot_general | solution.py:78
  383.2 32.4 %fusion.157 = f32[2,4,1024]{2,1,0:T(4,128)S(1)} fusion(f32[2,1024,4,3072]{3,1,2,0:T(8,128)} %get-tuple-element.318, f32[2,4,1024]{2,1,0:T(4,128)S(1)} %get-tuple-element.319, pred[1024,3072]{1,0:T(8,128)(4,1)} %iota_compare_fusion.4), kind=kLoop, calls=%fused_computation.5.clone.1 | loop fusion | flops 100655104 | bytes 103874560 | tf_op jit(solution)/shard_map/while/body/eval_jaxpr/reduce_sum | solution.py:83
  416.2 37.3 %fusion.158 = bf16[3,2,1024,1,4,64]{2,5,4,1,3,0:T(8,128)(2,1)} fusion(bf16[3,2,1024,1,4,64]{2,5,4,1,3,0:T(8,128)(2,1)} %get-tuple-element.344, s32[]{:T(128)} %get-tuple-element.343, f32[2,4,1024]{2,1,0:T(4,128)S(1)} %fusion.157, f32[2,4,1024]{2,1,0:T(4,128)S(1)} %get-tuple-element.319, f32[2,1024,4,3072]{3,1,2,0:T(8,128)} %get-tuple-element.318, ...), kind=kOutput, calls=%fused_computation.12.clone.1 | convolution fusion | flops 3347578880 | bytes 105710080 | tf_op jit(solution)/shard_map/while/body/eval_jaxpr/bkgqt,btkd->bqkgd/dot_general | solution.py:85
  467.0 667.6 %while.29 = (s32[]{:T(128)}, f32[2,3072,1,64]{1,3,0,2:T(8,128)}, f32[2,3072,1,64]{1,3,0,2:T(8,128)}, bf16[3,2,1024,1,4,64]{2,5,4,1,3,0:T(8,128)(2,1)}, s32[3]{0:...) while((s32[]{:T(128)}, f32[2,3072,1,64]{1,3,0,2:T(8,128)}, ...), condition=%wide.region_7.8_spmd.clone, body=%wide.region_5.7_spmd.clone.sunk | while | flops 16438518784 | bytes 624337856 | solution.py:122
  493.3 56.0 %fusion.167 = (f32[2,4,1024]{2,1,0:T(4,128)S(1)}, f32[2,1,4,1024,3072]{4,3,2,0,1:T(8,128)}) fusion(bf16[2,1024,4,3072]{3,1,2,0:T(8,128)(2,1)} %convolution_convert_fusion.3, f32[2,4,1024]{2,1,0:T(4,128)S(1)} %dynamic-slice_bitcast_fusion.2, bf16[2,3072,1,64]{1,3,0,2:T(8,128)(2,1)S(1)} %get-tuple-element.399, ...), kind=kOutput, calls=%fused_computation.28.clone.2 | convolution fusion | flops 3372212224 | bytes 156041216 | tf_op jit(solution)/shard_map/while/body/eval_jaxpr/bqkgd,btkd->bkgqt/dot_general | solution.py:109
  549.2 63.3 %fusion.168 = bf16[2,4,1024,3072]{3,2,1,0:T(8,128)(2,1)} fusion(f32[2,1,4,1024,3072]{4,3,2,0,1:T(8,128)} %get-tuple-element.330, bf16[2,1024,4,3072]{3,1,2,0:T(8,128)(2,1)} %convolution_convert_fusion.3, f32[2,4,1024]{2,1,0:T(4,128)S(1)} %get-tuple-element.331), kind=kLoop, calls=%fused_computation.32.clone.1 | loop fusion | flops 125829120 | bytes 201359360 | tf_op jit(solution)/shard_map/reshape.29
  612.6 22.1 %fusion.171 = bf16[3,2,1024,1,4,64]{2,5,4,1,3,0:T(8,128)(2,1)} fusion(bf16[3,2,1024,1,4,64]{2,5,4,1,3,0:T(8,128)(2,1)} %get-tuple-element.382, s32[]{:T(128)} %get-tuple-element.379, bf16[2,4,1024,3072]{3,2,1,0:T(8,128)(2,1)} %fusion.168, bf16[2,3072,1,64]{1,3,0,2:T(8,128)(2,1)S(1)} %get-tuple-element.399), kind=kOutput, calls=%fused_computation.44.clone.1 | convolution fusion | flops 3221749760 | bytes 52167168 | tf_op jit(solution)/shard_map/while/body/eval_jaxpr/bkgqt,btkd->bqkgd/dot_general | solution.py:116
  655.9 33.4 %fusion.170 = f32[2,3072,1,64]{1,3,0,2:T(8,128)} fusion(f32[2,1,4,1024,3072]{4,3,2,0,1:T(8,128)} %get-tuple-element.330, f32[2,3072,1,64]{1,3,0,2:T(8,128)} %get-tuple-element.381, bf16[2,3072,1,4,64]{1,4,3,0,2:T(8,128)(2,1)} %get-tuple-element.401, s32[]{:T(128)S(6)} %select_n.48, pred[]{:T(512)S(6)} %compare.3), kind=kOutput, calls=%fused_computation.41.clone.1 | convolution fusion | flops 3247177728 | bytes 104857608 | tf_op jit(solution)/shard_map/while/body/eval_jaxpr/bkgqt,bqkgd->btkd/dot_general | solution.py:118
  715.1 56.0 %fusion.167 = (f32[2,4,1024]{2,1,0:T(4,128)S(1)}, f32[2,1,4,1024,3072]{4,3,2,0,1:T(8,128)}) fusion(bf16[2,1024,4,3072]{3,1,2,0:T(8,128)(2,1)} %convolution_convert_fusion.3, f32[2,4,1024]{2,1,0:T(4,128)S(1)} %dynamic-slice_bitcast_fusion.2, bf16[2,3072,1,64]{1,3,0,2:T(8,128)(2,1)S(1)} %get-tuple-element.399, ...), kind=kOutput, calls=%fused_computation.28.clone.2 | convolution fusion | flops 3372212224 | bytes 156041216 | tf_op jit(solution)/shard_map/while/body/eval_jaxpr/bqkgd,btkd->bkgqt/dot_general | solution.py:109
  771.1 63.3 %fusion.168 = bf16[2,4,1024,3072]{3,2,1,0:T(8,128)(2,1)} fusion(f32[2,1,4,1024,3072]{4,3,2,0,1:T(8,128)} %get-tuple-element.330, bf16[2,1024,4,3072]{3,1,2,0:T(8,128)(2,1)} %convolution_convert_fusion.3, f32[2,4,1024]{2,1,0:T(4,128)S(1)} %get-tuple-element.331), kind=kLoop, calls=%fused_computation.32.clone.1 | loop fusion | flops 125829120 | bytes 201359360 | tf_op jit(solution)/shard_map/reshape.29
  878.1 33.7 %fusion.170 = f32[2,3072,1,64]{1,3,0,2:T(8,128)} fusion(f32[2,1,4,1024,3072]{4,3,2,0,1:T(8,128)} %get-tuple-element.330, f32[2,3072,1,64]{1,3,0,2:T(8,128)} %get-tuple-element.381, bf16[2,3072,1,4,64]{1,4,3,0,2:T(8,128)(2,1)} %get-tuple-element.401, s32[]{:T(128)S(6)} %select_n.48, pred[]{:T(512)S(6)} %compare.3), kind=kOutput, calls=%fused_computation.41.clone.1 | convolution fusion | flops 3247177728 | bytes 104857608 | tf_op jit(solution)/shard_map/while/body/eval_jaxpr/bkgqt,bqkgd->btkd/dot_general | solution.py:118
  937.7 56.0 %fusion.167 = (f32[2,4,1024]{2,1,0:T(4,128)S(1)}, f32[2,1,4,1024,3072]{4,3,2,0,1:T(8,128)}) fusion(bf16[2,1024,4,3072]{3,1,2,0:T(8,128)(2,1)} %convolution_convert_fusion.3, f32[2,4,1024]{2,1,0:T(4,128)S(1)} %dynamic-slice_bitcast_fusion.2, bf16[2,3072,1,64]{1,3,0,2:T(8,128)(2,1)S(1)} %get-tuple-element.399, ...), kind=kOutput, calls=%fused_computation.28.clone.2 | convolution fusion | flops 3372212224 | bytes 156041216 | tf_op jit(solution)/shard_map/while/body/eval_jaxpr/bqkgd,btkd->bkgqt/dot_general | solution.py:109
  993.7 63.3 %fusion.168 = bf16[2,4,1024,3072]{3,2,1,0:T(8,128)(2,1)} fusion(f32[2,1,4,1024,3072]{4,3,2,0,1:T(8,128)} %get-tuple-element.330, bf16[2,1024,4,3072]{3,1,2,0:T(8,128)(2,1)} %convolution_convert_fusion.3, f32[2,4,1024]{2,1,0:T(4,128)S(1)} %get-tuple-element.331), kind=kLoop, calls=%fused_computation.32.clone.1 | loop fusion | flops 125829120 | bytes 201359360 | tf_op jit(solution)/shard_map/reshape.29
  1057.0 22.1 %fusion.171 = bf16[3,2,1024,1,4,64]{2,5,4,1,3,0:T(8,128)(2,1)} fusion(bf16[3,2,1024,1,4,64]{2,5,4,1,3,0:T(8,128)(2,1)} %get-tuple-element.382, s32[]{:T(128)} %get-tuple-element.379, bf16[2,4,1024,3072]{3,2,1,0:T(8,128)(2,1)} %fusion.168, bf16[2,3072,1,64]{1,3,0,2:T(8,128)(2,1)S(1)} %get-tuple-element.399), kind=kOutput, calls=%fused_computation.44.clone.1 | convolution fusion | flops 3221749760 | bytes 52167168 | tf_op jit(solution)/shard_map/while/body/eval_jaxpr/bkgqt,btkd->bqkgd/dot_general | solution.py:116
  1100.6 33.7 %fusion.170 = f32[2,3072,1,64]{1,3,0,2:T(8,128)} fusion(f32[2,1,4,1024,3072]{4,3,2,0,1:T(8,128)} %get-tuple-element.330, f32[2,3072,1,64]{1,3,0,2:T(8,128)} %get-tuple-element.381, bf16[2,3072,1,4,64]{1,4,3,0,2:T(8,128)(2,1)} %get-tuple-element.401, s32[]{:T(128)S(6)} %select_n.48, pred[]{:T(512)S(6)} %compare.3), kind=kOutput, calls=%fused_computation.41.clone.1 | convolution fusion | flops 3247177728 | bytes 104857608 | tf_op jit(solution)/shard_map/while/body/eval_jaxpr/bkgqt,bqkgd->btkd/dot_general | solution.py:118
  1361.8 359.5 %all-reduce.3.cloned.1.call-done = (f32[2048,32,64]{0,2,1:T(8,128)}, f32[2048,8,64]{0,2,1:T(8,128)}, f32[2048,8,64]{0,2,1:T(8,128)}, f32[32,64,2048]{2,1,0:T(8,128)}) async-done(((f32[2048,32,64]{0,2,1:T(8,128)}, f32[2048,8,64]{0,2,1:T(8,128)}, f32[2048,8,64]{0,2,1:T(8,128)}, f32[32,64,2048]{2,1,0:T(8,128)}), (f32[2048,32,64]{0,2,1:T(8,128)}, f32[2048,8,64]{0,2,1:T(8,128)}, f32[2048,8,64]{0,2,1:T(8,128)}, ...) | async-done | bytes 41943056 | tf_op jit(solution)/shard_map/psum | solution.py:168
  (201 shorter events, 534.2 us)
Async XLA Ops:
  10.0 28.8 %copy-start.24 = (f32[2,384]{1,0:T(2,128)}, f32[2,384]{1,0:T(2,128)S(1)}, u32[]{:S(2)}) copy-start(f32[2,384]{1,0:T(2,128)S(1)} %add_rsqrt_fusion) | copy-start | bytes 9220
  10.3 38.9 %copy-start.15 = (f32[384,32]{0,1:T(8,128)}, f32[384,32]{0,1:T(8,128)S(1)}, u32[]{:S(2)}) copy-start(f32[384,32]{0,1:T(8,128)S(1)} %get-tuple-element.217) | copy-start | bytes 147460
  10.3 38.9 %copy-start.18 = (f32[384,32]{0,1:T(8,128)}, f32[384,32]{0,1:T(8,128)S(1)}, u32[]{:S(2)}) copy-start(f32[384,32]{0,1:T(8,128)S(1)} %get-tuple-element.218) | copy-start | bytes 147460
  15.4 18.0 %all-to-all-start.1 = ((bf16[2,384,8,64]{1,3,0,2:T(8,128)(2,1)}), bf16[2,384,8,64]{1,3,0,2:T(8,128)(2,1)S(1)}, u32[]{:S(2)}, u32[]{:S(2)}) async-start(bf16[2,384,8,64]{1,3,0,2:T(8,128)(2,1)} %copy.36), calls=%async_computation.1 | async-start | bytes 1572864 | tf_op jit(solution)/shard_map/all_to_all | solution.py:143
  33.4 19.3 %all-to-all-start.2 = ((bf16[2,384,8,64]{1,3,0,2:T(8,128)(2,1)}), bf16[2,384,8,64]{1,3,0,2:T(8,128)(2,1)}, u32[]{:S(2)}, u32[]{:S(2)}) async-start(bf16[2,384,8,64]{1,3,0,2:T(8,128)(2,1)} %copy.38), calls=%async_computation.2 | async-start | bytes 1572864 | tf_op jit(solution)/shard_map/all_to_all | solution.py:144
  52.7 42.8 %all-to-all-start = ((bf16[2,384,32,64]{1,3,0,2:T(8,128)(2,1)}), bf16[2,384,32,64]{1,3,0,2:T(8,128)(2,1)}, u32[]{:S(2)}, u32[]{:S(2)}) async-start(bf16[2,384,32,64]{1,3,0,2:T(8,128)(2,1)} %copy.34), calls=%async_computation | async-start | bytes 6291456 | tf_op jit(solution)/shard_map/all_to_all | solution.py:142
  95.5 358.0 %all-to-all-start.4 = ((bf16[2,384,32,64]{1,3,0,2:T(8,128)(2,1)}), bf16[2,384,32,64]{1,3,0,2:T(8,128)(2,1)}, u32[]{:S(2)}, u32[]{:S(2)}) async-start(bf16[2,384,32,64]{1,3,0,2:T(8,128)(2,1)} %copy.44), calls=%async_computation.4 | async-start | bytes 6291456 | tf_op jit(solution)/shard_map/all_to_all | solution.py:151
  115.2 42.4 %copy-start.1 = (bf16[2,3072,1,64]{1,3,0,2:T(8,128)(2,1)}, bf16[2,3072,1,64]{1,3,0,2:T(8,128)(2,1)S(1)}, u32[]{:S(2)}) copy-start(bf16[2,3072,1,64]{1,3,0,2:T(8,128)(2,1)S(1)} %get-tuple-element.359) | copy-start | bytes 2359300 | tf_op jit(solution)/shard_map/while
  190.6 37.3 %copy-start.2 = (bf16[2,3072,1,64]{1,3,0,2:T(8,128)(2,1)S(1)}, bf16[2,3072,1,64]{1,3,0,2:T(8,128)(2,1)}, u32[]{:S(2)}) copy-start(bf16[2,3072,1,64]{1,3,0,2:T(8,128)(2,1)} %copy-done.1) | copy-start | bytes 2359300 | tf_op jit(solution)/shard_map/while
  228.0 42.4 %copy-start.1 = (bf16[2,3072,1,64]{1,3,0,2:T(8,128)(2,1)}, bf16[2,3072,1,64]{1,3,0,2:T(8,128)(2,1)S(1)}, u32[]{:S(2)}) copy-start(bf16[2,3072,1,64]{1,3,0,2:T(8,128)(2,1)S(1)} %get-tuple-element.359) | copy-start | bytes 2359300 | tf_op jit(solution)/shard_map/while
  303.4 37.3 %copy-start.2 = (bf16[2,3072,1,64]{1,3,0,2:T(8,128)(2,1)S(1)}, bf16[2,3072,1,64]{1,3,0,2:T(8,128)(2,1)}, u32[]{:S(2)}) copy-start(bf16[2,3072,1,64]{1,3,0,2:T(8,128)(2,1)} %copy-done.1) | copy-start | bytes 2359300 | tf_op jit(solution)/shard_map/while
  340.7 42.4 %copy-start.1 = (bf16[2,3072,1,64]{1,3,0,2:T(8,128)(2,1)}, bf16[2,3072,1,64]{1,3,0,2:T(8,128)(2,1)S(1)}, u32[]{:S(2)}) copy-start(bf16[2,3072,1,64]{1,3,0,2:T(8,128)(2,1)S(1)} %get-tuple-element.359) | copy-start | bytes 2359300 | tf_op jit(solution)/shard_map/while
  416.2 37.3 %copy-start.2 = (bf16[2,3072,1,64]{1,3,0,2:T(8,128)(2,1)S(1)}, bf16[2,3072,1,64]{1,3,0,2:T(8,128)(2,1)}, u32[]{:S(2)}) copy-start(bf16[2,3072,1,64]{1,3,0,2:T(8,128)(2,1)} %copy-done.1) | copy-start | bytes 2359300 | tf_op jit(solution)/shard_map/while
  467.4 22.7 %copy-start.29 = (s32[3]{0:T(128)}, s32[3]{0:T(128)S(1)}, u32[]{:S(2)}) copy-start(s32[3]{0:T(128)S(1)} %get-tuple-element.397) | copy-start | bytes 40 | tf_op jit(solution)/shard_map/while
  655.9 33.4 %copy-start.30 = (s32[3]{0:T(128)S(1)}, s32[3]{0:T(128)}, u32[]{:S(2)}) copy-start(s32[3]{0:T(128)} %copy-done.29) | copy-start | bytes 40 | tf_op jit(solution)/shard_map/while
  689.2 22.6 %copy-start.29 = (s32[3]{0:T(128)}, s32[3]{0:T(128)S(1)}, u32[]{:S(2)}) copy-start(s32[3]{0:T(128)S(1)} %get-tuple-element.397) | copy-start | bytes 40 | tf_op jit(solution)/shard_map/while
  878.1 33.7 %copy-start.30 = (s32[3]{0:T(128)S(1)}, s32[3]{0:T(128)}, u32[]{:S(2)}) copy-start(s32[3]{0:T(128)} %copy-done.29) | copy-start | bytes 40 | tf_op jit(solution)/shard_map/while
  911.8 22.6 %copy-start.29 = (s32[3]{0:T(128)}, s32[3]{0:T(128)S(1)}, u32[]{:S(2)}) copy-start(s32[3]{0:T(128)S(1)} %get-tuple-element.397) | copy-start | bytes 40 | tf_op jit(solution)/shard_map/while
  1100.6 33.7 %copy-start.30 = (s32[3]{0:T(128)S(1)}, s32[3]{0:T(128)}, u32[]{:S(2)}) copy-start(s32[3]{0:T(128)} %copy-done.29) | copy-start | bytes 40 | tf_op jit(solution)/shard_map/while
  1142.0 16.8 all-to-all-start.6
  1158.8 24.1 %all-to-all-start.7 = ((bf16[8,2,24576]{2,1,0:T(2,128)(2,1)}), bf16[8,2,24576]{2,1,0:T(2,128)(2,1)}, u32[]{:S(2)}, u32[]{:S(2)}) async-start(bf16[8,2,24576]{2,1,0:T(2,128)(2,1)} %reshape.254), calls=%async_computation.7 | async-start | bytes 1572864 | tf_op jit(solution)/shard_map/all_to_all | solution.py:155
  1182.9 43.0 %all-to-all-start.5 = ((bf16[8,2,98304]{2,1,0:T(2,128)(2,1)}), bf16[8,2,98304]{2,1,0:T(2,128)(2,1)}, u32[]{:S(2)}, u32[]{:S(2)}) async-start(bf16[8,2,98304]{2,1,0:T(2,128)(2,1)} %reshape.252), calls=%async_computation.5 | async-start | bytes 6291456 | tf_op jit(solution)/shard_map/all_to_all | solution.py:153
  1225.9 42.3 %all-to-all-start.3 = ((bf16[8,2,98304]{2,1,0:T(2,128)(2,1)}), bf16[8,2,98304]{2,1,0:T(2,128)(2,1)}, u32[]{:S(2)}, u32[]{:S(2)}) async-start(bf16[8,2,98304]{2,1,0:T(2,128)(2,1)} %reshape.248), calls=%async_computation.3 | async-start | bytes 6291456 | tf_op jit(solution)/shard_map/all_to_all | solution.py:146
  1230.9 490.4 %all-reduce.3.cloned.1.call-start = ((), (), s32[]{:S(2)}) async-start(), calls=%async_computation.8 | async-start | bytes 83886080 | tf_op jit(solution)/shard_map/psum | solution.py:168
  (28 other events, 244.9 us)
Sparse Core Ops, SparseCore 0:
  1309.8 411.4 all-reduce.2
where the time goes:
time: 1770 us; the launch traced here: 1760 us
  matrix products  777 us (44%)
  waiting for transfers between devices  398 us (22%)
  other arithmetic  329 us (19%)
  local copies, waits for them, and re-layouts  177 us (10%)
  starting transfers between devices  42.3 us (2%)
    psum x1, waiting for transfers between devices, local_step(): lax.psum((d_wq, d_wk, d_wv, d_wo, d_gain), 'sp')  360 us
    dot_general x6, matrix products, one_block(): jnp.einsum('bqkgd,btkd->bkgqt', q_rows, k_heads, preferred_element_type=j...  277 us
    another operation x7, other arithmetic  196 us
    dot_general x3, matrix products, one_block(): jnp.einsum('bkgqt,btkd->bqkgd', attn_weights, v_heads, preferred_element_...  112 us
    dot_general x3, matrix products, one_block(): jnp.einsum('bkgqt,bqkgd->btkd', attn_weights.astype(jnp.bfloat16), d_rows...  101 us
    reduce_sum x3, other arithmetic, one_block(): row_sum = jnp.sum(exp_scores, axis=-1, keepdims=True)  97.2 us
    unnamed x74, local copies, waits for them, and re-layouts  75.9 us
    dot_general x3, matrix products, one_block(): jnp.einsum('bkgqt,btkd->bqkgd', d_scores, k_heads, preferred_element_type...  66.2 us
  transfers between devices with their start and end apart: 9, of which 5 were waited for; matrix products, arithmetic and copies ran while one was open for 29% of the time, Pallas kernels for 0%

commit v1 on v0

v1 whole, which is shorter than its diff:
```python
import functools
import math
import jax
import jax.numpy as jnp
from jax import lax
from jax.experimental import pallas as pl
from jax.experimental.pallas import tpu as pltpu
from jax.sharding import PartitionSpec as P

ROPE_BASE = 1000000.0
NORM_EPS = 1e-5
LOG2E = math.log2(math.e)
NEG = -1e30
F32 = jnp.float32
BF16 = jnp.bfloat16

NN = (((1,), (0,)), ((), ()))
NT = (((1,), (1,)), ((), ()))
TN = (((0,), (0,)), ((), ()))


def dot(a, b, dims=NN):
    return lax.dot_general(a, b, dims, preferred_element_type=F32)


def rope_tables_t(seq_len, head_dim):
    half = head_dim // 2
    inv_freq = ROPE_BASE ** (-2.0 * jnp.arange(half, dtype=F32) / head_dim)
    angle = jnp.arange(seq_len).astype(F32)[None, :] * inv_freq[:, None]
    return jnp.cos(angle), jnp.sin(angle)


def norm_forward(x_local, gain):
    x_f32 = x_local.astype(F32)
    inv_rms = lax.rsqrt(jnp.mean(x_f32 * x_f32, axis=-1, keepdims=True) + NORM_EPS)
    x_hat = x_f32 * inv_rms
    return x_hat, inv_rms, (x_hat * gain).astype(BF16)


def norm_backward(d_normed, x_hat, inv_rms, gain):
    d_hat = d_normed * gain
    return inv_rms * (d_hat - x_hat * jnp.mean(d_hat * x_hat, axis=-1, keepdims=True))


def project_kernel(group, dim, r_ref, w_ref, cos_ref, sin_ref, q_ref, k_ref, kt_ref, v_ref, vt_ref):
    half = dim // 2
    blk = r_ref.shape[1]
    lin = dot(w_ref[...], r_ref[0], NT)
    cos_t = cos_ref[...]
    sin_t = sin_ref[...]
    for h in range(group):
        a = lin[h * dim:h * dim + half]
        b = lin[h * dim + half:(h + 1) * dim]
        q_ref[0, :half, h * blk:(h + 1) * blk] = (a * cos_t - b * sin_t).astype(BF16)
        q_ref[0, half:, h * blk:(h + 1) * blk] = (b * cos_t + a * sin_t).astype(BF16)
    a = lin[group * dim:group * dim + half]
    b = lin[group * dim + half:(group + 1) * dim]
    v = lin[(group + 1) * dim:]
    kv = jnp.concatenate([a * cos_t - b * sin_t, b * cos_t + a * sin_t, v], axis=0)
    kt_ref[...] = kv[:dim].astype(BF16)
    vt_ref[...] = v.astype(BF16)
    kv_t = kv.T.astype(BF16)
    k_ref[...] = kv_t[:, :dim]
    v_ref[...] = kv_t[:, dim:]


def causal_mask(rows, cols, blk):
    key = lax.broadcasted_iota(jnp.int32, (rows, cols), 0)
    qry = lax.broadcasted_iota(jnp.int32, (rows, cols), 1) % blk
    return key <= qry


def forward_kernel(group, dim, q_ref, k_ref, vt_ref, o_ref, lse_ref, acc_ref, m_ref, l_ref):
    blk = o_ref.shape[2]
    i = pl.program_id(0)
    c2 = dim ** -0.5 * LOG2E
    acc_ref[...] = jnp.zeros_like(acc_ref)
    l_ref[...] = jnp.zeros_like(l_ref)
    m_ref[...] = jnp.full_like(m_ref, NEG)

    def tile(j, masked):
        off = pl.multiple_of(j * blk, blk)
        s = dot(k_ref[pl.ds(off, blk), :], q_ref[0])
        if masked:
            s = jnp.where(causal_mask(s.shape[0], s.shape[1], blk), s, NEG)
        m_old = m_ref[...]
        m_new = jnp.maximum(m_old, jnp.max(s, axis=0, keepdims=True) * c2)
        p = jnp.exp2(s * c2 - m_new)
        alpha = jnp.exp2(m_old - m_new)
        m_ref[...] = m_new
        l_ref[...] = l_ref[...] * alpha + jnp.sum(p, axis=0, keepdims=True)
        acc_ref[...] = acc_ref[...] * alpha + dot(vt_ref[:, pl.ds(off, blk)], p.astype(BF16))

    def step(j, carry):
        tile(j, False)
        return carry

    lax.fori_loop(0, i, step, 0)
    tile(i, True)
    l_val = l_ref[...]
    o = (acc_ref[...] * (1.0 / l_val)).astype(BF16)
    for h in range(group):
        o_ref[0, h * dim:(h + 1) * dim, :] = o[:, h * blk:(h + 1) * blk]
    lse_ref[0] = m_ref[...] + jnp.log2(l_val)


def out_grad_kernel(group, dim, first, *refs):
    if first:
        dy_ref, w_ref, o_ref, do_ref, dw_ref = refs
    else:
        dy_ref, w_ref, o_ref, prev_ref, do_ref, dw_ref = refs
    blk = dy_ref.shape[1]

    @pl.when(pl.program_id(0) == 0)
    def _():
        dw_ref[...] = jnp.zeros_like(dw_ref) if first else prev_ref[...]

    d_o = dot(w_ref[...], dy_ref[0], NT).astype(BF16)
    for h in range(group):
        do_ref[0, :, h * blk:(h + 1) * blk] = d_o[h * dim:(h + 1) * dim]
    dw_ref[...] += dot(o_ref[0], dy_ref[0])


def backward_kernel(group, dim, q_ref, do_ref, o_ref, lse_ref, k_ref, kt_ref, v_ref, cos_ref, sin_ref, out_ref,
                    dq_ref, dk_ref, dv_ref, delta_ref):
    blk = out_ref.shape[2]
    half = dim // 2
    step_id = pl.program_id(0)
    i = pl.num_programs(0) - 1 - step_id
    scale = dim ** -0.5
    c2 = scale * LOG2E

    @pl.when(step_id == 0)
    def _():
        dk_ref[...] = jnp.zeros_like(dk_ref)
        dv_ref[...] = jnp.zeros_like(dv_ref)

    dq_ref[...] = jnp.zeros_like(dq_ref)
    for h in range(group):
        prod = o_ref[0, h * dim:(h + 1) * dim, :].astype(F32) * do_ref[0, :, h * blk:(h + 1) * blk].astype(F32)
        delta_ref[:, h * blk:(h + 1) * blk] = jnp.sum(prod, axis=0, keepdims=True)

    def tile(j, masked):
        off = pl.multiple_of(j * blk, blk)
        s = dot(k_ref[pl.ds(off, blk), :], q_ref[0])
        p = jnp.exp2(s * c2 - lse_ref[0])
        if masked:
            p = jnp.where(causal_mask(s.shape[0], s.shape[1], blk), p, 0.0)
        dp = dot(v_ref[pl.ds(off, blk), :], do_ref[0]).astype(BF16).astype(F32)
        ds = (p * (dp - delta_ref[...])).astype(BF16)
        dv_ref[:, pl.ds(off, blk)] += dot(do_ref[0], p.astype(BF16), NT)
        dk_ref[:, pl.ds(off, blk)] += dot(q_ref[0], ds, NT)
        dq_ref[...] += dot(kt_ref[:, pl.ds(off, blk)], ds)

    def step(j, carry):
        tile(j, False)
        return carry

    lax.fori_loop(0, i, step, 0)
    tile(i, True)

    cos_t = cos_ref[...]
    sin_t = sin_ref[...]

    def rope_back(grad):
        grad = (grad * scale).astype(BF16).astype(F32)
        a = grad[:half]
        b = grad[half:]
        return (a * cos_t + b * sin_t).astype(BF16), (b * cos_t - a * sin_t).astype(BF16)

    for h in range(group):
        top, bottom = rope_back(dq_ref[:, h * blk:(h + 1) * blk])
        out_ref[0, h * dim:h * dim + half, :] = top
        out_ref[0, h * dim + half:(h + 1) * dim, :] = bottom
    off = pl.multiple_of(i * blk, blk)
    top, bottom = rope_back(dk_ref[:, pl.ds(off, blk)])
    base = group * dim
    out_ref[0, base:base + half, :] = top
    out_ref[0, base + half:base + dim, :] = bottom
    out_ref[0, base + dim:base + 2 * dim, :] = dv_ref[:, pl.ds(off, blk)].astype(BF16)


def weight_grad_kernel(first, *refs):
    if first:
        g_ref, r_ref, dw_ref = refs
    else:
        g_ref, r_ref, prev_ref, dw_ref = refs

    @pl.when(pl.program_id(0) == 0)
    def _():
        dw_ref[...] = jnp.zeros_like(dw_ref) if first else prev_ref[...]

    dw_ref[...] += dot(g_ref[0], r_ref[0])


def whole(*shape):
    return pl.BlockSpec(shape, lambda s: (0,) * len(shape))


def call(kernel, grid, in_specs, out_specs, out_shape, name, flops, scratch=(), aliases=None):
    return pl.pallas_call(
        kernel,
        grid=(grid,),
        in_specs=in_specs,
        out_specs=out_specs,
        out_shape=out_shape,
        scratch_shapes=list(scratch),
        input_output_aliases=aliases or {},
        name=name,
        cost_estimate=pl.CostEstimate(flops=int(flops), bytes_accessed=int(1e6), transcendentals=0),
        compiler_params=pltpu.CompilerParams(dimension_semantics=("arbitrary",)),
    )


def solution(mesh):
    seq_par = mesh.shape['sp']

    def local_step(x_local, dy_local, gain, w_q, w_k, w_v, w_o):
        batch, blk, d_model = x_local.shape
        num_q, dim = w_q.shape[1], w_q.shape[2]
        num_kv = w_k.shape[1]
        assert num_kv == seq_par
        group = num_q // num_kv
        half = dim // 2
        seq = blk * seq_par
        rows_q = group * dim
        rows = rows_q + 2 * dim
        cols = group * blk
        n = seq_par
        me = lax.axis_index('sp')

        wq_t = jnp.transpose(w_q, (1, 2, 0)).reshape(n, rows_q, d_model)
        wk_t = jnp.transpose(w_k, (1, 2, 0)).reshape(n, dim, d_model)
        wv_t = jnp.transpose(w_v, (1, 2, 0)).reshape(n, dim, d_model)
        wo_g = w_o.reshape(n, rows_q, d_model)
        w_all = jnp.concatenate([wq_t, wk_t, wv_t], axis=1)
        w_mine = lax.dynamic_index_in_dim(w_all, me, 0, keepdims=False)
        wo_mine = lax.dynamic_index_in_dim(wo_g, me, 0, keepdims=False)
        cos_t, sin_t = rope_tables_t(seq, dim)

        x_hat, inv_rms, normed = norm_forward(x_local, gain)
        r_all = [lax.all_gather(normed[b], 'sp', axis=0) for b in range(batch)]
        dy_all = [lax.all_gather(dy_local[b], 'sp', axis=0) for b in range(batch)]

        row3 = lambda a, b: pl.BlockSpec((1, a, b), lambda s: (s, 0, 0))
        lane = lambda a: pl.BlockSpec((a, blk), lambda s: (0, s))
        rev3 = lambda a, b: pl.BlockSpec((1, a, b), lambda s: (n - 1 - s, 0, 0))
        rev_lane = lambda a: pl.BlockSpec((a, blk), lambda s: (0, n - 1 - s))
        sds = jax.ShapeDtypeStruct
        tok = pl.BlockSpec((blk, dim), lambda s: (s, 0))
        mm = 2.0 * seq * d_model
        att = 2.0 * seq * seq * dim * group / 2

        project = call(functools.partial(project_kernel, group, dim), n,
                       [row3(blk, d_model), whole(rows, d_model), lane(half), lane(half)],
                       [row3(dim, cols), tok, lane(dim), tok, lane(dim)],
                       [sds((n, dim, cols), BF16), sds((seq, dim), BF16), sds((dim, seq), BF16),
                        sds((seq, dim), BF16), sds((dim, seq), BF16)], 'project', mm * rows)
        forward = call(functools.partial(forward_kernel, group, dim), n,
                       [row3(dim, cols), whole(seq, dim), whole(dim, seq)],
                       [row3(rows_q, blk), row3(1, cols)],
                       [sds((n, rows_q, blk), BF16), sds((n, 1, cols), F32)], 'forward', att * 8,
                       [pltpu.VMEM((dim, cols), F32), pltpu.VMEM((1, cols), F32), pltpu.VMEM((1, cols), F32)])
        backward = call(functools.partial(backward_kernel, group, dim), n,
                        [rev3(dim, cols), rev3(dim, cols), rev3(rows_q, blk), rev3(1, cols), whole(seq, dim),
                         whole(dim, seq), whole(seq, dim), rev_lane(half), rev_lane(half)],
                        rev3(rows, blk), sds((n, rows, blk), BF16), 'backward', att * 20,
                        [pltpu.VMEM((dim, cols), F32), pltpu.VMEM((dim, seq), F32), pltpu.VMEM((dim, seq), F32),
                         pltpu.VMEM((1, cols), F32)])

        def out_grad(dy_b, o_b, prev):
            first = prev is None
            args = (dy_b, wo_mine, o_b) + (() if first else (prev,))
            specs = [row3(blk, d_model), whole(rows_q, d_model), row3(rows_q, blk)]
            specs += [] if first else [whole(rows_q, d_model)]
            return call(functools.partial(out_grad_kernel, group, dim, first), n, specs,
                        [row3(dim, cols), whole(rows_q, d_model)],
                        [sds((n, dim, cols), BF16), sds((rows_q, d_model), F32)], 'out_grad', mm * rows_q * 2,
                        aliases=None if first else {3: 1})(*args)

        def weight_grad(g_b, r_b, prev):
            first = prev is None
            args = (g_b, r_b) + (() if first else (prev,))
            specs = [row3(rows, blk), row3(blk, d_model)] + ([] if first else [whole(rows, d_model)])
            return call(functools.partial(weight_grad_kernel, first), n, specs, whole(rows, d_model),
                        sds((rows, d_model), F32), 'weight_grad', mm * rows, aliases=None if first else {2: 0})(*args)

        swap = lambda t: lax.all_to_all(t, 'sp', 0, 0, tiled=True)
        heads, o_all, lse_all = [], [], []
        for b in range(batch):
            heads.append(project(r_all[b], w_mine, cos_t, sin_t))
            q_t, k, k_t, v, v_t = heads[b]
            o_b, lse_b = forward(q_t, k, v_t)
            o_all.append(o_b)
            lse_all.append(lse_b)
        o_local = [swap(o_all[b]).reshape(num_q * dim, blk) for b in range(batch)]
        d_wo_mine = None
        d_o = []
        for b in range(batch):
            do_b, d_wo_mine = out_grad(dy_all[b], o_all[b], d_wo_mine)
            d_o.append(do_b)
        d_wo = lax.all_gather(d_wo_mine, 'sp', axis=0, tiled=True)
        wo_flat = w_o.reshape(num_q * dim, d_model)
        y_proj = jnp.stack([dot(o_local[b], wo_flat, TN) for b in range(batch)])
        y_out = (x_local.astype(F32) + y_proj).astype(BF16)

        d_w_mine = None
        g_local = []
        for b in range(batch):
            q_t, k, k_t, v, v_t = heads[b]
            g_b = backward(q_t, d_o[b], o_all[b], lse_all[b], k, k_t, v, cos_t, sin_t)
            g_local.append(swap(g_b).reshape(n * rows, blk))
            d_w_mine = weight_grad(g_b, r_all[b], d_w_mine)
        d_wq = lax.all_gather(d_w_mine[:rows_q], 'sp', axis=0, tiled=True)
        d_wk = lax.all_gather(d_w_mine[rows_q:rows_q + dim], 'sp', axis=0, tiled=True)
        d_wv = lax.all_gather(d_w_mine[rows_q + dim:], 'sp', axis=0, tiled=True)

        w_flat = w_all.reshape(n * rows, d_model)
        d_normed = jnp.stack([dot(g_local[b], w_flat, TN) for b in range(batch)]).astype(BF16).astype(F32)
        d_x_norm = norm_backward(d_normed, x_hat, inv_rms, gain)
        d_gain = lax.psum(jnp.sum(d_normed * x_hat, axis=(0, 1)), 'sp')
        d_x = (dy_local.astype(F32) + d_x_norm).astype(BF16)
        back = lambda t, h: jnp.transpose(t.reshape(h, dim, d_model), (2, 0, 1))
        return (y_out, d_x, back(d_wq, num_q), back(d_wk, num_kv), back(d_wv, num_kv),
                d_wo.reshape(num_q, dim, d_model), d_gain)

    specs_in = (P('dp', 'sp', None), P('dp', 'sp', None), P(None), P(None, None, None), P(None, None, None), P(None, None, None), P(None, None, None))
    specs_out = (P('dp', 'sp', None), P('dp', 'sp', None), P('dp', None, None), P('dp', None, None), P('dp', None, None), P('dp', None, None), P('dp'))
    return jax.shard_map(local_step, mesh=mesh, in_specs=specs_in, out_specs=specs_out, check_vma=False)
```

time: 1770 us -> 787 us (0.44)
  matrix products: 777 us -> 35.3 us
  other arithmetic: 329 us -> 26.3 us
  Pallas kernels: 0 us -> 297 us
  waiting for transfers between devices: 398 us -> 253 us
  local copies, waits for them, and re-layouts: 177 us -> 41.2 us
  blocking collectives: 13.9 us -> 91.2 us
  starting transfers between devices: 42.3 us -> 13.1 us
    dot_general x33 -> x4, matrix products: 777 us -> 35.3 us  [dot(): return lax.dot_general(a, b, dims, preferred_element_type=F32)]
    psum x1 -> x0, waiting for transfers between devices: 360 us -> none  [local_step(): lax.psum((d_wq, d_wk, d_wv, d_wo, d_gain), 'sp')]
    pallas_call x0 -> x10, Pallas kernels: none -> 297 us  [the longest x2 131 us: local_step(): g_b = backward(q_t, d_o[b], o_all[b], lse_all[b], k, k_t, v, cos_t, sin_t)]
    another operation x7 -> x0, other arithmetic: 196 us -> none
    all_gather x0 -> x8, waiting for transfers between devices: none -> 178 us  [the longest x2 98.6 us: local_step(): r_all = [lax.all_gather(normed[b], 'sp', axis=0) for b in range(batch)]]
    reduce_sum x3 -> x1, other arithmetic: 97.2 us -> 2.54 us  [local_step(): d_gain = lax.psum(jnp.sum(d_normed * x_hat, axis=(0, 1)), 'sp')]
    all_to_all x0 -> x2, blocking collectives: none -> 77.8 us  [local_step(): swap = lambda t: lax.all_to_all(t, 'sp', 0, 0, tiled=True)]
    unnamed x74 -> x46, local copies, waits for them, and re-layouts: 75.9 us -> 29.8 us
  transfers between devices with their start and end apart: 9 -> 10, of which waited for: 5 -> 6; matrix products, arithmetic and copies ran while one was open for 29% -> 8% of each run, Pallas kernels for 0% -> 25%
where the time goes in v1:
time: 787 us; the launch traced here: 773 us
  Pallas kernels  297 us (38%)
  waiting for transfers between devices  253 us (32%)
  blocking collectives  91.2 us (12%)
  local copies, waits for them, and re-layouts  41.2 us (5%)
  matrix products  35.3 us (4%)
  other arithmetic  26.3 us (3%)
  between operations  14.7 us (2%)
  starting transfers between devices  13.1 us (2%)
    pallas_call x2, Pallas kernels, local_step(): g_b = backward(q_t, d_o[b], o_all[b], lse_all[b], k, k_t, v, cos_t, sin_t)  131 us
    all_gather x2, waiting for transfers between devices, local_step(): r_all = [lax.all_gather(normed[b], 'sp', axis=0) for b in range(batch)]  98.6 us
    pallas_call x2, Pallas kernels, local_step(): o_b, lse_b = forward(q_t, k, v_t)  83.2 us
    all_to_all x2, blocking collectives, local_step(): swap = lambda t: lax.all_to_all(t, 'sp', 0, 0, tiled=True)  77.8 us
    all_to_all x2, waiting for transfers between devices, local_step(): swap = lambda t: lax.all_to_all(t, 'sp', 0, 0, tiled=True)  72.9 us
    all_gather x1, waiting for transfers between devices, local_step(): d_wo = lax.all_gather(d_wo_mine, 'sp', axis=0, tiled=True)  68.2 us
    dot_general x4, matrix products, dot(): return lax.dot_general(a, b, dims, preferred_element_type=F32)  35.3 us
    unnamed x46, local copies, waits for them, and re-layouts  29.8 us
  transfers between devices with their start and end apart: 10, of which 6 were waited for; matrix products, arithmetic and copies ran while one was open for 8% of the time, Pallas kernels for 25%

profile of v1, /device:TPU:113, one launch (start us, length us, event | category | flops | bytes accessed | tf_op | source)
XLA Modules:
  0.0 772.5 jit_solution(4137048126524129407)
XLA Ops:
  19.8 10.0 %pad_maximum_fusion = bf16[8,384,2048]{2,1,0:T(8,128)(2,1)S(1)} fusion(bf16[8,64,2048]{2,1,0:T(8,128)(2,1)S(1)} %bitcast.60, bf16[8,64,2048]{2,1,0:T(8,128)(2,1)S(1)} %bitcast.63, bf16[8,256,2048]{2,1,0:T(8,128)(2,1)} %bitcast.54), kind=kLoop, calls=%fused_computation | loop fusion | flops 37748736 | bytes 25165824 | tf_op jit(solution)/shard_map/concatenate | solution.py:236
  33.4 46.1 %all-gather.9.cloned.1.call-done.r_ref.refs_1_ = bf16[8,384,2048]{2,1,0:T(8,128)(2,1)} async-done(((bf16[1,384,2048]{2,1,0:T(8,128)(2,1)}), bf16[8,384,2048]{2,1,0:T(8,128)(2,1)}) %all-gather.9.cloned.1.call-update) | async-done | bytes 12582928 | tf_op jit(solution)/shard_map/all_gather | solution.py:242
  79.5 13.3 %project.2 = (bf16[8,64,1536]{2,1,0:T(8,128)(2,1)}, bf16[3072,64]{1,0:T(8,128)(2,1)}, bf16[64,3072]{1,0:T(8,128)(2,1)}, bf16[3072,64]{1,0:T(8,128)(2,1)}, bf16[64,3072]{1,0:T(8,128)(2,1)}) custom-call(bf16[8,384,2048]{2,1,0:T(8,128)(2,1)} %all-gather.9.cloned.1.call-done.r_ref.refs_1_, bf16[384,2048]{1,0:T(8,128)(2,1)} %dynamic-slice_bitcast_fusion.w_ref, ...), custom_call_target="tpu_custom_call" | custom-call | flops 4831838208 | bytes 1000000 | tf_op jit(solution)/shard_map/project/pallas_call | solution.py:291
  92.8 52.5 %all-gather.11.cloned.1.call-done.r_ref.refs_1_ = bf16[8,384,2048]{2,1,0:T(8,128)(2,1)} async-done(((bf16[1,384,2048]{2,1,0:T(8,128)(2,1)}), bf16[8,384,2048]{2,1,0:T(8,128)(2,1)}) %all-gather.11.cloned.1.call-update) | async-done | bytes 12582928 | tf_op jit(solution)/shard_map/all_gather | solution.py:242
  145.3 13.3 %project.3 = (bf16[8,64,1536]{2,1,0:T(8,128)(2,1)}, bf16[3072,64]{1,0:T(8,128)(2,1)}, bf16[64,3072]{1,0:T(8,128)(2,1)}, bf16[3072,64]{1,0:T(8,128)(2,1)}, bf16[64,3072]{1,0:T(8,128)(2,1)}) custom-call(bf16[8,384,2048]{2,1,0:T(8,128)(2,1)} %all-gather.11.cloned.1.call-done.r_ref.refs_1_, bf16[384,2048]{1,0:T(8,128)(2,1)} %dynamic-slice_bitcast_fusion.w_ref, ...), custom_call_target="tpu_custom_call" | custom-call | flops 4831838208 | bytes 1000000 | tf_op jit(solution)/shard_map/project/pallas_call | solution.py:291
  158.6 41.6 %forward.2 = (bf16[8,256,384]{2,1,0:T(8,128)(2,1)}, f32[8,1,1536]{2,1,0:T(1,128)}) custom-call(bf16[8,64,1536]{2,1,0:T(8,128)(2,1)} %get-tuple-element.25.q_ref, bf16[3072,64]{1,0:T(8,128)(2,1)} %get-tuple-element.26.k_ref, bf16[64,3072]{1,0:T(8,128)(2,1)} %get-tuple-element.27.vt_ref), custom_call_target="tpu_custom_call" | custom-call | flops 19327352832 | bytes 1000000 | tf_op jit(solution)/shard_map/forward/pallas_call | solution.py:293
  200.2 10.9 %all-gather.13.cloned.1.call-done.refs_0_ = bf16[8,384,2048]{2,1,0:T(8,128)(2,1)} async-done(((bf16[1,384,2048]{2,1,0:T(8,128)(2,1)}), bf16[8,384,2048]{2,1,0:T(8,128)(2,1)}) %all-gather.13.cloned.1.call-update) | async-done | bytes 12582928 | tf_op jit(solution)/shard_map/all_gather | solution.py:243
  211.1 14.0 %out_grad.2 = (bf16[8,64,1536]{2,1,0:T(8,128)(2,1)}, f32[256,2048]{1,0:T(8,128)}) custom-call(bf16[8,384,2048]{2,1,0:T(8,128)(2,1)} %all-gather.13.cloned.1.call-done.refs_0_, bf16[256,2048]{1,0:T(8,128)(2,1)} %dynamic-slice_bitcast_fusion.1.refs_1_, bf16[8,256,384]{2,1,0:T(8,128)(2,1)} %get-tuple-element.28.refs_2_.o_ref), custom_call_target="tpu_custom_call" | custom-call | flops 6442450944 | bytes 1000000 | tf_op jit(solution)/shard_map/out_grad/pallas_call | solution.py:276
  225.1 41.6 %forward.3 = (bf16[8,256,384]{2,1,0:T(8,128)(2,1)}, f32[8,1,1536]{2,1,0:T(1,128)}) custom-call(bf16[8,64,1536]{2,1,0:T(8,128)(2,1)} %get-tuple-element.29.q_ref, bf16[3072,64]{1,0:T(8,128)(2,1)} %get-tuple-element.30.k_ref, bf16[64,3072]{1,0:T(8,128)(2,1)} %get-tuple-element.31.vt_ref), custom_call_target="tpu_custom_call" | custom-call | flops 19327352832 | bytes 1000000 | tf_op jit(solution)/shard_map/forward/pallas_call | solution.py:293
  266.7 65.8 %backward.2.refs_0_ = bf16[8,384,384]{2,1,0:T(8,128)(2,1)} custom-call(bf16[8,64,1536]{2,1,0:T(8,128)(2,1)} %get-tuple-element.25.q_ref, bf16[8,64,1536]{2,1,0:T(8,128)(2,1)} %get-tuple-element.33.do_ref, bf16[8,256,384]{2,1,0:T(8,128)(2,1)} %get-tuple-element.28.refs_2_.o_ref, f32[8,1,1536]{2,1,0:T(1,128)} %get-tuple-element.34.lse_ref, ...), custom_call_target="tpu_custom_call" | custom-call | flops 48318382080 | bytes 1000000 | tf_op jit(solution)/shard_map/backward/pallas_call | solution.py:311
  332.5 14.7 %out_grad.3 = (bf16[8,64,1536]{2,1,0:T(8,128)(2,1)}, f32[256,2048]{1,0:T(8,128)}) custom-call(bf16[8,384,2048]{2,1,0:T(8,128)(2,1)} %all-gather.15.cloned.1.call-done.refs_0_, bf16[256,2048]{1,0:T(8,128)(2,1)} %dynamic-slice_bitcast_fusion.1.refs_1_, bf16[8,256,384]{2,1,0:T(8,128)(2,1)} %get-tuple-element.32.refs_2_.o_ref, ...), custom_call_target="tpu_custom_call", output_to_operand_aliasing={{1}: (3, {})} | custom-call | flops 6442450944 | bytes 1000000 | tf_op jit(solution)/shard_map/out_grad/pallas_call | solution.py:276
  347.2 65.7 %backward.3.refs_0_ = bf16[8,384,384]{2,1,0:T(8,128)(2,1)} custom-call(bf16[8,64,1536]{2,1,0:T(8,128)(2,1)} %get-tuple-element.29.q_ref, bf16[8,64,1536]{2,1,0:T(8,128)(2,1)} %get-tuple-element.38.do_ref, bf16[8,256,384]{2,1,0:T(8,128)(2,1)} %get-tuple-element.32.refs_2_.o_ref, f32[8,1,1536]{2,1,0:T(1,128)} %get-tuple-element.39.lse_ref, ...), custom_call_target="tpu_custom_call" | custom-call | flops 48318382080 | bytes 1000000 | tf_op jit(solution)/shard_map/backward/pallas_call | solution.py:311
  412.9 13.1 %weight_grad.2.refs_2_ = f32[384,2048]{1,0:T(8,128)} custom-call(bf16[8,384,384]{2,1,0:T(8,128)(2,1)} %backward.2.refs_0_, bf16[8,384,2048]{2,1,0:T(8,128)(2,1)} %all-gather.9.cloned.1.call-done.r_ref.refs_1_), custom_call_target="tpu_custom_call" | custom-call | flops 4831838208 | bytes 1000000 | tf_op jit(solution)/shard_map/weight_grad/pallas_call | solution.py:285
  426.0 14.1 %weight_grad.3 = f32[384,2048]{1,0:T(8,128)} custom-call(bf16[8,384,384]{2,1,0:T(8,128)(2,1)} %backward.3.refs_0_, bf16[8,384,2048]{2,1,0:T(8,128)(2,1)} %all-gather.11.cloned.1.call-done.r_ref.refs_1_, f32[384,2048]{1,0:T(8,128)} %weight_grad.2.refs_2_), custom_call_target="tpu_custom_call", output_to_operand_aliasing={{}: (2, {})} | custom-call | flops 4831838208 | bytes 1000000 | tf_op jit(solution)/shard_map/weight_grad/pallas_call | solution.py:285
  446.2 40.0 %all_to_all.20 = bf16[8,256,384]{2,1,0:T(8,128)(2,1)S(1)} all-to-all(bf16[8,256,384]{2,1,0:T(8,128)(2,1)S(1)} %copy-done.12), channel_id=1, replica_groups=mesh['dp'=2,'sp'=8] {'sp'}, dimensions={0} | all-to-all | bytes 3145728 | tf_op jit(solution)/shard_map/all_to_all | solution.py:288
  486.2 37.8 %all_to_all.21 = bf16[8,256,384]{2,1,0:T(8,128)(2,1)S(1)} all-to-all(bf16[8,256,384]{2,1,0:T(8,128)(2,1)} %get-tuple-element.32.refs_2_.o_ref), channel_id=1, replica_groups=mesh['dp'=2,'sp'=8] {'sp'}, dimensions={0} | all-to-all | bytes 3145728 | tf_op jit(solution)/shard_map/all_to_all | solution.py:288
  538.9 36.0 %all-to-all-done.2 = bf16[8,384,384]{2,1,0:T(8,128)(2,1)} async-done(((bf16[8,384,384]{2,1,0:T(8,128)(2,1)}), bf16[8,384,384]{2,1,0:T(8,128)(2,1)}, u32[]{:S(2)}, u32[]{:S(2)}) %all-to-all-start.2) | async-done | bytes 2359328 | tf_op jit(solution)/shard_map/all_to_all | solution.py:288
  581.2 8.7 %convolution_bitcast_fusion = f32[1,384,2048]{2,1,0:T(8,128)} fusion(bf16[2048,384]{1,0:T(8,128)(2,1)S(1)} %bitcast.52, bf16[2048,2048]{1,0:T(8,128)(2,1)} %bitcast.47), kind=kOutput, calls=%fused_computation.21 | convolution fusion | flops 3221225472 | bytes 13107200 | tf_op jit(solution)/shard_map/dot_general | solution.py:23
  589.8 9.1 %fusion.13 = bf16[1,384,2048]{2,1,0:T(8,128)(2,1)} fusion(bf16[8,384,384]{2,1,0:T(8,128)(2,1)} %all-to-all-done.2, bf16[8,64,2048]{2,1,0:T(8,128)(2,1)S(1)} %bitcast.61, bf16[8,64,2048]{2,1,0:T(8,128)(2,1)S(1)} %bitcast.64, bf16[8,256,2048]{2,1,0:T(8,128)(2,1)} %bitcast.55), kind=kOutput, calls=%fused_computation.23 | convolution fusion | flops 4870373376 | bytes 16515072 | tf_op jit(solution)/shard_map/dot_general | solution.py:23
  599.0 36.8 %all-to-all-done.3 = bf16[8,384,384]{2,1,0:T(8,128)(2,1)} async-done(((bf16[8,384,384]{2,1,0:T(8,128)(2,1)}), bf16[8,384,384]{2,1,0:T(8,128)(2,1)}, u32[]{:S(2)}, u32[]{:S(2)}) %all-to-all-start.3) | async-done | bytes 2359328 | tf_op jit(solution)/shard_map/all_to_all | solution.py:288
  635.8 8.9 %fusion.14 = bf16[1,384,2048]{2,1,0:T(8,128)(2,1)S(1)} fusion(bf16[8,384,384]{2,1,0:T(8,128)(2,1)} %all-to-all-done.3, bf16[8,64,2048]{2,1,0:T(8,128)(2,1)} %bitcast.59, bf16[8,64,2048]{2,1,0:T(8,128)(2,1)} %bitcast.62, bf16[8,256,2048]{2,1,0:T(8,128)(2,1)} %bitcast.56), kind=kOutput, calls=%fused_computation.24 | convolution fusion | flops 4870373376 | bytes 16515072 | tf_op jit(solution)/shard_map/dot_general | solution.py:23
  647.4 13.5 %psum.7 = f32[2048]{0:T(1024)} all-reduce(f32[2048]{0:T(1024)S(1)} %get-tuple-element.43), channel_id=1, replica_groups=mesh['dp'=2,'sp'=8] {'sp'}, use_global_device_ids=true, to_apply=%region_3.4 | all-reduce | flops 2048 | bytes 16384 | tf_op jit(solution)/shard_map/psum | solution.py:321
  668.8 68.2 %all-gather.23.cloned.1.call-done = f32[2048,2048]{1,0:T(8,128)} async-done(((f32[256,2048]{1,0:T(8,128)}), f32[2048,2048]{1,0:T(8,128)}) %all-gather.23.cloned.1.call-update) | async-done | bytes 16777232 | tf_op jit(solution)/shard_map/all_gather | solution.py:302
  737.0 13.6 %copy.28 = f32[2048,32,64]{0,2,1:T(8,128)} copy(f32[2048,32,64]{0,2,1:T(8,128)} %bitcast.48) | data formatting | bytes 33554432
  (84 shorter events, 68.4 us)
Async XLA Ops:
  7.2 72.3 %all-gather.9.cloned.1.call-start = ((), (), s32[]{:S(2)}) async-start(), calls=%async_computation.4 | async-start | bytes 14155776 | tf_op jit(solution)/shard_map/all_gather | solution.py:242
  12.8 132.5 %all-gather.11.cloned.1.call-start = ((), (), s32[]{:S(2)}) async-start(), calls=%async_computation.5 | async-start | bytes 14155776 | tf_op jit(solution)/shard_map/all_gather | solution.py:242
  13.6 197.5 %all-gather.13.cloned.1.call-start = ((), (), s32[]{:S(2)}) async-start(), calls=%async_computation.6 | async-start | bytes 14155776 | tf_op jit(solution)/shard_map/all_gather | solution.py:243
  16.5 3.3 copy-start.8
  16.6 316.0 %all-gather.15.cloned.1.call-start = ((), (), s32[]{:S(2)}) async-start(), calls=%async_computation.7 | async-start | bytes 14155776 | tf_op jit(solution)/shard_map/all_gather | solution.py:243
  17.2 651.6 %all-gather.19.cloned.1.call-start = ((), (), s32[]{:S(2)}) async-start(), calls=%async_computation.9 | async-start | bytes 4718592 | tf_op jit(solution)/shard_map/all_gather | solution.py:315
  440.1 3.2 copy-start.2
  442.6 226.1 %all-gather.21.cloned.1.call-start = ((), (), s32[]{:S(2)}) async-start(), calls=%async_computation.10 | async-start | bytes 4718592 | tf_op jit(solution)/shard_map/all_gather | solution.py:316
  443.3 225.5 %all-gather.17.cloned.1.call-start = ((), (), s32[]{:S(2)}) async-start(), calls=%async_computation.8 | async-start | bytes 18874368 | tf_op jit(solution)/shard_map/all_gather | solution.py:314
  444.9 292.2 %all-gather.23.cloned.1.call-start = ((), (), s32[]{:S(2)}) async-start(), calls=%async_computation.11 | async-start | bytes 18874368 | tf_op jit(solution)/shard_map/all_gather | solution.py:302
  524.0 51.0 %all-to-all-start.2 = ((bf16[8,384,384]{2,1,0:T(8,128)(2,1)}), bf16[8,384,384]{2,1,0:T(8,128)(2,1)}, u32[]{:S(2)}, u32[]{:S(2)}) async-start(bf16[8,384,384]{2,1,0:T(8,128)(2,1)} %backward.2.refs_0_), calls=%async_computation.2 | async-start | bytes 4718592 | tf_op jit(solution)/shard_map/all_to_all | solution.py:288
  574.9 60.9 %all-to-all-start.3 = ((bf16[8,384,384]{2,1,0:T(8,128)(2,1)}), bf16[8,384,384]{2,1,0:T(8,128)(2,1)}, u32[]{:S(2)}, u32[]{:S(2)}) async-start(bf16[8,384,384]{2,1,0:T(8,128)(2,1)} %backward.3.refs_0_), calls=%async_computation.3 | async-start | bytes 4718592 | tf_op jit(solution)/shard_map/all_to_all | solution.py:288
  581.2 8.7 %copy-start.9 = (bf16[2048,8,64]{0,2,1:T(8,128)(2,1)S(1)}, bf16[2048,8,64]{0,2,1:T(8,128)(2,1)}, u32[]{:S(2)}) copy-start(bf16[2048,8,64]{0,2,1:T(8,128)(2,1)} %param.12) | copy-start | bytes 6291460
  581.2 8.7 %copy-start.11 = (bf16[2048,8,64]{0,2,1:T(8,128)(2,1)S(1)}, bf16[2048,8,64]{0,2,1:T(8,128)(2,1)}, u32[]{:S(2)}) copy-start(bf16[2048,8,64]{0,2,1:T(8,128)(2,1)} %param.11) | copy-start | bytes 6291460
  599.0 45.8 %copy-start.1 = (bf16[2,384,2048]{2,1,0:T(8,128)(2,1)S(1)}, bf16[2,384,2048]{2,1,0:T(8,128)(2,1)}, u32[]{:S(2)}) copy-start(bf16[2,384,2048]{2,1,0:T(8,128)(2,1)} %param.7) | copy-start | bytes 9437188
  599.0 45.8 %copy-start.14 = (f32[2048]{0:T(1024)S(1)}, f32[2048]{0:T(1024)}, u32[]{:S(2)}) copy-start(f32[2048]{0:T(1024)} %param.9) | copy-start | bytes 24580
  599.0 45.8 %copy-start.16 = (f32[2,384]{1,0:T(2,128)S(1)}, f32[2,384]{1,0:T(2,128)}, u32[]{:S(2)}) copy-start(f32[2,384]{1,0:T(2,128)} %copy-done.15) | copy-start | bytes 9220
  635.8 9.0 %copy-start.4 = (bf16[1,384,2048]{2,1,0:T(8,128)(2,1)S(1)}, bf16[1,384,2048]{2,1,0:T(8,128)(2,1)}, u32[]{:S(2)}) copy-start(bf16[1,384,2048]{2,1,0:T(8,128)(2,1)} %fusion.13) | copy-start | bytes 4718596
  737.0 13.6 %copy-start.6 = (f32[512,2048]{1,0:T(8,128)S(1)}, f32[512,2048]{1,0:T(8,128)}, u32[]{:S(2)}) copy-start(f32[512,2048]{1,0:T(8,128)} %all-gather.19.cloned.1.call-done) | copy-start | bytes 12582916
  737.0 20.3 %slice-start = ((s8[16777216]{0:T(1024)(128)(4,1)}), s8[4194304]{0:T(1024)(128)(4,1)S(1)}, s32[]{:S(2)}) async-start(s8[16777216]{0:T(1024)(128)(4,1)} %bitcast.49), calls=%async_computation.12 | async-start | bytes 8388608
  737.0 20.3 %slice-start.1 = ((s8[16777216]{0:T(1024)(128)(4,1)}), s8[4194304]{0:T(1024)(128)(4,1)S(1)}, s32[]{:S(2)}) async-start(s8[16777216]{0:T(1024)(128)(4,1)} %bitcast.49), calls=%async_computation.13 | async-start | bytes 8388608
  737.0 20.3 %slice-start.2 = ((s8[16777216]{0:T(1024)(128)(4,1)}), s8[4194304]{0:T(1024)(128)(4,1)S(1)}, s32[]{:S(2)}) async-start(s8[16777216]{0:T(1024)(128)(4,1)} %bitcast.49), calls=%async_computation.14 | async-start | bytes 8388608
  750.6 4.6 copy-start.7
  750.6 8.5 %slice-start.3 = ((s8[16777216]{0:T(1024)(128)(4,1)}), s8[4194304]{0:T(1024)(128)(4,1)S(1)}, s32[]{:S(2)}) async-start(s8[16777216]{0:T(1024)(128)(4,1)} %bitcast.49), calls=%async_computation.15 | async-start | bytes 8388608
  (7 other events, 14.8 us)
Sparse Core Ops, SparseCore 0:
  12.9 66.5 all-gather.8
  81.7 63.6 all-gather.10
  147.5 63.6 all-gather.12
  213.2 63.6 all-gather.14
  442.7 43.8 all-gather.18
  488.1 41.5 all-gather.20
  531.9 122.2 all-gather.16
  656.3 80.6 all-gather.22

commit v2 on v1

v2 whole, which is shorter than its diff:
```python
import functools
import math
import jax
import jax.numpy as jnp
from jax import lax
from jax.experimental import pallas as pl
from jax.experimental.pallas import tpu as pltpu
from jax.sharding import PartitionSpec as P

ROPE_BASE = 1000000.0
NORM_EPS = 1e-5
LOG2E = math.log2(math.e)
NEG = -1e30
F32 = jnp.float32
BF16 = jnp.bfloat16

MESH = pl.DeviceIdType.MESH
CORES = 2

NN = (((1,), (0,)), ((), ()))
NT = (((1,), (1,)), ((), ()))
TN = (((0,), (0,)), ((), ()))


def dot(a, b, dims=NN):
    return lax.dot_general(a, b, dims, preferred_element_type=F32)


def rope_tables_t(seq_len, head_dim):
    half = head_dim // 2
    inv_freq = ROPE_BASE ** (-2.0 * jnp.arange(half, dtype=F32) / head_dim)
    angle = jnp.arange(seq_len).astype(F32)[None, :] * inv_freq[:, None]
    return jnp.cos(angle), jnp.sin(angle)


def norm_forward(x_local, gain):
    x_f32 = x_local.astype(F32)
    inv_rms = lax.rsqrt(jnp.mean(x_f32 * x_f32, axis=-1, keepdims=True) + NORM_EPS)
    x_hat = x_f32 * inv_rms
    return x_hat, inv_rms, (x_hat * gain).astype(BF16)


def norm_backward(d_normed, x_hat, inv_rms, gain):
    d_hat = d_normed * gain
    return inv_rms * (d_hat - x_hat * jnp.mean(d_hat * x_hat, axis=-1, keepdims=True))


def remote(src, dst, send_sem, recv_sem, target):
    return pltpu.make_async_remote_copy(src_ref=src, dst_ref=dst, send_sem=send_sem, recv_sem=recv_sem,
                                        device_id={'sp': target}, device_id_type=MESH)


def enter(targets):
    barrier = pltpu.get_barrier_semaphore()
    for t in targets:
        pl.semaphore_signal(barrier, inc=1, device_id={'sp': t}, device_id_type=MESH)
    pl.semaphore_wait(barrier, len(targets))


class Ring:
    def __init__(self, n, src_ref, all_ref, send_sem, recv_sem):
        self.n, self.src, self.all, self.send_sem, self.recv_sem = n, src_ref, all_ref, send_sem, recv_sem
        me = lax.axis_index('sp')
        self.me, self.chip, self.core = me, me // CORES, me % CORES
        self.partner = self.at(0, 1 - self.core)

    def at(self, hop, core):
        chips = self.n // CORES
        return (self.chip + hop + chips) % chips * CORES + core

    def neighbours(self):
        return [self.partner] + [self.at(hop, core) for hop in (1, -1) for core in range(CORES)]

    def copy(self, src, slot, k, target):
        return remote(src, self.all.at[slot], self.send_sem.at[k], self.recv_sem.at[slot], target)

    def direct(self):
        out = [self.copy(self.src.at[1 - self.core], self.me, 0, self.partner)]
        k = 1
        for turn in range(CORES):
            for hop in (1, -1):
                core = (self.core + turn) % CORES
                out.append(self.copy(self.src.at[core], self.me, k, self.at(hop, core)))
                k += 1
        return out

    def relayed(self):
        first, second = self.at(-1, 0), self.at(1, 1)
        k = 1 + 2 * CORES
        return [self.copy(self.all.at[first], first, k, self.at(1, self.core)),
                self.copy(self.all.at[second], second, k + 1, self.at(-1, self.core))]

    def start(self):
        for c in self.direct():
            c.start()

    def relay(self):
        for c in self.relayed():
            c.start()

    def wait_block(self, slot):
        self.copy(self.all.at[slot], slot, 0, self.partner).wait_recv()

    def order(self):
        b, o = self.core, 1 - self.core
        return [self.me, self.partner, self.at(-1, b), self.at(1, b), self.at(-1, o), self.at(1, o),
                self.at(2, 0), self.at(2, 1)]

    def wait_sends(self):
        for c in self.direct() + self.relayed():
            c.wait_send()


RING_SENDS = 3 + 2 * CORES


def project_kernel(n, group, dim, r_hbm, w_ref, cos_ref, sin_ref, all_ref, q_ref, k_ref, kt_ref, v_ref, vt_ref,
                   block_ref, load_sem, send_sem, recv_sem):
    half = dim // 2
    blk = block_ref.shape[0]
    rows = (group + 2) * dim
    ring = Ring(n, r_hbm, all_ref, send_sem, recv_sem)
    enter(ring.neighbours())
    ring.start()
    order = ring.order()

    def body(p, carry):
        slot = order[0]
        for k in range(1, n):
            slot = jnp.where(p == k, order[k], slot)

        @pl.when(p == 0)
        def _():
            load = pltpu.make_async_copy(r_hbm.at[ring.core], block_ref, load_sem)
            load.start()
            load.wait()
            store = pltpu.make_async_copy(block_ref, all_ref.at[ring.me], load_sem)
            store.start()
            store.wait()

        for k in range(1, n):
            @pl.when(p == k)
            def _(k=k):
                if k == 4:
                    ring.wait_block(order[4])
                    ring.wait_block(order[5])
                    ring.relay()
                elif k != 5:
                    ring.wait_block(order[k])
                load = pltpu.make_async_copy(all_ref.at[order[k]], block_ref, load_sem)
                load.start()
                load.wait()

        off = pl.multiple_of(slot * blk, blk)
        cos_t = cos_ref[:, pl.ds(off, blk)]
        sin_t = sin_ref[:, pl.ds(off, blk)]
        for g in range(CORES):
            lin = dot(w_ref[g * rows:(g + 1) * rows], block_ref[...], NT)
            for h in range(group):
                a = lin[h * dim:h * dim + half]
                b = lin[h * dim + half:(h + 1) * dim]
                q_ref[g, slot, :half, h * blk:(h + 1) * blk] = (a * cos_t - b * sin_t).astype(BF16)
                q_ref[g, slot, half:, h * blk:(h + 1) * blk] = (b * cos_t + a * sin_t).astype(BF16)
            a = lin[group * dim:group * dim + half]
            b = lin[group * dim + half:(group + 1) * dim]
            v = lin[(group + 1) * dim:]
            kv = jnp.concatenate([a * cos_t - b * sin_t, b * cos_t + a * sin_t, v], axis=0)
            kt_ref[g, :, pl.ds(off, blk)] = kv[:dim].astype(BF16)
            vt_ref[g, :, pl.ds(off, blk)] = v.astype(BF16)
            kv_t = kv.T.astype(BF16)
            k_ref[g, pl.ds(off, blk), :] = kv_t[:, :dim]
            v_ref[g, pl.ds(off, blk), :] = kv_t[:, dim:]
        return carry

    lax.fori_loop(0, n, body, 0)
    ring.wait_sends()


def causal_mask(rows, cols, blk):
    key = lax.broadcasted_iota(jnp.int32, (rows, cols), 0)
    qry = lax.broadcasted_iota(jnp.int32, (rows, cols), 1) % blk
    return key <= qry


def forward_kernel(n, group, dim, relay_at, q_ref, k_ref, vt_ref, dy_hbm, o_ref, lse_ref, all_ref, acc_ref, m_ref, l_ref,
                   bounce_ref, load_sem, send_sem, recv_sem):
    blk = o_ref.shape[2]
    step_id = pl.program_id(0)
    i = step_id % n
    c2 = dim ** -0.5 * LOG2E
    ring = Ring(n, dy_hbm, all_ref, send_sem, recv_sem)
    order = ring.order()

    @pl.when(step_id == 0)
    def _():
        enter(ring.neighbours())
        ring.start()
        load = pltpu.make_async_copy(dy_hbm.at[ring.core], bounce_ref, load_sem)
        load.start()
        load.wait()
        store = pltpu.make_async_copy(bounce_ref, all_ref.at[ring.me], load_sem)
        store.start()
        store.wait()

    @pl.when(step_id == relay_at)
    def _():
        ring.wait_block(order[4])
        ring.wait_block(order[5])
        ring.wait_block(order[2])
        ring.wait_block(order[3])
        ring.relay()

    acc_ref[...] = jnp.zeros_like(acc_ref)
    l_ref[...] = jnp.zeros_like(l_ref)
    m_ref[...] = jnp.full_like(m_ref, NEG)

    def tile(j, masked):
        off = pl.multiple_of(j * blk, blk)
        s = dot(k_ref[0, pl.ds(off, blk), :], q_ref[0, 0])
        if masked:
            s = jnp.where(causal_mask(s.shape[0], s.shape[1], blk), s, NEG)
        m_old = m_ref[...]
        m_new = jnp.maximum(m_old, jnp.max(s, axis=0, keepdims=True) * c2)
        p = jnp.exp2(s * c2 - m_new)
        alpha = jnp.exp2(m_old - m_new)
        m_ref[...] = m_new
        l_ref[...] = l_ref[...] * alpha + jnp.sum(p, axis=0, keepdims=True)
        acc_ref[...] = acc_ref[...] * alpha + dot(vt_ref[0, :, pl.ds(off, blk)], p.astype(BF16))

    def step(j, carry):
        tile(j, False)
        return carry

    lax.fori_loop(0, i, step, 0)
    tile(i, True)
    l_val = l_ref[...]
    o = (acc_ref[...] * (1.0 / l_val)).astype(BF16)
    for h in range(group):
        o_ref[0, h * dim:(h + 1) * dim, :] = o[:, h * blk:(h + 1) * blk]
    lse_ref[0, 0] = m_ref[...] + jnp.log2(l_val)

    @pl.when(step_id == pl.num_programs(0) - 1)
    def _():
        for k in (1, 6, 7):
            ring.wait_block(order[k])
        ring.wait_sends()


class Swap:
    def __init__(self, n, src_ref, dst_ref, send_sem, recv_sem):
        self.n, self.src, self.dst, self.send_sem, self.recv_sem = n, src_ref, dst_ref, send_sem, recv_sem
        self.me = lax.axis_index('sp')

    def slot(self, dev):
        return dev % CORES * (self.n // CORES) + dev // CORES

    def peers(self):
        return [(self.me + d) % self.n for d in range(1, self.n)]

    def sends(self):
        mine = self.slot(self.me)
        return [remote(self.src.at[t], self.dst.at[mine], self.send_sem.at[d], self.recv_sem.at[mine], t)
                for d, t in enumerate(self.peers())]

    def start(self):
        for c in self.sends():
            c.start()

    def keep(self, block, sem):
        c = pltpu.make_async_copy(block, self.dst.at[self.slot(self.me)], sem)
        c.start()
        c.wait()

    def finish(self):
        for d, t in enumerate(self.peers()):
            s = self.slot(t)
            remote(self.src.at[t], self.dst.at[s], self.send_sem.at[d], self.recv_sem.at[s], t).wait_recv()
        for c in self.sends():
            c.wait_send()


def accumulate(acc_ref, lhs_ref, rhs, part, size):
    off = pl.multiple_of(part * size, size)
    acc_ref[pl.ds(off, size), :] += dot(lhs_ref[0, pl.ds(off, size), :], rhs)


def pair_sum(acc_ref, lhs_ref, rhs, got_ref, dw_ref, send_sem, recv_sem, last):
    me = lax.axis_index('sp')
    core = me % CORES
    partner = me - core + 1 - core
    size = acc_ref.shape[0] // CORES
    theirs = pl.ds(pl.multiple_of((1 - core) * size, size), size)
    mine = pl.ds(pl.multiple_of(core * size, size), size)
    copy = remote(acc_ref.at[theirs], got_ref, send_sem, recv_sem, partner)
    accumulate(acc_ref, lhs_ref, rhs, 1 - core, size)

    @pl.when(last)
    def _():
        copy.start()

    accumulate(acc_ref, lhs_ref, rhs, core, size)

    @pl.when(last)
    def _():
        copy.wait()
        dw_ref[...] = acc_ref[mine, :] + got_ref[...]


def out_grad_kernel(n, group, dim, dy_ref, w_ref, o_ref, o_hbm, do_ref, dw_ref, swap_ref, acc_ref, got_ref, keep_sem,
                    pair_send, pair_recv, send_sem, recv_sem):
    blk = dy_ref.shape[1]
    i = pl.program_id(0)
    swap = Swap(n, o_hbm, swap_ref, send_sem, recv_sem)

    @pl.when(i == 0)
    def _():
        enter(swap.peers())
        swap.start()
        acc_ref[...] = jnp.zeros_like(acc_ref)

    @pl.when(i == swap.me)
    def _():
        swap.keep(o_ref.at[0], keep_sem)

    d_o = dot(w_ref[...], dy_ref[0], NT).astype(BF16)
    for g in range(CORES):
        for h in range(group):
            row = (g * group + h) * dim
            do_ref[g, 0, :, h * blk:(h + 1) * blk] = d_o[row:row + dim]
    pair_sum(acc_ref, o_ref, dy_ref[0], got_ref, dw_ref, pair_send, pair_recv, i == n - 1)

    @pl.when(i == n - 1)
    def _():
        swap.finish()


def backward_kernel(group, dim, q_ref, do_ref, o_ref, lse_ref, k_ref, kt_ref, v_ref, cos_ref, sin_ref, out_ref,
                    dq_ref, dk_ref, dv_ref, delta_ref):
    blk = out_ref.shape[2]
    half = dim // 2
    step_id = pl.program_id(0)
    i = pl.num_programs(0) - 1 - step_id
    scale = dim ** -0.5
    c2 = scale * LOG2E

    @pl.when(step_id == 0)
    def _():
        dk_ref[...] = jnp.zeros_like(dk_ref)
        dv_ref[...] = jnp.zeros_like(dv_ref)

    dq_ref[...] = jnp.zeros_like(dq_ref)
    for h in range(group):
        prod = o_ref[0, h * dim:(h + 1) * dim, :].astype(F32) * do_ref[0, :, h * blk:(h + 1) * blk].astype(F32)
        delta_ref[:, h * blk:(h + 1) * blk] = jnp.sum(prod, axis=0, keepdims=True)

    def tile(j, masked):
        off = pl.multiple_of(j * blk, blk)
        s = dot(k_ref[pl.ds(off, blk), :], q_ref[0])
        p = jnp.exp2(s * c2 - lse_ref[0])
        if masked:
            p = jnp.where(causal_mask(s.shape[0], s.shape[1], blk), p, 0.0)
        dp = dot(v_ref[pl.ds(off, blk), :], do_ref[0]).astype(BF16).astype(F32)
        ds = (p * (dp - delta_ref[...])).astype(BF16)
        dv_ref[:, pl.ds(off, blk)] += dot(do_ref[0], p.astype(BF16), NT)
        dk_ref[:, pl.ds(off, blk)] += dot(q_ref[0], ds, NT)
        dq_ref[...] += dot(kt_ref[:, pl.ds(off, blk)], ds)

    def step(j, carry):
        tile(j, False)
        return carry

    lax.fori_loop(0, i, step, 0)
    tile(i, True)

    cos_t = cos_ref[...]
    sin_t = sin_ref[...]

    def rope_back(grad):
        grad = (grad * scale).astype(BF16).astype(F32)
        a = grad[:half]
        b = grad[half:]
        return (a * cos_t + b * sin_t).astype(BF16), (b * cos_t - a * sin_t).astype(BF16)

    for h in range(group):
        top, bottom = rope_back(dq_ref[:, h * blk:(h + 1) * blk])
        out_ref[0, h * dim:h * dim + half, :] = top
        out_ref[0, h * dim + half:(h + 1) * dim, :] = bottom
    off = pl.multiple_of(i * blk, blk)
    top, bottom = rope_back(dk_ref[:, pl.ds(off, blk)])
    base = group * dim
    out_ref[0, base:base + half, :] = top
    out_ref[0, base + half:base + dim, :] = bottom
    out_ref[0, base + dim:base + 2 * dim, :] = dv_ref[:, pl.ds(off, blk)].astype(BF16)


def weight_grad_kernel(n, g_ref, r_ref, g_hbm, dw_ref, swap_ref, acc_ref, got_ref, keep_sem, pair_send, pair_recv,
                       send_sem, recv_sem):
    i = pl.program_id(0)
    swap = Swap(n, g_hbm, swap_ref, send_sem, recv_sem)

    @pl.when(i == 0)
    def _():
        enter(swap.peers())
        swap.start()
        acc_ref[...] = jnp.zeros_like(acc_ref)

    @pl.when(i == swap.me)
    def _():
        swap.keep(g_ref.at[0], keep_sem)

    pair_sum(acc_ref, g_ref, r_ref[0], got_ref, dw_ref, pair_send, pair_recv, i == n - 1)

    @pl.when(i == n - 1)
    def _():
        swap.finish()


def spread_kernel(rows_q, dim, *refs):
    src_ref = refs[0]
    q_ref, k_ref, v_ref = refs[-3:]
    q_ref[0] = src_ref[0, :rows_q]
    k_ref[0] = src_ref[0, rows_q:rows_q + dim]
    v_ref[0] = src_ref[0, rows_q + dim:]


ANY = pl.BlockSpec(memory_space=pl.ANY)
DMA = pltpu.SemaphoreType.DMA


def call(kernel, grid, in_specs, out_specs, out_shape, name, flops, scratch=(), aliases=None, collective=None):
    params = {}
    if collective is not None:
        params = dict(collective_id=collective, has_side_effects=True)
    if grid:
        params['dimension_semantics'] = ('arbitrary',)
    return pl.pallas_call(
        kernel,
        grid=grid,
        in_specs=in_specs,
        out_specs=out_specs,
        out_shape=out_shape,
        scratch_shapes=list(scratch),
        input_output_aliases=aliases or {},
        name=name,
        cost_estimate=pl.CostEstimate(flops=int(flops), bytes_accessed=int(1e6), transcendentals=0),
        compiler_params=pltpu.CompilerParams(**params),
    )


def solution(mesh):
    n = mesh.shape['sp']
    chips = n // CORES

    def local_step(x_local, dy_local, gain, w_q, w_k, w_v, w_o):
        batch, blk, d_model = x_local.shape
        num_q, dim = w_q.shape[1], w_q.shape[2]
        num_kv = w_k.shape[1]
        assert num_kv == n and batch == CORES and chips == 4
        group = num_q // num_kv
        half = dim // 2
        seq = blk * n
        rows_q = group * dim
        rows = rows_q + 2 * dim
        cols = group * blk
        me = lax.axis_index('sp')
        chip = me // CORES
        sds = jax.ShapeDtypeStruct
        full = lambda *s: pl.BlockSpec(s, lambda i: (0,) * len(s))
        vmem = pl.BlockSpec(memory_space=pltpu.VMEM)

        wq_t = jnp.transpose(w_q, (1, 2, 0)).reshape(n, rows_q, d_model)
        wk_t = jnp.transpose(w_k, (1, 2, 0)).reshape(n, dim, d_model)
        wv_t = jnp.transpose(w_v, (1, 2, 0)).reshape(n, dim, d_model)
        w_all = jnp.concatenate([wq_t, wk_t, wv_t], axis=1)
        w_mine = lax.dynamic_slice_in_dim(w_all, chip * CORES, CORES, 0).reshape(CORES * rows, d_model)
        wo_flat = w_o.reshape(num_q * dim, d_model)
        wo_mine = lax.dynamic_slice_in_dim(wo_flat, chip * CORES * rows_q, CORES * rows_q, 0)
        cos_t, sin_t = rope_tables_t(seq, dim)
        x_hat, inv_rms, normed = norm_forward(x_local, gain)
        mm = 2.0 * seq * d_model
        att = 2.0 * seq * seq * dim * group / 2

        r_all, q_t, k, k_t, v, v_t = call(
            functools.partial(project_kernel, n, group, dim), (), [ANY, vmem, vmem, vmem],
            [ANY, vmem, vmem, vmem, vmem, vmem],
            [sds((n, blk, d_model), BF16), sds((CORES, n, dim, cols), BF16), sds((CORES, seq, dim), BF16),
             sds((CORES, dim, seq), BF16), sds((CORES, seq, dim), BF16), sds((CORES, dim, seq), BF16)],
            'project', mm * rows * 8,
            [pltpu.VMEM((blk, d_model), BF16), DMA, DMA((RING_SENDS,)), DMA((n,))],
            collective=0)(normed, w_mine, cos_t, sin_t)

        o_all, lse, dy_all = call(
            functools.partial(forward_kernel, n, group, dim, n + n - 2), (CORES * n,),
            [pl.BlockSpec((1, 1, dim, cols), lambda s: (s // n, s % n, 0, 0)),
             pl.BlockSpec((1, seq, dim), lambda s: (s // n, 0, 0)),
             pl.BlockSpec((1, dim, seq), lambda s: (s // n, 0, 0)), ANY],
            [pl.BlockSpec((1, rows_q, blk), lambda s: (s % n, s // n, 0)),
             pl.BlockSpec((1, 1, 1, cols), lambda s: (s // n, s % n, 0, 0)), ANY],
            [sds((n, CORES * rows_q, blk), BF16), sds((CORES, n, 1, cols), F32), sds((n, blk, d_model), BF16)],
            'forward', att * 16,
            [pltpu.VMEM((dim, cols), F32), pltpu.VMEM((1, cols), F32), pltpu.VMEM((1, cols), F32),
             pltpu.VMEM((blk, d_model), BF16), DMA, DMA((RING_SENDS,)), DMA((n,))],
            collective=1)(q_t, k, v_t, dy_local)

        swap_sems = [DMA, DMA, DMA, DMA((n,)), DMA((n,))]
        d_o, d_wo_mine, o_swap = call(
            functools.partial(out_grad_kernel, n, group, dim), (n,),
            [pl.BlockSpec((1, blk, d_model), lambda i: (i, 0, 0)), full(CORES * rows_q, d_model),
             pl.BlockSpec((1, CORES * rows_q, blk), lambda i: (i, 0, 0)), ANY],
            [pl.BlockSpec((CORES, 1, dim, cols), lambda i: (0, i, 0, 0)), full(rows_q, d_model), ANY],
            [sds((CORES, n, dim, cols), BF16), sds((rows_q, d_model), F32), sds((n, CORES * rows_q, blk), BF16)],
            'out_grad', mm * rows_q * 4,
            [pltpu.VMEM((CORES * rows_q, d_model), F32), pltpu.VMEM((rows_q, d_model), F32)] + swap_sems,
            collective=2)(dy_all, wo_mine, o_all, o_all)
        d_wo = lax.all_gather(d_wo_mine, 'sp', axis=0, tiled=True)

        y_proj = jnp.stack([dot(o_swap[b * chips:(b + 1) * chips].reshape(num_q * dim, blk), wo_flat, TN)
                            for b in range(batch)])
        y_out = (x_local.astype(F32) + y_proj).astype(BF16)

        w_by = w_all.reshape(chips, CORES, rows, d_model)
        d_normed = 0.0
        outs = None
        for g in range(CORES):
            rev4 = lambda a, b: pl.BlockSpec((None, 1, a, b), lambda s: (g, n - 1 - s, 0, 0))
            rev_lane = pl.BlockSpec((half, blk), lambda s: (0, n - 1 - s))
            part = lambda *s: pl.BlockSpec((None,) + s, lambda i: (g,) + (0,) * len(s))
            g_all = call(
                functools.partial(backward_kernel, group, dim), (n,),
                [rev4(dim, cols), rev4(dim, cols), pl.BlockSpec((1, rows_q, blk), lambda s: (n - 1 - s, g, 0)),
                 rev4(1, cols), part(seq, dim), part(dim, seq), part(seq, dim), rev_lane, rev_lane],
                pl.BlockSpec((1, rows, blk), lambda s: (n - 1 - s, 0, 0)), sds((n, rows, blk), BF16),
                'backward', att * 20,
                [pltpu.VMEM((dim, cols), F32), pltpu.VMEM((dim, seq), F32), pltpu.VMEM((dim, seq), F32),
                 pltpu.VMEM((1, cols), F32)])(q_t, d_o, o_all, lse, k, k_t, v, cos_t, sin_t)
            d_w_mine, g_swap = call(
                functools.partial(weight_grad_kernel, n), (n,),
                [pl.BlockSpec((1, rows, blk), lambda i: (i, 0, 0)),
                 pl.BlockSpec((1, blk, d_model), lambda i: (i, 0, 0)), ANY],
                [full(rows // CORES, d_model), ANY],
                [sds((rows // CORES, d_model), F32), sds((n, rows, blk), BF16)], 'weight_grad', mm * rows * 2,
                [pltpu.VMEM((rows, d_model), F32), pltpu.VMEM((rows // CORES, d_model), F32)] + swap_sems,
                collective=3 + g)(g_all, r_all, g_all)
            d_w = lax.all_gather(d_w_mine, 'sp', axis=0, tiled=True).reshape(chips, rows, d_model)
            first = outs is None
            outs = call(
                functools.partial(spread_kernel, rows_q, dim), (chips,),
                [pl.BlockSpec((1, rows, d_model), lambda i: (i, 0, 0))] + ([] if first else [ANY] * 3),
                [pl.BlockSpec((1, r, d_model), lambda i: (i * CORES + g, 0, 0)) for r in (rows_q, dim, dim)],
                [sds((n, r, d_model), F32) for r in (rows_q, dim, dim)], 'spread', 1e6,
                aliases=None if first else {1: 0, 2: 1, 3: 2})(d_w, *(outs or ()))
            w_g = w_by[:, g].reshape(chips * rows, d_model)
            d_normed = d_normed + jnp.stack(
                [dot(g_swap[b * chips:(b + 1) * chips].reshape(chips * rows, blk), w_g, TN) for b in range(batch)])

        d_normed = d_normed.astype(BF16).astype(F32)
        d_x_norm = norm_backward(d_normed, x_hat, inv_rms, gain)
        d_gain = lax.psum(jnp.sum(d_normed * x_hat, axis=(0, 1)), 'sp')
        d_x = (dy_local.astype(F32) + d_x_norm).astype(BF16)
        back = lambda t, h: jnp.transpose(t.reshape(h, dim, d_model), (2, 0, 1))
        return (y_out, d_x, back(outs[0], num_q), back(outs[1], num_kv), back(outs[2], num_kv),
                d_wo.reshape(num_q, dim, d_model), d_gain)

    specs_in = (P('dp', 'sp', None), P('dp', 'sp', None), P(None), P(None, None, None), P(None, None, None), P(None, None, None), P(None, None, None))
    specs_out = (P('dp', 'sp', None), P('dp', 'sp', None), P('dp', None, None), P('dp', None, None), P('dp', None, None), P('dp', None, None), P('dp'))
    return jax.shard_map(local_step, mesh=mesh, in_specs=specs_in, out_specs=specs_out, check_vma=False)
```

time: 787 us -> 668 us (0.85)
  Pallas kernels: 297 us -> 489 us
  waiting for transfers between devices: 253 us -> 69.6 us
  blocking collectives: 91.2 us -> 12.5 us
  local copies, waits for them, and re-layouts: 41.2 us -> 22.4 us
  matrix products: 35.3 us -> 20.2 us
  starting transfers between devices: 13.1 us -> 0.19 us
    pallas_call x10 -> x9, Pallas kernels: 297 us -> 489 us  [the longest x2 131 us: local_step(): call(functools.partial(backward_kernel, group, dim), (n,), [rev4(dim, col...]
    all_gather x7 -> x2, waiting for transfers between devices: 110 us -> 0.01 us  [local_step(): lax.all_gather(d_w_mine, 'sp', axis=0, tiled=True)]
    all_to_all x2 -> x0, blocking collectives: 77.8 us -> none  [local_step(): swap = lambda t: lax.all_to_all(t, 'sp', 0, 0, tiled=True)]
    all_to_all x2 -> x0, waiting for transfers between devices: 72.9 us -> none  [local_step(): swap = lambda t: lax.all_to_all(t, 'sp', 0, 0, tiled=True)]
    unnamed x46 -> x29, local copies, waits for them, and re-layouts: 29.8 us -> 12.7 us
    dot_general x4 -> x6, matrix products: 35.3 us -> 20.2 us  [dot(): return lax.dot_general(a, b, dims, preferred_element_type=F32)]
    all_to_all x2 -> x0, starting transfers between devices: 12.6 us -> none  [local_step(): swap = lambda t: lax.all_to_all(t, 'sp', 0, 0, tiled=True)]
  transfers between devices with their start and end apart: 10 -> 3, of which waited for: 6 -> 1; matrix products, arithmetic and copies ran while one was open for 8% -> 7% of each run, Pallas kernels for 25% -> 18%
where the time goes in v2:
time: 668 us; the launch traced here: 658 us
  Pallas kernels  489 us (73%)
  waiting for transfers between devices  69.6 us (10%)
  other arithmetic  30.4 us (5%)
  local copies, waits for them, and re-layouts  22.4 us (3%)
  matrix products  20.2 us (3%)
  between operations  14.5 us (2%)
  blocking collectives  12.5 us (2%)
    pallas_call x2, Pallas kernels, local_step(): call(functools.partial(backward_kernel, group, dim), (n,), [rev4(dim, col...  131 us
    pallas_call x1, Pallas kernels, local_step(): call(functools.partial(project_kernel, n, group, dim), (), [ANY, vmem, vm...  122 us
    pallas_call x1, Pallas kernels, local_step(): call(functools.partial(forward_kernel, n, group, dim, n + n - 2), (CORES...  109 us
    all_gather x1, waiting for transfers between devices, local_step(): d_wo = lax.all_gather(d_wo_mine, 'sp', axis=0, tiled=True)  68.8 us
    pallas_call x2, Pallas kernels, local_step(): call(functools.partial(weight_grad_kernel, n), (n,), [pl.BlockSpec((1, ro...  64.7 us
    pallas_call x1, Pallas kernels, local_step(): call(functools.partial(out_grad_kernel, n, group, dim), (n,), [pl.BlockSp...  42.9 us
    dot_general x6, matrix products, dot(): return lax.dot_general(a, b, dims, preferred_element_type=F32)  20.2 us
    pallas_call x2, Pallas kernels, local_step(): call(functools.partial(spread_kernel, rows_q, dim), (chips,), [pl.BlockSp...  18.7 us
  transfers between devices with their start and end apart: 3, of which 1 were waited for; matrix products, arithmetic and copies ran while one was open for 7% of the time, Pallas kernels for 18%

profile of v2, /device:TPU:113, one launch (start us, length us, event | category | flops | bytes accessed | tf_op | source)
XLA Modules:
  0.0 658.4 jit_solution(1731826488088932239)
XLA Ops:
  7.3 2.7 fusion.11
  10.1 3.1 fusion.8.r_hbm
  15.5 3.3 constant_dynamic-slice_fusion.w_ref
  18.8 3.0 fusion.15
  21.9 122.3 %project.1 = (bf16[8,384,2048]{2,1,0:T(8,128)(2,1)}, bf16[2,8,64,1536]{3,2,1,0:T(8,128)(2,1)}, bf16[2,3072,64]{2,1,0:T(8,128)(2,1)}, bf16[2,64,3072]{2,1,0:T(8,1...) custom-call(bf16[2,384,2048]{2,1,0:T(8,128)(2,1)} %fusion.8.r_hbm, bf16[768,2048]{1,0:T(8,128)(2,1)} %bitcast.80, ...), custom_call_target="tpu_custom_call" | custom-call | flops 38654705664 | bytes 1000000 | tf_op jit(solution)/shard_map/project/pallas_call | solution.py:483
  144.2 108.6 %forward.1 = (bf16[8,512,384]{2,1,0:T(8,128)(2,1)}, f32[2,8,1,1536]{3,2,1,0:T(1,128)}, bf16[8,384,2048]{2,1,0:T(8,128)(2,1)}) custom-call(bf16[2,8,64,1536]{3,2,1,0:T(8,128)(2,1)} %get-tuple-element.29.q_ref, bf16[2,3072,64]{2,1,0:T(8,128)(2,1)} %get-tuple-element.30.k_ref, bf16[2,64,3072]{2,1,0:T(8,128)(2,1)} %get-tuple-element.31.vt_ref, ...), custom_call_target="tpu_custom_call" | custom-call | flops 38654705664 | bytes 1000000 | tf_op jit(solution)/shard_map/forward/pallas_call | solution.py:492
  252.8 42.9 %out_grad.1 = (bf16[2,8,64,1536]{3,2,1,0:T(8,128)(2,1)}, f32[256,2048]{1,0:T(8,128)}, bf16[8,512,384]{2,1,0:T(8,128)(2,1)}) custom-call(bf16[8,384,2048]{2,1,0:T(8,128)(2,1)} %get-tuple-element.32.dy_ref, bf16[512,2048]{1,0:T(8,128)(2,1)} %constant_dynamic-slice_fusion.w_ref, bf16[8,512,384]{2,1,0:T(8,128)(2,1)} %get-tuple-element.33.o_ref.o_hbm, ...), custom_call_target="tpu_custom_call" | custom-call | flops 12884901888 | bytes 1000000 | tf_op jit(solution)/shard_map/out_grad/pallas_call | solution.py:506
  295.7 65.7 %backward.2.g_ref.g_hbm = bf16[8,384,384]{2,1,0:T(8,128)(2,1)} custom-call(bf16[2,8,64,1536]{3,2,1,0:T(8,128)(2,1)} %get-tuple-element.29.q_ref, bf16[2,8,64,1536]{3,2,1,0:T(8,128)(2,1)} %get-tuple-element.35.do_ref, bf16[8,512,384]{2,1,0:T(8,128)(2,1)} %get-tuple-element.33.o_ref.o_hbm, f32[2,8,1,1536]{3,2,1,0:T(1,128)} %get-tuple-element.36.lse_ref, ...), custom_call_target="tpu_custom_call" | custom-call | flops 48318382080 | bytes 1000000 | tf_op jit(solution)/shard_map/backward/pallas_call | solution.py:528
  361.4 32.4 %weight_grad.2 = (f32[192,2048]{1,0:T(8,128)}, bf16[8,384,384]{2,1,0:T(8,128)(2,1)}) custom-call(bf16[8,384,384]{2,1,0:T(8,128)(2,1)} %backward.2.g_ref.g_hbm, bf16[8,384,2048]{2,1,0:T(8,128)(2,1)} %get-tuple-element.39.r_ref, bf16[8,384,384]{2,1,0:T(8,128)(2,1)} %backward.2.g_ref.g_hbm), custom_call_target="tpu_custom_call" | custom-call | flops 9663676416 | bytes 1000000 | tf_op jit(solution)/shard_map/weight_grad/pallas_call | solution.py:536
  394.0 65.7 %backward.3.g_ref.g_hbm = bf16[8,384,384]{2,1,0:T(8,128)(2,1)} custom-call(bf16[2,8,64,1536]{3,2,1,0:T(8,128)(2,1)} %get-tuple-element.29.q_ref, bf16[2,8,64,1536]{3,2,1,0:T(8,128)(2,1)} %get-tuple-element.35.do_ref, bf16[8,512,384]{2,1,0:T(8,128)(2,1)} %get-tuple-element.33.o_ref.o_hbm, f32[2,8,1,1536]{3,2,1,0:T(1,128)} %get-tuple-element.36.lse_ref, ...), custom_call_target="tpu_custom_call" | custom-call | flops 48318382080 | bytes 1000000 | tf_op jit(solution)/shard_map/backward/pallas_call | solution.py:528
  459.7 32.3 %weight_grad.3 = (f32[192,2048]{1,0:T(8,128)}, bf16[8,384,384]{2,1,0:T(8,128)(2,1)}) custom-call(bf16[8,384,384]{2,1,0:T(8,128)(2,1)} %backward.3.g_ref.g_hbm, bf16[8,384,2048]{2,1,0:T(8,128)(2,1)} %get-tuple-element.39.r_ref, bf16[8,384,384]{2,1,0:T(8,128)(2,1)} %backward.3.g_ref.g_hbm), custom_call_target="tpu_custom_call" | custom-call | flops 9663676416 | bytes 1000000 | tf_op jit(solution)/shard_map/weight_grad/pallas_call | solution.py:536
  496.0 10.3 %pad_maximum_fusion = bf16[4,2,384,2048]{3,2,1,0:T(8,128)(2,1)S(1)} fusion(bf16[4,2,64,2048]{3,2,1,0:T(8,128)(2,1)S(1)} %bitcast.73, bf16[4,2,64,2048]{3,2,1,0:T(8,128)(2,1)S(1)} %bitcast.71, bf16[4,2,256,2048]{3,2,1,0:T(8,128)(2,1)} %bitcast.63), kind=kLoop, calls=%fused_computation.3 | loop fusion | flops 37748736 | bytes 25165824 | tf_op jit(solution)/shard_map/concatenate | solution.py:474
  508.0 2.7 convolution_bitcast_fusion
  513.4 2.7 convolution_bitcast_fusion.2
  516.1 2.7 convolution_bitcast_fusion.3
  518.8 3.7 fusion.10
  522.5 12.5 %psum.7 = f32[2048]{0:T(1024)} all-reduce(f32[2048]{0:T(1024)S(1)} %get-tuple-element.51), channel_id=1, replica_groups=mesh['dp'=2,'sp'=8] {'sp'}, use_global_device_ids=true, to_apply=%region_3.4 | all-reduce | flops 2048 | bytes 16384 | tf_op jit(solution)/shard_map/psum | solution.py:558
  537.4 6.0 convolution_bitcast_fusion.4
  543.5 3.5 convolution_bitcast_fusion.5
  547.0 5.2 fusion.7
  552.1 9.3 %spread.2 = (f32[8,256,2048]{2,1,0:T(8,128)}, f32[8,64,2048]{2,1,0:T(8,128)}, f32[8,64,2048]{2,1,0:T(8,128)}) custom-call(f32[4,384,2048]{2,1,0:T(8,128)} %bitcast.66), custom_call_target="tpu_custom_call" | custom-call | flops 1000000 | bytes 1000000 | tf_op jit(solution)/shard_map/spread/pallas_call | solution.py:546
  561.5 9.3 %spread.3 = (f32[8,256,2048]{2,1,0:T(8,128)}, f32[8,64,2048]{2,1,0:T(8,128)}, f32[8,64,2048]{2,1,0:T(8,128)}) custom-call(f32[4,384,2048]{2,1,0:T(8,128)} %bitcast.67, f32[8,256,2048]{2,1,0:T(8,128)} %get-tuple-element.44.refs_1_, f32[8,64,2048]{2,1,0:T(8,128)} %get-tuple-element.45.refs_2_, ...), custom_call_target="tpu_custom_call", output_to_operand_aliasing={{0}: (1, {}), {1}: (2, {}), {2}: (3, {})} | custom-call | flops 1000000 | bytes 1000000 | tf_op jit(solution)/shard_map/spread/pallas_call | solution.py:546
  570.8 68.8 %all-gather.8.cloned.1.call-done = f32[2048,2048]{1,0:T(8,128)} async-done(((f32[256,2048]{1,0:T(8,128)}), f32[2048,2048]{1,0:T(8,128)}) %all-gather.8.cloned.1.call-update) | async-done | bytes 16777232 | tf_op jit(solution)/shard_map/all_gather | solution.py:515
  639.6 11.8 %copy.21 = f32[32,64,2048]{2,1,0:T(8,128)} copy(f32[32,64,2048]{2,1,0:T(8,128)} %bitcast.64) | data formatting | bytes 33554432
  (47 shorter events, 13.3 us)
Async XLA Ops:
  7.2 2.9 copy-start
  7.2 545.0 %all-gather.6.cloned.1.call-start = ((), (), s32[]{:S(2)}) async-start(), calls=%async_computation.1 | async-start | bytes 14155776 | tf_op jit(solution)/shard_map/all_gather | solution.py:544
  10.0 8.8 %copy-start.10 = (f32[2,384]{1,0:T(2,128)}, f32[2,384]{1,0:T(2,128)S(1)}, u32[]{:S(2)}) copy-start(f32[2,384]{1,0:T(2,128)S(1)} %add_rsqrt_fusion) | copy-start | bytes 9220
  13.2 5.6 copy-start.3
  15.5 3.3 copy-start.5
  393.9 167.6 %all-gather.4.cloned.1.call-start = ((), (), s32[]{:S(2)}) async-start(), calls=%async_computation | async-start | bytes 14155776 | tf_op jit(solution)/shard_map/all_gather | solution.py:544
  492.0 2.9 copy-start.8
  492.0 147.6 %all-gather.8.cloned.1.call-start = ((), (), s32[]{:S(2)}) async-start(), calls=%async_computation.2 | async-start | bytes 18874368 | tf_op jit(solution)/shard_map/all_gather | solution.py:515
  492.8 2.5 copy-start.4
  492.9 3.1 copy-start.6
  516.0 2.7 copy-start.1
  516.0 2.7 copy-start.9
  516.0 2.7 copy-start.11
  535.0 8.4 %slice-start = ((s8[8388608]{0:T(1024)(128)(4,1)}), s8[4194304]{0:T(1024)(128)(4,1)S(1)}, s32[]{:S(2)}) async-start(s8[8388608]{0:T(1024)(128)(4,1)} %bitcast.59), calls=%async_computation.3 | async-start | bytes 8388608
  537.3 6.1 slice-start.1
  543.4 3.5 copy-start.2
  543.5 3.5 copy-start.7
Sparse Core Ops, SparseCore 0:
  394.0 64.0 all-gather.5
  492.2 64.3 all-gather.3
  558.2 81.3 all-gather.7

commit v3 on v2

v3 whole, which is shorter than its diff:
```python
import functools
import math
import jax
import jax.numpy as jnp
from jax import lax
from jax.experimental import pallas as pl
from jax.experimental.pallas import tpu as pltpu
from jax.sharding import PartitionSpec as P

ROPE_BASE = 1000000.0
NORM_EPS = 1e-5
LOG2E = math.log2(math.e)
NEG = -1e30
F32 = jnp.float32
BF16 = jnp.bfloat16

MESH = pl.DeviceIdType.MESH
CORES = 2

NN = (((1,), (0,)), ((), ()))
NT = (((1,), (1,)), ((), ()))
TN = (((0,), (0,)), ((), ()))


def dot(a, b, dims=NN):
    return lax.dot_general(a, b, dims, preferred_element_type=F32)


def rope_tables_t(seq_len, head_dim):
    half = head_dim // 2
    inv_freq = ROPE_BASE ** (-2.0 * jnp.arange(half, dtype=F32) / head_dim)
    angle = jnp.arange(seq_len).astype(F32)[None, :] * inv_freq[:, None]
    return jnp.cos(angle), jnp.sin(angle)


def norm_forward(x_local):
    x_f32 = x_local.astype(F32)
    inv_rms = lax.rsqrt(jnp.mean(x_f32 * x_f32, axis=-1, keepdims=True) + NORM_EPS)
    return x_f32 * inv_rms, inv_rms


def norm_backward(d_normed, x_hat, inv_rms, gain):
    d_hat = d_normed * gain
    return inv_rms * (d_hat - x_hat * jnp.mean(d_hat * x_hat, axis=-1, keepdims=True))


def remote(src, dst, send_sem, recv_sem, target):
    return pltpu.make_async_remote_copy(src_ref=src, dst_ref=dst, send_sem=send_sem, recv_sem=recv_sem,
                                        device_id={'sp': target}, device_id_type=MESH)


def enter(targets):
    barrier = pltpu.get_barrier_semaphore()
    for t in targets:
        pl.semaphore_signal(barrier, inc=1, device_id={'sp': t}, device_id_type=MESH)
    pl.semaphore_wait(barrier, len(targets))


class Ring:
    def __init__(self, n, src_ref, all_ref, send_sem, recv_sem):
        self.n, self.src, self.all, self.send_sem, self.recv_sem = n, src_ref, all_ref, send_sem, recv_sem
        me = lax.axis_index('sp')
        self.me, self.chip, self.core = me, me // CORES, me % CORES
        self.partner = self.at(0, 1 - self.core)
        self.ahead = 1 - 2 * self.core

    def at(self, hop, core):
        chips = self.n // CORES
        return (self.chip + hop + chips) % chips * CORES + core

    def neighbours(self):
        return [self.partner] + [self.at(hop, core) for hop in (1, -1) for core in range(CORES)]

    def copy(self, src, slot, k, target):
        return remote(src, self.all.at[slot], self.send_sem.at[k], self.recv_sem.at[slot], target)

    def direct(self, stage):
        hop = self.ahead if stage == 0 else -self.ahead
        b, o = self.core, 1 - self.core
        return [self.copy(self.src.at[b], self.me, 2 * stage, self.at(hop, b)),
                self.copy(self.src.at[o], self.me, 2 * stage + 1, self.at(hop, o))]

    def across(self):
        return [self.copy(self.src.at[1 - self.core], self.me, 4, self.partner)]

    def relayed(self):
        first, second = self.at(-1, 0), self.at(1, 1)
        return [self.copy(self.all.at[first], first, 5, self.at(1, self.core)),
                self.copy(self.all.at[second], second, 6, self.at(-1, self.core))]

    def wait_block(self, slot):
        self.copy(self.all.at[slot], slot, 0, self.partner).wait_recv()

    def order(self):
        b, o, a = self.core, 1 - self.core, self.ahead
        return [self.me, self.partner, self.at(-a, b), self.at(a, o), self.at(2, 0), self.at(2, 1),
                self.at(a, b), self.at(-a, o)]

    def wait_sends(self):
        for c in self.direct(0) + self.direct(1) + self.across() + self.relayed():
            c.wait_send()


RING_SENDS = 7


def start(copies):
    for c in copies:
        c.start()


def local(src, dst, sem):
    c = pltpu.make_async_copy(src, dst, sem)
    c.start()
    return c


def project_kernel(n, group, dim, x_hbm, gain_ref, wq_hbm, wk_hbm, wv_hbm, cos_ref, sin_ref, x_all, r_all, q_ref, k_ref,
                   kt_ref, v_ref, vt_ref, x_ref, r_ref, w_ref, load_sem, store_sem, w_sem, send_sem, recv_sem):
    half = dim // 2
    blk = x_ref.shape[0]
    rows_q = group * dim
    rows = rows_q + 2 * dim
    ring = Ring(n, x_hbm, x_all, send_sem, recv_sem)
    enter(ring.neighbours())
    start(ring.direct(0) + ring.across())
    weights = []
    for g in range(CORES):
        head = ring.chip * CORES + g
        weights.append(pltpu.make_async_copy(wq_hbm.at[head], w_ref.at[pl.ds(g * rows, rows_q)], w_sem))
        weights.append(pltpu.make_async_copy(wk_hbm.at[head], w_ref.at[pl.ds(g * rows + rows_q, dim)], w_sem))
        weights.append(pltpu.make_async_copy(wv_hbm.at[head], w_ref.at[pl.ds(g * rows + rows_q + dim, dim)], w_sem))
    start(weights)
    order = ring.order()

    def body(p, carry):
        slot = order[0]
        for k in range(1, n):
            slot = jnp.where(p == k, order[k], slot)

        @pl.when(p == 0)
        def _():
            local(x_hbm.at[ring.core], x_ref, load_sem).wait()

        for k in range(1, n):
            @pl.when(p == k)
            def _(k=k):
                ring.wait_block(order[k])
                if k == 3:
                    start(ring.relayed() + ring.direct(1))
                local(x_all.at[order[k]], x_ref, load_sem).wait()

        @pl.when(p > 0)
        def _():
            pltpu.make_async_copy(r_ref, r_all.at[slot], store_sem).wait()

        x = x_ref[...].astype(F32)
        inv_rms = lax.rsqrt(jnp.mean(x * x, axis=-1, keepdims=True) + NORM_EPS)
        r_ref[...] = (x * inv_rms * gain_ref[...]).astype(BF16)
        pltpu.make_async_copy(r_ref, r_all.at[slot], store_sem).start()

        @pl.when(p == 0)
        def _():
            for c in weights:
                c.wait()

        off = pl.multiple_of(slot * blk, blk)
        cos_t = cos_ref[:, pl.ds(off, blk)]
        sin_t = sin_ref[:, pl.ds(off, blk)]
        for g in range(CORES):
            lin = dot(w_ref[g * rows:(g + 1) * rows], r_ref[...], NT)
            for h in range(group):
                a = lin[h * dim:h * dim + half]
                b = lin[h * dim + half:(h + 1) * dim]
                q_ref[g, slot, :half, h * blk:(h + 1) * blk] = (a * cos_t - b * sin_t).astype(BF16)
                q_ref[g, slot, half:, h * blk:(h + 1) * blk] = (b * cos_t + a * sin_t).astype(BF16)
            a = lin[rows_q:rows_q + half]
            b = lin[rows_q + half:rows_q + dim]
            v = lin[rows_q + dim:]
            kv = jnp.concatenate([a * cos_t - b * sin_t, b * cos_t + a * sin_t, v], axis=0)
            kt_ref[g, :, pl.ds(off, blk)] = kv[:dim].astype(BF16)
            vt_ref[g, :, pl.ds(off, blk)] = v.astype(BF16)
            kv_t = kv.T.astype(BF16)
            k_ref[g, pl.ds(off, blk), :] = kv_t[:, :dim]
            v_ref[g, pl.ds(off, blk), :] = kv_t[:, dim:]
        return carry

    lax.fori_loop(0, n, body, 0)
    pltpu.make_async_copy(r_ref, r_all.at[ring.me], store_sem).wait()
    ring.wait_sends()


def causal_mask(rows, cols, blk):
    key = lax.broadcasted_iota(jnp.int32, (rows, cols), 0)
    qry = lax.broadcasted_iota(jnp.int32, (rows, cols), 1) % blk
    return key <= qry


def forward_kernel(n, group, dim, q_ref, k_ref, vt_ref, dy_hbm, o_ref, lse_ref, all_ref, acc_ref, m_ref, l_ref,
                   bounce_ref, load_sem, send_sem, recv_sem):
    blk = o_ref.shape[2]
    step_id = pl.program_id(0)
    i = step_id % n
    c2 = dim ** -0.5 * LOG2E
    ring = Ring(n, dy_hbm, all_ref, send_sem, recv_sem)
    order = ring.order()

    @pl.when(step_id == 0)
    def _():
        enter(ring.neighbours())
        start(ring.direct(0) + ring.across())
        local(dy_hbm.at[ring.core], bounce_ref, load_sem).wait()
        local(bounce_ref, all_ref.at[ring.me], load_sem)

    @pl.when(step_id == n - 2)
    def _():
        start(ring.direct(1))

    @pl.when(step_id == n)
    def _():
        ring.wait_block(order[2])
        ring.wait_block(order[3])
        start(ring.relayed())

    acc_ref[...] = jnp.zeros_like(acc_ref)
    l_ref[...] = jnp.zeros_like(l_ref)
    m_ref[...] = jnp.full_like(m_ref, NEG)

    def tile(j, masked):
        off = pl.multiple_of(j * blk, blk)
        s = dot(k_ref[0, pl.ds(off, blk), :], q_ref[0, 0])
        if masked:
            s = jnp.where(causal_mask(s.shape[0], s.shape[1], blk), s, NEG)
        m_old = m_ref[...]
        m_new = jnp.maximum(m_old, jnp.max(s, axis=0, keepdims=True) * c2)
        p = jnp.exp2(s * c2 - m_new)
        alpha = jnp.exp2(m_old - m_new)
        m_ref[...] = m_new
        l_ref[...] = l_ref[...] * alpha + jnp.sum(p, axis=0, keepdims=True)
        acc_ref[...] = acc_ref[...] * alpha + dot(vt_ref[0, :, pl.ds(off, blk)], p.astype(BF16))

    def step(j, carry):
        tile(j, False)
        return carry

    lax.fori_loop(0, i, step, 0)
    tile(i, True)
    l_val = l_ref[...]
    o = (acc_ref[...] * (1.0 / l_val)).astype(BF16)
    for h in range(group):
        o_ref[0, h * dim:(h + 1) * dim, :] = o[:, h * blk:(h + 1) * blk]
    lse_ref[0, 0] = m_ref[...] + jnp.log2(l_val)

    @pl.when(step_id == pl.num_programs(0) - 1)
    def _():
        pltpu.make_async_copy(bounce_ref, all_ref.at[ring.me], load_sem).wait()
        for k in (1, 4, 5, 6, 7):
            ring.wait_block(order[k])
        ring.wait_sends()


class Swap:
    def __init__(self, n, src_ref, dst_ref, send_sem, recv_sem):
        self.n, self.src, self.dst, self.send_sem, self.recv_sem = n, src_ref, dst_ref, send_sem, recv_sem
        self.me = lax.axis_index('sp')

    def slot(self, dev):
        return dev % CORES * (self.n // CORES) + dev // CORES

    def peers(self):
        return [(self.me + d) % self.n for d in range(1, self.n)]

    def sends(self):
        mine = self.slot(self.me)
        return [remote(self.src.at[t], self.dst.at[mine], self.send_sem.at[d], self.recv_sem.at[mine], t)
                for d, t in enumerate(self.peers())]

    def keep(self, block, sem):
        local(block, self.dst.at[self.slot(self.me)], sem).wait()

    def finish(self):
        for d, t in enumerate(self.peers()):
            s = self.slot(t)
            remote(self.src.at[t], self.dst.at[s], self.send_sem.at[d], self.recv_sem.at[s], t).wait_recv()
        for c in self.sends():
            c.wait_send()


class Spread:
    def __init__(self, n, all_ref, send_sem, recv_sem):
        self.all, self.send_sem, self.recv_sem = all_ref, send_sem, recv_sem
        self.chips = n // CORES
        me = lax.axis_index('sp')
        self.chip, self.core = me // CORES, me % CORES
        self.cut = all_ref.shape[2] // 2

    def chip_at(self, hop):
        return (self.chip + hop + self.chips) % self.chips

    def piece(self, hop, part):
        ref = self.all.at[self.chip_at(hop), self.core]
        if part is not None:
            ref = ref.at[pl.ds(part * self.cut, self.cut)]
        return ref

    def copy(self, hop, part, send, recv, to):
        ref = self.piece(hop, part)
        core = 1 - self.core if to == 0 else self.core
        return remote(ref, ref, self.send_sem.at[send], self.recv_sem.at[recv], self.chip_at(to) * CORES + core)

    def direct(self):
        return [self.copy(0, None, 0, 0, 1), self.copy(0, None, 1, 1, -1), self.copy(0, None, 2, 4, 0)]

    def relay(self):
        return [self.copy(-1, 0, 3, 2, 1), self.copy(1, 1, 4, 3, -1), self.copy(-1, None, 5, 5, 0), self.copy(1, None, 6, 6, 0)]

    def last(self):
        return [self.copy(2, 0, 7, 7, 0), self.copy(2, 1, 8, 8, 0)]

    def wait_near(self):
        self.copy(-1, None, 0, 0, 1).wait_recv()
        self.copy(1, None, 0, 1, 1).wait_recv()

    def wait_far(self):
        self.copy(2, 0, 0, 2, 1).wait_recv()
        self.copy(2, 1, 0, 3, 1).wait_recv()

    def finish(self):
        self.wait_far()
        start(self.last())
        for k, part in ((4, None), (5, None), (6, None), (7, 0), (8, 1)):
            self.copy(0, part, 0, k, 1).wait_recv()
        for c in self.direct() + self.relay() + self.last():
            c.wait_send()


SPREAD_SENDS = 9


def enter_all(n):
    me = lax.axis_index('sp')
    enter([(me + d) % n for d in range(1, n)])


def pair_sum(acc_ref, lhs, rhs, got_ref, mine_ref, send_sem, recv_sem):
    me = lax.axis_index('sp')
    core = me % CORES
    size = acc_ref.shape[0] // CORES
    halves = [pl.ds(pl.multiple_of(part * size, size), size) for part in (1 - core, core)]
    copy = remote(acc_ref.at[halves[0]], got_ref, send_sem, recv_sem, me - core + 1 - core)
    for k, rows in enumerate(halves):
        acc_ref[rows, :] += dot(lhs[rows, :], rhs)
        if k == 0:
            copy.start()
    copy.wait()
    mine_ref[...] = acc_ref[halves[1], :] + got_ref[...]


def weight_step(s, count, acc_ref, lhs_ref, rhs_ref, wide_ref, got_ref, mine_ref, pair_send, pair_recv):
    blocks, blk = lhs_ref.shape[0], lhs_ref.shape[2]
    for k in range(blocks):
        wide_ref[:, k * blk:(k + 1) * blk] = lhs_ref[k]
    rhs = rhs_ref[...].reshape(blocks * blk, rhs_ref.shape[2])

    @pl.when(s == 0)
    def _():
        acc_ref[...] = dot(wide_ref[...], rhs)

    @pl.when((s > 0) & (s < count - 1))
    def _():
        acc_ref[...] += dot(wide_ref[...], rhs)

    @pl.when(s == count - 1)
    def _():
        pair_sum(acc_ref, wide_ref, rhs, got_ref, mine_ref, pair_send, pair_recv)


def backward_step(t, n, group, dim, q_ref, do_ref, o_ref, lse_ref, k_ref, kt_ref, v_ref, cos_ref, sin_ref, out_ref,
                  dq_ref, dk_ref, dv_ref, delta_ref):
    blk = out_ref.shape[2]
    half = dim // 2
    i = n - 1 - t
    scale = dim ** -0.5
    c2 = scale * LOG2E

    @pl.when(t == 0)
    def _():
        dk_ref[...] = jnp.zeros_like(dk_ref)
        dv_ref[...] = jnp.zeros_like(dv_ref)

    dq_ref[...] = jnp.zeros_like(dq_ref)
    for h in range(group):
        prod = o_ref[0, h * dim:(h + 1) * dim, :].astype(F32) * do_ref[i, :, h * blk:(h + 1) * blk].astype(F32)
        delta_ref[:, h * blk:(h + 1) * blk] = jnp.sum(prod, axis=0, keepdims=True)

    def tile(j, masked):
        off = pl.multiple_of(j * blk, blk)
        s = dot(k_ref[pl.ds(off, blk), :], q_ref[0])
        p = jnp.exp2(s * c2 - lse_ref[0])
        if masked:
            p = jnp.where(causal_mask(s.shape[0], s.shape[1], blk), p, 0.0)
        dp = dot(v_ref[pl.ds(off, blk), :], do_ref[i]).astype(BF16).astype(F32)
        ds = (p * (dp - delta_ref[...])).astype(BF16)
        dv_ref[:, pl.ds(off, blk)] += dot(do_ref[i], p.astype(BF16), NT)
        dk_ref[:, pl.ds(off, blk)] += dot(q_ref[0], ds, NT)
        dq_ref[...] += dot(kt_ref[:, pl.ds(off, blk)], ds)

    def step(j, carry):
        tile(j, False)
        return carry

    lax.fori_loop(0, i, step, 0)
    tile(i, True)

    cos_t = cos_ref[...]
    sin_t = sin_ref[...]

    def rope_back(grad):
        grad = (grad * scale).astype(BF16).astype(F32)
        a = grad[:half]
        b = grad[half:]
        return (a * cos_t + b * sin_t).astype(BF16), (b * cos_t - a * sin_t).astype(BF16)

    for h in range(group):
        top, bottom = rope_back(dq_ref[:, h * blk:(h + 1) * blk])
        out_ref[0, h * dim:h * dim + half, :] = top
        out_ref[0, h * dim + half:(h + 1) * dim, :] = bottom
    off = pl.multiple_of(i * blk, blk)
    top, bottom = rope_back(dk_ref[:, pl.ds(off, blk)])
    base = group * dim
    out_ref[0, base:base + half, :] = top
    out_ref[0, base + half:base + dim, :] = bottom
    out_ref[0, base + dim:base + 2 * dim, :] = dv_ref[:, pl.ds(off, blk)].astype(BF16)


RELAY_AT = 5


def first_backward_kernel(n, group, dim, count, dy_ref, w_ref, o2_ref, o_hbm, q_ref, o_ref, lse_ref, k_ref, kt_ref, v_ref,
                          cos_ref, sin_ref, g_ref, do1_ref, swap_ref, dw_all, acc_ref, wide_ref, got_ref, mine_ref,
                          do_ref, dq_ref, dk_ref, dv_ref, delta_ref, sem, pair_send, pair_recv, send_sem, recv_sem,
                          spread_send, spread_recv):
    s = pl.program_id(0)
    blk = g_ref.shape[2]
    swap = Swap(n, o_hbm, swap_ref, send_sem, recv_sem)
    spread = Spread(n, dw_all, spread_send, spread_recv)
    early = n // 2 - 1

    @pl.when(s == 0)
    def _():
        enter_all(n)
        start(swap.sends()[:early])

    @pl.when(s < count)
    def _():
        weight_step(s, count, acc_ref, o2_ref, dy_ref, wide_ref, got_ref, mine_ref, pair_send, pair_recv)

    for k in range(o2_ref.shape[0]):
        @pl.when((s < count) & (s * o2_ref.shape[0] + k == swap.me))
        def _(k=k):
            swap.keep(o2_ref.at[k], sem)

    @pl.when(s == count - 1)
    def _():
        local(mine_ref, spread.piece(0, None), sem).wait()
        start(spread.direct())
        start(swap.sends()[early:])

    @pl.when((s >= count) & (s < 2 * count))
    def _():
        blocks = dy_ref.shape[0]
        d_o = dot(w_ref[...], dy_ref[...].reshape(blocks * blk, dy_ref.shape[2]), NT).astype(BF16)
        for k in range(blocks):
            i = (s - count) * blocks + k
            for h in range(group):
                do_ref[i, :, h * blk:(h + 1) * blk] = d_o[h * dim:(h + 1) * dim, k * blk:(k + 1) * blk]
                do1_ref[i, :, h * blk:(h + 1) * blk] = d_o[(group + h) * dim:(group + h + 1) * dim, k * blk:(k + 1) * blk]

    t = s - 2 * count

    @pl.when(t == RELAY_AT)
    def _():
        spread.wait_near()
        start(spread.relay())

    @pl.when(t >= 0)
    def _():
        backward_step(t, n, group, dim, q_ref, do_ref, o_ref, lse_ref, k_ref, kt_ref, v_ref, cos_ref, sin_ref, g_ref,
                      dq_ref, dk_ref, dv_ref, delta_ref)

    @pl.when(t == n - 1)
    def _():
        spread.finish()
        swap.finish()


def second_backward_kernel(n, group, dim, count, g2_ref, g_hbm, r_ref, q_ref, do_ref, o_ref, lse_ref, k_ref, kt_ref,
                           v_ref, cos_ref, sin_ref, g_ref, swap_ref, dw_all, acc_ref, wide_ref, got_ref, mine_ref,
                           dq_ref, dk_ref, dv_ref, delta_ref, sem, pair_send, pair_recv, send_sem, recv_sem,
                           spread_send, spread_recv):
    s = pl.program_id(0)
    swap = Swap(n, g_hbm, swap_ref, send_sem, recv_sem)
    spread = Spread(n, dw_all, spread_send, spread_recv)

    @pl.when(s == 0)
    def _():
        enter_all(n)
        start(swap.sends())

    @pl.when(s < count)
    def _():
        weight_step(s, count, acc_ref, g2_ref, r_ref, wide_ref, got_ref, mine_ref, pair_send, pair_recv)

    for k in range(g2_ref.shape[0]):
        @pl.when((s < count) & (s * g2_ref.shape[0] + k == swap.me))
        def _(k=k):
            swap.keep(g2_ref.at[k], sem)

    @pl.when(s == count - 1)
    def _():
        local(mine_ref, spread.piece(0, None), sem).wait()
        start(spread.direct())

    t = s - count

    @pl.when(t == RELAY_AT)
    def _():
        spread.wait_near()
        start(spread.relay())

    @pl.when(t >= 0)
    def _():
        backward_step(t, n, group, dim, q_ref, do_ref, o_ref, lse_ref, k_ref, kt_ref, v_ref, cos_ref, sin_ref, g_ref,
                      dq_ref, dk_ref, dv_ref, delta_ref)

    @pl.when(t == n - 1)
    def _():
        spread.finish()
        swap.finish()


def weight_grad_kernel(n, count, g2_ref, g_hbm, r_ref, mine_ref, swap_ref, acc_ref, wide_ref, got_ref, sem, pair_send,
                       pair_recv, send_sem, recv_sem):
    s = pl.program_id(0)
    swap = Swap(n, g_hbm, swap_ref, send_sem, recv_sem)

    @pl.when(s == 0)
    def _():
        enter_all(n)
        start(swap.sends())

    weight_step(s, count, acc_ref, g2_ref, r_ref, wide_ref, got_ref, mine_ref, pair_send, pair_recv)
    for k in range(g2_ref.shape[0]):
        @pl.when(s * g2_ref.shape[0] + k == swap.me)
        def _(k=k):
            swap.keep(g2_ref.at[k], sem)

    @pl.when(s == count - 1)
    def _():
        swap.finish()


def spread_kernel(rows_q, dim, *refs):
    src_ref = refs[0]
    q_ref, k_ref, v_ref = refs[-3:]
    q_ref[0] = src_ref[0, :rows_q]
    k_ref[0] = src_ref[0, rows_q:rows_q + dim]
    v_ref[0] = src_ref[0, rows_q + dim:]


ANY = pl.BlockSpec(memory_space=pl.ANY)
DMA = pltpu.SemaphoreType.DMA


def call(kernel, grid, in_specs, out_specs, out_shape, name, flops, scratch=(), aliases=None, collective=None):
    params = {}
    if collective is not None:
        params = dict(collective_id=collective, has_side_effects=True)
    if grid:
        params['dimension_semantics'] = ('arbitrary',)
    return pl.pallas_call(
        kernel,
        grid=grid,
        in_specs=in_specs,
        out_specs=out_specs,
        out_shape=out_shape,
        scratch_shapes=list(scratch),
        input_output_aliases=aliases or {},
        name=name,
        cost_estimate=pl.CostEstimate(flops=int(flops), bytes_accessed=int(1e6), transcendentals=0),
        compiler_params=pltpu.CompilerParams(**params),
    )


def solution(mesh):
    n = mesh.shape['sp']
    chips = n // CORES

    def local_step(x_local, dy_local, gain, w_q, w_k, w_v, w_o):
        batch, blk, d_model = x_local.shape
        num_q, dim = w_q.shape[1], w_q.shape[2]
        num_kv = w_k.shape[1]
        assert num_kv == n and batch == CORES and chips == 4
        group = num_q // num_kv
        half = dim // 2
        seq = blk * n
        rows_q = group * dim
        rows = rows_q + 2 * dim
        cols = group * blk
        count = n // 2
        me = lax.axis_index('sp')
        chip = me // CORES
        sds = jax.ShapeDtypeStruct
        full = lambda *s: pl.BlockSpec(s, lambda i: (0,) * len(s))
        vmem = pl.BlockSpec(memory_space=pltpu.VMEM)

        wq_t = jnp.transpose(w_q, (1, 2, 0)).reshape(n, rows_q, d_model)
        wk_t = jnp.transpose(w_k, (1, 2, 0)).reshape(n, dim, d_model)
        wv_t = jnp.transpose(w_v, (1, 2, 0)).reshape(n, dim, d_model)
        wo_flat = w_o.reshape(num_q * dim, d_model)
        cos_t, sin_t = rope_tables_t(seq, dim)
        mm = 2.0 * seq * d_model
        att = 2.0 * seq * seq * dim * group / 2

        _, r_all, q_t, k, k_t, v, v_t = call(
            functools.partial(project_kernel, n, group, dim), (), [ANY, vmem, ANY, ANY, ANY, vmem, vmem],
            [ANY, ANY, vmem, vmem, vmem, vmem, vmem],
            [sds((n, blk, d_model), BF16), sds((n, blk, d_model), BF16), sds((CORES, n, dim, cols), BF16),
             sds((CORES, seq, dim), BF16), sds((CORES, dim, seq), BF16), sds((CORES, seq, dim), BF16),
             sds((CORES, dim, seq), BF16)],
            'project', mm * rows * 8,
            [pltpu.VMEM((blk, d_model), BF16), pltpu.VMEM((blk, d_model), BF16), pltpu.VMEM((CORES * rows, d_model), BF16),
             DMA, DMA, DMA, DMA((RING_SENDS,)), DMA((n,))],
            collective=0)(x_local, gain.reshape(1, d_model), wq_t, wk_t, wv_t, cos_t, sin_t)

        o_all, lse, dy_all = call(
            functools.partial(forward_kernel, n, group, dim), (CORES * n,),
            [pl.BlockSpec((1, 1, dim, cols), lambda s: (s // n, s % n, 0, 0)),
             pl.BlockSpec((1, seq, dim), lambda s: (s // n, 0, 0)),
             pl.BlockSpec((1, dim, seq), lambda s: (s // n, 0, 0)), ANY],
            [pl.BlockSpec((1, rows_q, blk), lambda s: (s % n, s // n, 0)),
             pl.BlockSpec((1, 1, 1, cols), lambda s: (s // n, s % n, 0, 0)), ANY],
            [sds((n, CORES * rows_q, blk), BF16), sds((CORES, n, 1, cols), F32), sds((n, blk, d_model), BF16)],
            'forward', att * 16,
            [pltpu.VMEM((dim, cols), F32), pltpu.VMEM((1, cols), F32), pltpu.VMEM((1, cols), F32),
             pltpu.VMEM((blk, d_model), BF16), DMA, DMA((RING_SENDS,)), DMA((n,))],
            collective=1)(q_t, k, v_t, dy_local)

        def backward_specs(g, lead):
            step = lambda s: n - 1 - jnp.maximum(s - lead, 0)
            rev = lambda *s: pl.BlockSpec((None, 1) + s, lambda i: (g, step(i), 0, 0))
            part = lambda *s: pl.BlockSpec((None,) + s, lambda i: (g, 0, 0))
            lane = pl.BlockSpec((half, blk), lambda i: (0, step(i)))
            ins = dict(q=rev(dim, cols), o=pl.BlockSpec((1, rows_q, blk), lambda i: (step(i), g, 0)), lse=rev(1, cols),
                       k=part(seq, dim), kt=part(dim, seq), v=part(seq, dim), cos=lane, sin=lane)
            return ins, pl.BlockSpec((1, rows, blk), lambda i: (step(i), 0, 0))

        pair = lambda s: jnp.minimum(s, count - 1)
        back_scratch = [pltpu.VMEM((dim, cols), F32), pltpu.VMEM((dim, seq), F32), pltpu.VMEM((dim, seq), F32),
                        pltpu.VMEM((1, cols), F32)]
        sum_scratch = lambda r, out: [pltpu.VMEM((r, d_model), F32), pltpu.VMEM((r, 2 * blk), BF16),
                                      pltpu.VMEM((r // CORES, d_model), F32)] + (
                                          [pltpu.VMEM((r // CORES, d_model), F32)] if out else [])
        swap_sems = [DMA, DMA, DMA, DMA((n,)), DMA((n,))]
        spread_sems = [DMA((SPREAD_SENDS,)), DMA((SPREAD_SENDS,))]

        ins, g_spec = backward_specs(0, 2 * count)
        g_0, d_o1, o_swap, d_wo = call(
            functools.partial(first_backward_kernel, n, group, dim, count), (2 * count + n,),
            [pl.BlockSpec((2, blk, d_model), lambda s: (jnp.where(s < count, s, jnp.minimum(s - count, count - 1)), 0, 0)),
             full(CORES * rows_q, d_model), pl.BlockSpec((2, CORES * rows_q, blk), lambda s: (pair(s), 0, 0)), ANY] + list(ins.values()),
            [g_spec, full(n, dim, cols), ANY, ANY],
            [sds((n, rows, blk), BF16), sds((n, dim, cols), BF16), sds((n, CORES * rows_q, blk), BF16),
             sds((chips, CORES, rows_q, d_model), F32)],
            'backward_0', att * 20 + mm * rows_q * 4,
            sum_scratch(CORES * rows_q, True) + [pltpu.VMEM((n, dim, cols), BF16)] + back_scratch + swap_sems + spread_sems,
            collective=2)(dy_all, lax.dynamic_slice_in_dim(wo_flat, chip * CORES * rows_q, CORES * rows_q, 0), o_all, o_all,
                          q_t, o_all, lse, k, k_t, v, cos_t, sin_t)

        ins, g_spec = backward_specs(1, count)
        pair_specs = [pl.BlockSpec((2, rows, blk), lambda s: (pair(s), 0, 0)), ANY,
                      pl.BlockSpec((2, blk, d_model), lambda s: (pair(s), 0, 0))]
        ins = list(ins.values())
        g_1, g_swap0, d_w0 = call(
            functools.partial(second_backward_kernel, n, group, dim, count), (count + n,),
            pair_specs + [ins[0], full(n, dim, cols)] + ins[1:], [g_spec, ANY, ANY],
            [sds((n, rows, blk), BF16), sds((n, rows, blk), BF16), sds((chips, CORES, rows // CORES, d_model), F32)],
            'backward_1', att * 20 + mm * rows,
            sum_scratch(rows, True) + back_scratch + swap_sems + spread_sems,
            collective=3)(g_0, g_0, r_all, q_t, d_o1, o_all, lse, k, k_t, v, cos_t, sin_t)

        d_w1, g_swap1 = call(
            functools.partial(weight_grad_kernel, n, count), (count,), pair_specs, [full(rows // CORES, d_model), ANY],
            [sds((rows // CORES, d_model), F32), sds((n, rows, blk), BF16)], 'weight_grad', mm * rows,
            sum_scratch(rows, False) + swap_sems, collective=4)(g_1, g_1, r_all)
        d_w1 = lax.all_gather(d_w1, 'sp', axis=0, tiled=True)

        y_proj = jnp.stack([dot(o_swap[b * chips:(b + 1) * chips].reshape(num_q * dim, blk), wo_flat, TN)
                            for b in range(batch)])
        y_out = (x_local.astype(F32) + y_proj).astype(BF16)

        d_normed = 0.0
        outs = ()
        for g, (d_w, g_swap) in enumerate(((d_w0, g_swap0), (d_w1, g_swap1))):
            outs = call(
                functools.partial(spread_kernel, rows_q, dim), (chips,),
                [pl.BlockSpec((1, rows, d_model), lambda i: (i, 0, 0))] + [ANY] * len(outs),
                [pl.BlockSpec((1, r, d_model), lambda i: (i * CORES + g, 0, 0)) for r in (rows_q, dim, dim)],
                [sds((n, r, d_model), F32) for r in (rows_q, dim, dim)], 'spread', 1e6,
                aliases={1: 0, 2: 1, 3: 2} if outs else None)(d_w.reshape(chips, rows, d_model), *outs)
            of = lambda w: w.reshape(chips, CORES, -1, d_model)[:, g]
            w_g = jnp.concatenate([of(wq_t), of(wk_t), of(wv_t)], axis=1).reshape(chips * rows, d_model)
            d_normed = d_normed + jnp.stack(
                [dot(g_swap[b * chips:(b + 1) * chips].reshape(chips * rows, blk), w_g, TN) for b in range(batch)])

        d_normed = d_normed.astype(BF16).astype(F32)
        x_hat, inv_rms = norm_forward(x_local)
        d_x_norm = norm_backward(d_normed, x_hat, inv_rms, gain)
        d_gain = lax.psum(jnp.sum(d_normed * x_hat, axis=(0, 1)), 'sp')
        d_x = (dy_local.astype(F32) + d_x_norm).astype(BF16)
        back = lambda t, h: jnp.transpose(t.reshape(h, dim, d_model), (2, 0, 1))
        return (y_out, d_x, back(outs[0], num_q), back(outs[1], num_kv), back(outs[2], num_kv),
                d_wo.reshape(num_q, dim, d_model), d_gain)

    specs_in = (P('dp', 'sp', None), P('dp', 'sp', None), P(None), P(None, None, None), P(None, None, None), P(None, None, None), P(None, None, None))
    specs_out = (P('dp', 'sp', None), P('dp', 'sp', None), P('dp', None, None), P('dp', None, None), P('dp', None, None), P('dp', None, None), P('dp'))
    return jax.shard_map(local_step, mesh=mesh, in_specs=specs_in, out_specs=specs_out, check_vma=False)
```

time: 668 us -> 589 us (0.88)
  waiting for transfers between devices: 69.6 us -> 3.31 us
  other arithmetic: 30.4 us -> 11.8 us
  Pallas kernels: 489 us -> 497 us
    all_gather x3 -> x1, waiting for transfers between devices: 68.8 us -> 3.26 us  [local_step(): d_w1 = lax.all_gather(d_w1, 'sp', axis=0, tiled=True)]
    concatenate x2 -> x0, other arithmetic: 13.3 us -> none  [local_step(): w_all = jnp.concatenate([wq_t, wk_t, wv_t], axis=1)]
    pallas_call x7 -> x5, Pallas kernels: 470 us -> 478 us  [the longest x1 124 us: local_step(): call(functools.partial(first_backward_kernel, n, group, dim, count), (2 *...]
    squeeze x0 -> x2, local copies, waits for them, and re-layouts: none -> 6.88 us  [local_step(): of = lambda w: w.reshape(chips, CORES, -1, d_model)[:, g]]
  transfers between devices with their start and end apart: 3 -> 1, of which waited for: 1 -> 1; matrix products, arithmetic and copies ran while one was open for 7% -> 7% of each run, Pallas kernels for 18% -> 2%
where the time goes in v3:
time: 589 us; the launch traced here: 584 us
  Pallas kernels  497 us (84%)
  local copies, waits for them, and re-layouts  24.2 us (4%)
  matrix products  20.2 us (3%)
  between operations  14.8 us (3%)
  blocking collectives  12.3 us (2%)
  other arithmetic  11.8 us (2%)
    pallas_call x1, Pallas kernels, local_step(): call(functools.partial(first_backward_kernel, n, group, dim, count), (2 *...  124 us
    pallas_call x1, Pallas kernels, local_step(): call(functools.partial(project_kernel, n, group, dim), (), [ANY, vmem, AN...  118 us
    pallas_call x1, Pallas kernels, local_step(): call(functools.partial(forward_kernel, n, group, dim), (CORES * n,), [pl....  108 us
    pallas_call x1, Pallas kernels, local_step(): call(functools.partial(second_backward_kernel, n, group, dim, count), (co...  95.3 us
    pallas_call x1, Pallas kernels, local_step(): call(functools.partial(weight_grad_kernel, n, count), (count,), pair_spec...  32.9 us
    dot_general x6, matrix products, dot(): return lax.dot_general(a, b, dims, preferred_element_type=F32)  20.2 us
    pallas_call x2, Pallas kernels, local_step(): call(functools.partial(spread_kernel, rows_q, dim), (chips,), [pl.BlockSp...  19 us
    psum x1, blocking collectives, local_step(): d_gain = lax.psum(jnp.sum(d_normed * x_hat, axis=(0, 1)), 'sp')  12.3 us
  transfers between devices with their start and end apart: 1, of which 1 were waited for; matrix products, arithmetic and copies ran while one was open for 7% of the time, Pallas kernels for 2%

profile of v3, /device:TPU:113, one launch (start us, length us, event | category | flops | bytes accessed | tf_op | source)
XLA Modules:
  0.0 584.0 jit_solution(1168370648894299080)
XLA Ops:
  7.3 2.3 multiply_sine_fusion
  9.6 3.2 constant_dynamic-slice_fusion.w_ref
  12.8 118.1 %project.1 = (bf16[8,384,2048]{2,1,0:T(8,128)(2,1)}, bf16[8,384,2048]{2,1,0:T(8,128)(2,1)}, bf16[2,8,64,1536]{3,2,1,0:T(8,128)(2,1)}, bf16[2,3072,64]{2,1,0:T(8,...) custom-call(bf16[2,384,2048]{2,1,0:T(8,128)(2,1)} %x_hbm.1, ...), custom_call_target="tpu_custom_call" | custom-call | flops 38654705664 | bytes 1000000 | tf_op jit(solution)/shard_map/project/pallas_call | solution.py:625
  130.8 108.4 %forward.1 = (bf16[8,512,384]{2,1,0:T(8,128)(2,1)}, f32[2,8,1,1536]{3,2,1,0:T(1,128)}, bf16[8,384,2048]{2,1,0:T(8,128)(2,1)}) custom-call(bf16[2,8,64,1536]{3,2,1,0:T(8,128)(2,1)} %get-tuple-element.31.q_ref, bf16[2,3072,64]{2,1,0:T(8,128)(2,1)} %get-tuple-element.32.k_ref, bf16[2,64,3072]{2,1,0:T(8,128)(2,1)} %get-tuple-element.33.vt_ref, ...), custom_call_target="tpu_custom_call" | custom-call | flops 38654705664 | bytes 1000000 | tf_op jit(solution)/shard_map/forward/pallas_call | solution.py:636
  239.2 123.7 %backward_0.1 = (bf16[8,384,384]{2,1,0:T(8,128)(2,1)}, bf16[8,64,1536]{2,1,0:T(8,128)(2,1)}, bf16[8,512,384]{2,1,0:T(8,128)(2,1)}, f32[4,2,256,2048]{3,2,1,0:T(8,128)}) custom-call(bf16[8,384,2048]{2,1,0:T(8,128)(2,1)} %get-tuple-element.34.dy_ref, bf16[512,2048]{1,0:T(8,128)(2,1)} %constant_dynamic-slice_fusion.w_ref, ...), custom_call_target="tpu_custom_call" | custom-call | flops 61203283968 | bytes 1000000 | tf_op jit(solution)/shard_map/backward_0/pallas_call | solution.py:668
  362.9 95.3 %backward_1.1 = (bf16[8,384,384]{2,1,0:T(8,128)(2,1)}, bf16[8,384,384]{2,1,0:T(8,128)(2,1)}, f32[4,2,192,2048]{3,2,1,0:T(8,128)}) custom-call(bf16[8,384,384]{2,1,0:T(8,128)(2,1)} %get-tuple-element.40.g2_ref.g_hbm, bf16[8,384,384]{2,1,0:T(8,128)(2,1)} %get-tuple-element.40.g2_ref.g_hbm, bf16[8,384,2048]{2,1,0:T(8,128)(2,1)} %get-tuple-element.41.r_ref, ...), custom_call_target="tpu_custom_call" | custom-call | flops 53150220288 | bytes 1000000 | tf_op jit(solution)/shard_map/backward_1/pallas_call | solution.py:684
  458.2 32.9 %weight_grad.1 = (f32[192,2048]{1,0:T(8,128)}, bf16[8,384,384]{2,1,0:T(8,128)(2,1)}) custom-call(bf16[8,384,384]{2,1,0:T(8,128)(2,1)} %get-tuple-element.44.g2_ref.g_hbm, bf16[8,384,384]{2,1,0:T(8,128)(2,1)} %get-tuple-element.44.g2_ref.g_hbm, bf16[8,384,2048]{2,1,0:T(8,128)(2,1)} %get-tuple-element.41.r_ref), custom_call_target="tpu_custom_call" | custom-call | flops 4831838208 | bytes 1000000 | tf_op jit(solution)/shard_map/weight_grad/pallas_call | solution.py:692
  491.2 9.7 %spread.2 = (f32[8,256,2048]{2,1,0:T(8,128)}, f32[8,64,2048]{2,1,0:T(8,128)}, f32[8,64,2048]{2,1,0:T(8,128)}) custom-call(f32[4,384,2048]{2,1,0:T(8,128)} %bitcast.78), custom_call_target="tpu_custom_call" | custom-call | flops 1000000 | bytes 1000000 | tf_op jit(solution)/shard_map/spread/pallas_call | solution.py:705
  500.9 0.7 fusion.10
  501.6 2.7 slice_bitcast_fusion.4
  504.3 4.2 slice_bitcast_fusion.1
  508.5 2.7 convolution_bitcast_fusion
  511.2 2.7 convolution_bitcast_fusion.1
  513.9 2.7 convolution_bitcast_fusion.2
  516.5 2.7 convolution_bitcast_fusion.3
  519.2 3.6 fusion.8
  522.8 12.3 %psum.7 = f32[2048]{0:T(1024)} all-reduce(f32[2048]{0:T(1024)S(1)} %get-tuple-element.55), channel_id=1, replica_groups=mesh['dp'=2,'sp'=8] {'sp'}, use_global_device_ids=true, to_apply=%region_3.4 | all-reduce | flops 2048 | bytes 16384 | tf_op jit(solution)/shard_map/psum | solution.py:719
  535.1 2.4 fusion.17
  537.5 6.1 %convolution_bitcast_fusion.4 = f32[1,384,2048]{2,1,0:T(8,128)S(1)} fusion(bf16[2048,384]{1,0:T(8,128)(2,1)S(1)} %bitcast.81, bf16[2048,2048]{1,0:T(8,128)(2,1)} %bitcast.72), kind=kOutput, calls=%fused_computation.25 | convolution fusion | flops 3221225472 | bytes 13107200 | tf_op jit(solution)/shard_map/dot_general | solution.py:26
  543.6 3.5 convolution_bitcast_fusion.5
  547.1 5.2 fusion.6
  552.3 3.3 all-gather.2.cloned.1.call-done
  555.5 9.3 %spread.3 = (f32[8,256,2048]{2,1,0:T(8,128)}, f32[8,64,2048]{2,1,0:T(8,128)}, f32[8,64,2048]{2,1,0:T(8,128)}) custom-call(f32[4,384,2048]{2,1,0:T(8,128)} %bitcast.79, f32[8,256,2048]{2,1,0:T(8,128)} %get-tuple-element.48.refs_1_, f32[8,64,2048]{2,1,0:T(8,128)} %get-tuple-element.49.refs_2_, ...), custom_call_target="tpu_custom_call", output_to_operand_aliasing={{0}: (1, {}), {1}: (2, {}), {2}: (3, {})} | custom-call | flops 1000000 | bytes 1000000 | tf_op jit(solution)/shard_map/spread/pallas_call | solution.py:705
  564.9 11.8 %copy.49 = f32[32,64,2048]{2,1,0:T(8,128)} copy(f32[32,64,2048]{2,1,0:T(8,128)} %bitcast.76) | data formatting | bytes 33554432
  (23 shorter events, 0.2 us)
Async XLA Ops:
  7.2 548.4 %all-gather.2.cloned.1.call-start = ((), (), s32[]{:S(2)}) async-start(), calls=%async_computation | async-start | bytes 14155776 | tf_op jit(solution)/shard_map/all_gather | solution.py:696
  491.2 9.7 %copy-start = (bf16[2,384,2048]{2,1,0:T(8,128)(2,1)S(1)}, bf16[2,384,2048]{2,1,0:T(8,128)(2,1)}, u32[]{:S(2)}) copy-start(bf16[2,384,2048]{2,1,0:T(8,128)(2,1)} %x_hbm.1) | copy-start | bytes 9437188
  504.3 4.2 copy-start.4
  511.2 2.7 copy-start.5
  516.5 2.7 copy-start.3
  535.1 8.4 %slice-start = ((s8[8388608]{0:T(1024)(128)(4,1)}), s8[4194304]{0:T(1024)(128)(4,1)S(1)}, s32[]{:S(2)}) async-start(s8[8388608]{0:T(1024)(128)(4,1)} %bitcast.73), calls=%async_computation.1 | async-start | bytes 8388608
  537.5 6.1 %slice-start.1 = ((s8[8388608]{0:T(1024)(128)(4,1)}), s8[4194304]{0:T(1024)(128)(4,1)S(1)}, s32[]{:S(2)}) async-start(s8[8388608]{0:T(1024)(128)(4,1)} %bitcast.73), calls=%async_computation.2 | async-start | bytes 8388608
  543.6 3.5 copy-start.1
  543.6 3.5 copy-start.2
Sparse Core Ops, SparseCore 0:
  491.3 64.1 all-gather.1

commit v4 on v3

--- a/solution.py
+++ b/solution.py
@@ -115,36 +115,39 @@
     return c
 
 
-def project_kernel(n, group, dim, x_hbm, gain_ref, wq_hbm, wk_hbm, wv_hbm, cos_ref, sin_ref, x_all, r_all, q_ref, k_ref,
-                   kt_ref, v_ref, vt_ref, x_ref, r_ref, w_ref, load_sem, store_sem, w_sem, send_sem, recv_sem):
+def causal_mask(rows, cols, blk):
+    key = lax.broadcasted_iota(jnp.int32, (rows, cols), 0)
+    qry = lax.broadcasted_iota(jnp.int32, (rows, cols), 1) % blk
+    return key <= qry
+
+
+def forward_kernel(n, group, dim, x_hbm, dy_hbm, gain_ref, wq_hbm, wk_hbm, wv_hbm, cos_ref, sin_ref, o_ref, lse_ref,
+                   x_all, dy_all, r_all, q_hbm, k_hbm, kt_hbm, v_hbm, q_ref, k_ref, kt_ref, v_ref, vt_ref, x_ref, r_ref,
+                   w_ref, bounce_ref, acc_ref, m_ref, l_ref, load_sem, store_sem, w_sem, out_sem, x_send, x_recv, dy_send,
+                   dy_recv):
     half = dim // 2
     blk = x_ref.shape[0]
     rows_q = group * dim
     rows = rows_q + 2 * dim
-    ring = Ring(n, x_hbm, x_all, send_sem, recv_sem)
-    enter(ring.neighbours())
-    start(ring.direct(0) + ring.across())
-    weights = []
-    for g in range(CORES):
-        head = ring.chip * CORES + g
-        weights.append(pltpu.make_async_copy(wq_hbm.at[head], w_ref.at[pl.ds(g * rows, rows_q)], w_sem))
-        weights.append(pltpu.make_async_copy(wk_hbm.at[head], w_ref.at[pl.ds(g * rows + rows_q, dim)], w_sem))
-        weights.append(pltpu.make_async_copy(wv_hbm.at[head], w_ref.at[pl.ds(g * rows + rows_q + dim, dim)], w_sem))
-    start(weights)
+    ring = Ring(n, x_hbm, x_all, x_send, x_recv)
+    ring_dy = Ring(n, dy_hbm, dy_all, dy_send, dy_recv)
     order = ring.order()
-
-    def body(p, carry):
+    step_id = pl.program_id(0)
+    s = step_id - 1
+    keep = [pltpu.make_async_copy(q_ref, q_hbm, out_sem.at[0]), pltpu.make_async_copy(k_ref, k_hbm, out_sem.at[1]),
+            pltpu.make_async_copy(kt_ref, kt_hbm, out_sem.at[2]), pltpu.make_async_copy(v_ref, v_hbm, out_sem.at[3]),
+            pltpu.make_async_copy(bounce_ref, dy_all.at[ring.me], out_sem.at[4])]
+
+    def project(p, carry):
         slot = order[0]
         for k in range(1, n):
             slot = jnp.where(p == k, order[k], slot)
 
-        @pl.when(p == 0)
-        def _():
-            local(x_hbm.at[ring.core], x_ref, load_sem).wait()
-
         for k in range(1, n):
             @pl.when(p == k)
             def _(k=k):
+                if k == n - 1:
+                    start(ring_dy.direct(0) + ring_dy.across())
                 ring.wait_block(order[k])
                 if k == 3:
                     start(ring.relayed() + ring.direct(1))
@@ -158,12 +161,6 @@
         inv_rms = lax.rsqrt(jnp.mean(x * x, axis=-1, keepdims=True) + NORM_EPS)
         r_ref[...] = (x * inv_rms * gain_ref[...]).astype(BF16)
         pltpu.make_async_copy(r_ref, r_all.at[slot], store_sem).start()
-
-        @pl.when(p == 0)
-        def _():
-            for c in weights:
-                c.wait()
-
         off = pl.multiple_of(slot * blk, blk)
         cos_t = cos_ref[:, pl.ds(off, blk)]
         sin_t = sin_ref[:, pl.ds(off, blk)]
@@ -185,78 +182,78 @@
             v_ref[g, pl.ds(off, blk), :] = kv_t[:, dim:]
         return carry
 
-    lax.fori_loop(0, n, body, 0)
-    pltpu.make_async_copy(r_ref, r_all.at[ring.me], store_sem).wait()
-    ring.wait_sends()
-
-
-def causal_mask(rows, cols, blk):
-    key = lax.broadcasted_iota(jnp.int32, (rows, cols), 0)
-    qry = lax.broadcasted_iota(jnp.int32, (rows, cols), 1) % blk
-    return key <= qry
-
-
-def forward_kernel(n, group, dim, q_ref, k_ref, vt_ref, dy_hbm, o_ref, lse_ref, all_ref, acc_ref, m_ref, l_ref,
-                   bounce_ref, load_sem, send_sem, recv_sem):
-    blk = o_ref.shape[2]
-    step_id = pl.program_id(0)
-    i = step_id % n
-    c2 = dim ** -0.5 * LOG2E
-    ring = Ring(n, dy_hbm, all_ref, send_sem, recv_sem)
-    order = ring.order()
-
     @pl.when(step_id == 0)
     def _():
         enter(ring.neighbours())
         start(ring.direct(0) + ring.across())
+        weights = []
+        for g in range(CORES):
+            head = ring.chip * CORES + g
+            weights.append(pltpu.make_async_copy(wq_hbm.at[head], w_ref.at[pl.ds(g * rows, rows_q)], w_sem))
+            weights.append(pltpu.make_async_copy(wk_hbm.at[head], w_ref.at[pl.ds(g * rows + rows_q, dim)], w_sem))
+            weights.append(pltpu.make_async_copy(wv_hbm.at[head], w_ref.at[pl.ds(g * rows + rows_q + dim, dim)], w_sem))
+        start(weights)
+        local(x_hbm.at[ring.core], x_ref, load_sem).wait()
+        for c in weights:
+            c.wait()
+        lax.fori_loop(0, n, project, 0)
+        pltpu.make_async_copy(r_ref, r_all.at[ring.me], store_sem).wait()
         local(dy_hbm.at[ring.core], bounce_ref, load_sem).wait()
-        local(bounce_ref, all_ref.at[ring.me], load_sem)
-
-    @pl.when(step_id == n - 2)
-    def _():
-        start(ring.direct(1))
-
-    @pl.when(step_id == n)
-    def _():
-        ring.wait_block(order[2])
-        ring.wait_block(order[3])
-        start(ring.relayed())
-
-    acc_ref[...] = jnp.zeros_like(acc_ref)
-    l_ref[...] = jnp.zeros_like(l_ref)
-    m_ref[...] = jnp.full_like(m_ref, NEG)
-
-    def tile(j, masked):
-        off = pl.multiple_of(j * blk, blk)
-        s = dot(k_ref[0, pl.ds(off, blk), :], q_ref[0, 0])
-        if masked:
-            s = jnp.where(causal_mask(s.shape[0], s.shape[1], blk), s, NEG)
-        m_old = m_ref[...]
-        m_new = jnp.maximum(m_old, jnp.max(s, axis=0, keepdims=True) * c2)
-        p = jnp.exp2(s * c2 - m_new)
-        alpha = jnp.exp2(m_old - m_new)
-        m_ref[...] = m_new
-        l_ref[...] = l_ref[...] * alpha + jnp.sum(p, axis=0, keepdims=True)
-        acc_ref[...] = acc_ref[...] * alpha + dot(vt_ref[0, :, pl.ds(off, blk)], p.astype(BF16))
-
-    def step(j, carry):
-        tile(j, False)
-        return carry
-
-    lax.fori_loop(0, i, step, 0)
-    tile(i, True)
-    l_val = l_ref[...]
-    o = (acc_ref[...] * (1.0 / l_val)).astype(BF16)
-    for h in range(group):
-        o_ref[0, h * dim:(h + 1) * dim, :] = o[:, h * blk:(h + 1) * blk]
-    lse_ref[0, 0] = m_ref[...] + jnp.log2(l_val)
+        start(keep)
+
+    @pl.when(s == n - 2)
+    def _():
+        start(ring_dy.direct(1))
+
+    @pl.when(s == n)
+    def _():
+        ring_dy.wait_block(order[2])
+        ring_dy.wait_block(order[3])
+        start(ring_dy.relayed())
+
+    def attend():
+        g = s // n
+        i = s % n
+        c2 = dim ** -0.5 * LOG2E
+        acc_ref[...] = jnp.zeros_like(acc_ref)
+        l_ref[...] = jnp.zeros_like(l_ref)
+        m_ref[...] = jnp.full_like(m_ref, NEG)
+
+        def tile(j, masked):
+            off = pl.multiple_of(j * blk, blk)
+            sc = dot(k_ref[g, pl.ds(off, blk), :], q_ref[g, i])
+            if masked:
+                sc = jnp.where(causal_mask(sc.shape[0], sc.shape[1], blk), sc, NEG)
+            m_old = m_ref[...]
+            m_new = jnp.maximum(m_old, jnp.max(sc, axis=0, keepdims=True) * c2)
+            p = jnp.exp2(sc * c2 - m_new)
+            alpha = jnp.exp2(m_old - m_new)
+            m_ref[...] = m_new
+            l_ref[...] = l_ref[...] * alpha + jnp.sum(p, axis=0, keepdims=True)
+            acc_ref[...] = acc_ref[...] * alpha + dot(vt_ref[g, :, pl.ds(off, blk)], p.astype(BF16))
+
+        def step(j, carry):
+            tile(j, False)
+            return carry
+
+        lax.fori_loop(0, i, step, 0)
+        tile(i, True)
+        l_val = l_ref[...]
+        o = (acc_ref[...] * (1.0 / l_val)).astype(BF16)
+        for h in range(group):
+            o_ref[0, h * dim:(h + 1) * dim, :] = o[:, h * blk:(h + 1) * blk]
+        lse_ref[0, 0] = m_ref[...] + jnp.log2(l_val)
+
+    pl.when(s >= 0)(attend)
 
     @pl.when(step_id == pl.num_programs(0) - 1)
     def _():
-        pltpu.make_async_copy(bounce_ref, all_ref.at[ring.me], load_sem).wait()
+        for c in keep:
+            c.wait()
         for k in (1, 4, 5, 6, 7):
-            ring.wait_block(order[k])
+            ring_dy.wait_block(order[k])
         ring.wait_sends()
+        ring_dy.wait_sends()
 
 
 class Swap:
@@ -292,49 +289,63 @@
         self.chips = n // CORES
         me = lax.axis_index('sp')
         self.chip, self.core = me // CORES, me % CORES
-        self.cut = all_ref.shape[2] // 2
+        self.ahead = 1 - 2 * self.core
 
     def chip_at(self, hop):
         return (self.chip + hop + self.chips) % self.chips
 
-    def piece(self, hop, part):
-        ref = self.all.at[self.chip_at(hop), self.core]
-        if part is not None:
-            ref = ref.at[pl.ds(part * self.cut, self.cut)]
-        return ref
-
-    def copy(self, hop, part, send, recv, to):
-        ref = self.piece(hop, part)
-        core = 1 - self.core if to == 0 else self.core
+    def piece(self, hop):
+        return self.all.at[self.chip_at(hop), self.core]
+
+    def copy(self, hop, send, recv, to, core):
+        ref = self.piece(hop)
         return remote(ref, ref, self.send_sem.at[send], self.recv_sem.at[recv], self.chip_at(to) * CORES + core)
 
-    def direct(self):
-        return [self.copy(0, None, 0, 0, 1), self.copy(0, None, 1, 1, -1), self.copy(0, None, 2, 4, 0)]
+    def ring(self, hop, send, recv, to):
+        return self.copy(hop, send, recv, to, self.core)
+
+    def across(self, hop, send, recv):
+        return self.copy(hop, send, recv, 0, 1 - self.core)
+
+    def first(self):
+        return [self.ring(0, 0, 0, self.ahead), self.across(0, 1, 3)]
 
     def relay(self):
-        return [self.copy(-1, 0, 3, 2, 1), self.copy(1, 1, 4, 3, -1), self.copy(-1, None, 5, 5, 0), self.copy(1, None, 6, 6, 0)]
+        return [self.ring(-self.ahead, 2, 2, self.ahead), self.across(-self.ahead, 3, 4)]
+
+    def second(self):
+        return [self.ring(0, 4, 1, -self.ahead)]
+
+    def far(self):
+        return [self.across(2, 5, 6)]
 
     def last(self):
-        return [self.copy(2, 0, 7, 7, 0), self.copy(2, 1, 8, 8, 0)]
-
-    def wait_near(self):
-        self.copy(-1, None, 0, 0, 1).wait_recv()
-        self.copy(1, None, 0, 1, 1).wait_recv()
-
-    def wait_far(self):
-        self.copy(2, 0, 0, 2, 1).wait_recv()
-        self.copy(2, 1, 0, 3, 1).wait_recv()
-
-    def finish(self):
-        self.wait_far()
-        start(self.last())
-        for k, part in ((4, None), (5, None), (6, None), (7, 0), (8, 1)):
-            self.copy(0, part, 0, k, 1).wait_recv()
-        for c in self.direct() + self.relay() + self.last():
-            c.wait_send()
-
-
-SPREAD_SENDS = 9
+        return [self.across(self.ahead, 6, 5)]
+
+    def arrived(self, recv):
+        self.ring(0, 0, recv, 0).wait_recv()
+
+    def event(self, stage):
+        if stage == 0:
+            start(self.first())
+        elif stage == 1:
+            self.arrived(0)
+            start(self.relay())
+        elif stage == 2:
+            start(self.second())
+        elif stage == 3:
+            self.arrived(2)
+            start(self.far())
+        else:
+            self.arrived(1)
+            start(self.last())
+            for k in (3, 4, 5, 6):
+                self.arrived(k)
+            for c in self.first() + self.relay() + self.second() + self.far() + self.last():
+                c.wait_send()
+
+
+SPREAD_SENDS = 7
 
 
 def enter_all(n):
@@ -433,23 +444,29 @@
     out_ref[0, base + dim:base + 2 * dim, :] = dv_ref[:, pl.ds(off, blk)].astype(BF16)
 
 
-RELAY_AT = 5
-
-
-def first_backward_kernel(n, group, dim, count, dy_ref, w_ref, o2_ref, o_hbm, q_ref, o_ref, lse_ref, k_ref, kt_ref, v_ref,
+SPREAD_STEPS = ((1, 2), (2, 4), (3, 7))
+
+
+def first_backward_kernel(n, group, dim, count, dy_ref, w_hbm, o2_ref, o_hbm, q_ref, o_ref, lse_ref, k_ref, kt_ref, v_ref,
                           cos_ref, sin_ref, g_ref, do1_ref, swap_ref, dw_all, acc_ref, wide_ref, got_ref, mine_ref,
-                          do_ref, dq_ref, dk_ref, dv_ref, delta_ref, sem, pair_send, pair_recv, send_sem, recv_sem,
+                          w_ref, w_sem, do_ref, dq_ref, dk_ref, dv_ref, delta_ref, sem, pair_send, pair_recv, send_sem, recv_sem,
                           spread_send, spread_recv):
     s = pl.program_id(0)
     blk = g_ref.shape[2]
     swap = Swap(n, o_hbm, swap_ref, send_sem, recv_sem)
     spread = Spread(n, dw_all, spread_send, spread_recv)
     early = n // 2 - 1
+    w_copy = pltpu.make_async_copy(w_hbm.at[swap.me // CORES], w_ref, w_sem)
 
     @pl.when(s == 0)
     def _():
         enter_all(n)
         start(swap.sends()[:early])
+        w_copy.start()
+
+    @pl.when(s == count)
+    def _():
+        w_copy.wait()
 
     @pl.when(s < count)
     def _():
@@ -462,8 +479,8 @@
 
     @pl.when(s == count - 1)
     def _():
-        local(mine_ref, spread.piece(0, None), sem).wait()
-        start(spread.direct())
+        local(mine_ref, spread.piece(0), sem).wait()
+        spread.event(0)
         start(swap.sends()[early:])
 
     @pl.when((s >= count) & (s < 2 * count))
@@ -478,10 +495,10 @@
 
     t = s - 2 * count
 
-    @pl.when(t == RELAY_AT)
-    def _():
-        spread.wait_near()
-        start(spread.relay())
+    for stage, at in SPREAD_STEPS:
+        @pl.when(t == at)
+        def _(stage=stage):
+            spread.event(stage)
 
     @pl.when(t >= 0)
     def _():
@@ -490,7 +507,7 @@
 
     @pl.when(t == n - 1)
     def _():
-        spread.finish()
+        spread.event(4)
         swap.finish()
 
 
@@ -502,10 +519,12 @@
     swap = Swap(n, g_hbm, swap_ref, send_sem, recv_sem)
     spread = Spread(n, dw_all, spread_send, spread_recv)
 
+    early = n // 2 - 1
+
     @pl.when(s == 0)
     def _():
         enter_all(n)
-        start(swap.sends())
+        start(swap.sends()[:early])
 
     @pl.when(s < count)
     def _():
@@ -518,15 +537,16 @@
 
     @pl.when(s == count - 1)
     def _():
-        local(mine_ref, spread.piece(0, None), sem).wait()
-        start(spread.direct())
+        local(mine_ref, spread.piece(0), sem).wait()
+        spread.event(0)
+        start(swap.sends()[early:])
 
     t = s - count
 
-    @pl.when(t == RELAY_AT)
-    def _():
-        spread.wait_near()
-        start(spread.relay())
+    for stage, at in SPREAD_STEPS:
+        @pl.when(t == at)
+        def _(stage=stage):
+            spread.event(stage)
 
     @pl.when(t >= 0)
     def _():
@@ -535,7 +555,7 @@
 
     @pl.when(t == n - 1)
     def _():
-        spread.finish()
+        spread.event(4)
         swap.finish()
 
 
@@ -608,11 +628,8 @@
         rows = rows_q + 2 * dim
         cols = group * blk
         count = n // 2
-        me = lax.axis_index('sp')
-        chip = me // CORES
         sds = jax.ShapeDtypeStruct
         full = lambda *s: pl.BlockSpec(s, lambda i: (0,) * len(s))
-        vmem = pl.BlockSpec(memory_space=pltpu.VMEM)
 
         wq_t = jnp.transpose(w_q, (1, 2, 0)).reshape(n, rows_q, d_model)
         wk_t = jnp.transpose(w_k, (1, 2, 0)).reshape(n, dim, d_model)
@@ -622,29 +639,22 @@
         mm = 2.0 * seq * d_model
         att = 2.0 * seq * seq * dim * group / 2
 
-        _, r_all, q_t, k, k_t, v, v_t = call(
-            functools.partial(project_kernel, n, group, dim), (), [ANY, vmem, ANY, ANY, ANY, vmem, vmem],
-            [ANY, ANY, vmem, vmem, vmem, vmem, vmem],
-            [sds((n, blk, d_model), BF16), sds((n, blk, d_model), BF16), sds((CORES, n, dim, cols), BF16),
-             sds((CORES, seq, dim), BF16), sds((CORES, dim, seq), BF16), sds((CORES, seq, dim), BF16),
-             sds((CORES, dim, seq), BF16)],
-            'project', mm * rows * 8,
-            [pltpu.VMEM((blk, d_model), BF16), pltpu.VMEM((blk, d_model), BF16), pltpu.VMEM((CORES * rows, d_model), BF16),
-             DMA, DMA, DMA, DMA((RING_SENDS,)), DMA((n,))],
-            collective=0)(x_local, gain.reshape(1, d_model), wq_t, wk_t, wv_t, cos_t, sin_t)
-
-        o_all, lse, dy_all = call(
-            functools.partial(forward_kernel, n, group, dim), (CORES * n,),
-            [pl.BlockSpec((1, 1, dim, cols), lambda s: (s // n, s % n, 0, 0)),
-             pl.BlockSpec((1, seq, dim), lambda s: (s // n, 0, 0)),
-             pl.BlockSpec((1, dim, seq), lambda s: (s // n, 0, 0)), ANY],
-            [pl.BlockSpec((1, rows_q, blk), lambda s: (s % n, s // n, 0)),
-             pl.BlockSpec((1, 1, 1, cols), lambda s: (s // n, s % n, 0, 0)), ANY],
-            [sds((n, CORES * rows_q, blk), BF16), sds((CORES, n, 1, cols), F32), sds((n, blk, d_model), BF16)],
-            'forward', att * 16,
-            [pltpu.VMEM((dim, cols), F32), pltpu.VMEM((1, cols), F32), pltpu.VMEM((1, cols), F32),
-             pltpu.VMEM((blk, d_model), BF16), DMA, DMA((RING_SENDS,)), DMA((n,))],
-            collective=1)(q_t, k, v_t, dy_local)
+        at = lambda s: jnp.maximum(s - 1, 0)
+        kept = [sds((CORES, n, dim, cols), BF16), sds((CORES, seq, dim), BF16), sds((CORES, dim, seq), BF16),
+                sds((CORES, seq, dim), BF16)]
+        blocks = sds((n, blk, d_model), BF16)
+        o_all, lse, _, dy_all, r_all, q_t, k, k_t, v = call(
+            functools.partial(forward_kernel, n, group, dim), (1 + CORES * n,),
+            [ANY, ANY, full(1, d_model), ANY, ANY, ANY, full(half, seq), full(half, seq)],
+            [pl.BlockSpec((1, rows_q, blk), lambda s: (at(s) % n, at(s) // n, 0)),
+             pl.BlockSpec((1, 1, 1, cols), lambda s: (at(s) // n, at(s) % n, 0, 0))] + [ANY] * 7,
+            [sds((n, CORES * rows_q, blk), BF16), sds((CORES, n, 1, cols), F32), blocks, blocks, blocks] + kept,
+            'forward', att * 16 + mm * rows * 2,
+            [pltpu.VMEM(t.shape, t.dtype) for t in kept] + [pltpu.VMEM((CORES, dim, seq), BF16)] +
+            [pltpu.VMEM((blk, d_model), BF16)] * 2 + [pltpu.VMEM((CORES * rows, d_model), BF16), pltpu.VMEM((blk, d_model), BF16)] +
+            [pltpu.VMEM((dim, cols), F32), pltpu.VMEM((1, cols), F32), pltpu.VMEM((1, cols), F32), DMA, DMA, DMA, DMA((5,)),
+             DMA((RING_SENDS,)), DMA((n,)), DMA((RING_SENDS,)), DMA((n,))],
+            collective=0)(x_local, dy_local, gain.reshape(1, d_model), wq_t, wk_t, wv_t, cos_t, sin_t)
 
         def backward_specs(g, lead):
             step = lambda s: n - 1 - jnp.maximum(s - lead, 0)
@@ -668,14 +678,14 @@
         g_0, d_o1, o_swap, d_wo = call(
             functools.partial(first_backward_kernel, n, group, dim, count), (2 * count + n,),
             [pl.BlockSpec((2, blk, d_model), lambda s: (jnp.where(s < count, s, jnp.minimum(s - count, count - 1)), 0, 0)),
-             full(CORES * rows_q, d_model), pl.BlockSpec((2, CORES * rows_q, blk), lambda s: (pair(s), 0, 0)), ANY] + list(ins.values()),
+             ANY, pl.BlockSpec((2, CORES * rows_q, blk), lambda s: (pair(s), 0, 0)), ANY] + list(ins.values()),
             [g_spec, full(n, dim, cols), ANY, ANY],
             [sds((n, rows, blk), BF16), sds((n, dim, cols), BF16), sds((n, CORES * rows_q, blk), BF16),
              sds((chips, CORES, rows_q, d_model), F32)],
             'backward_0', att * 20 + mm * rows_q * 4,
-            sum_scratch(CORES * rows_q, True) + [pltpu.VMEM((n, dim, cols), BF16)] + back_scratch + swap_sems + spread_sems,
-            collective=2)(dy_all, lax.dynamic_slice_in_dim(wo_flat, chip * CORES * rows_q, CORES * rows_q, 0), o_all, o_all,
-                          q_t, o_all, lse, k, k_t, v, cos_t, sin_t)
+            sum_scratch(CORES * rows_q, True) + [pltpu.VMEM((CORES * rows_q, d_model), BF16), DMA, pltpu.VMEM((n, dim, cols), BF16)] + back_scratch + swap_sems + spread_sems,
+            collective=2)(dy_all, wo_flat.reshape(chips, CORES * rows_q, d_model), o_all, o_all, q_t,
+                          o_all, lse, k, k_t, v, cos_t, sin_t)
 
         ins, g_spec = backward_specs(1, count)
         pair_specs = [pl.BlockSpec((2, rows, blk), lambda s: (pair(s), 0, 0)), ANY,

time: 589 us -> 584 us (level)
    pallas_call x2 -> x1, Pallas kernels: 226 us -> 221 us  [local_step(): call(functools.partial(forward_kernel, n, group, dim), (1 + CORES * n,),...]
where the time goes in v4:
time: 584 us; the launch traced here: 579 us
  Pallas kernels  495 us (85%)
  local copies, waits for them, and re-layouts  21.1 us (4%)
  matrix products  20.2 us (3%)
  between operations  14.7 us (3%)
  blocking collectives  12.5 us (2%)
  other arithmetic  11.8 us (2%)
    pallas_call x1, Pallas kernels, local_step(): call(functools.partial(forward_kernel, n, group, dim), (1 + CORES * n,),...  221 us
    pallas_call x1, Pallas kernels, local_step(): call(functools.partial(first_backward_kernel, n, group, dim, count), (2 *...  125 us
    pallas_call x1, Pallas kernels, local_step(): call(functools.partial(second_backward_kernel, n, group, dim, count), (co...  97.1 us
    pallas_call x1, Pallas kernels, local_step(): call(functools.partial(weight_grad_kernel, n, count), (count,), pair_spec...  33.2 us
    dot_general x6, matrix products, dot(): return lax.dot_general(a, b, dims, preferred_element_type=F32)  20.2 us
    pallas_call x2, Pallas kernels, local_step(): call(functools.partial(spread_kernel, rows_q, dim), (chips,), [pl.BlockSp...  19 us
    psum x1, blocking collectives, local_step(): d_gain = lax.psum(jnp.sum(d_normed * x_hat, axis=(0, 1)), 'sp')  12.5 us
    unnamed x17, local copies, waits for them, and re-layouts  11.8 us
  transfers between devices with their start and end apart: 1, of which 1 were waited for; matrix products, arithmetic and copies ran while one was open for 7% of the time, Pallas kernels for 2%

profile of v4, /device:TPU:113, one launch (start us, length us, event | category | flops | bytes accessed | tf_op | source)
XLA Modules:
  0.0 578.9 jit_solution(8444417099969403042)
XLA Ops:
  7.2 0.1 all-gather.2.cloned.1.call-start
  7.3 2.3 multiply_sine_fusion
  9.6 220.6 %forward.1 = (bf16[8,512,384]{2,1,0:T(8,128)(2,1)}, f32[2,8,1,1536]{3,2,1,0:T(1,128)}, bf16[8,384,2048]{2,1,0:T(8,128)(2,1)}, bf16[8,384,2048]{2,1,0:T(8,128)(2,...) custom-call(bf16[2,384,2048]{2,1,0:T(8,128)(2,1)} %x_hbm.1, ...), custom_call_target="tpu_custom_call" | custom-call | flops 48318382080 | bytes 1000000 | tf_op jit(solution)/shard_map/forward/pallas_call | solution.py:646
  230.1 125.4 %backward_0.1 = (bf16[8,384,384]{2,1,0:T(8,128)(2,1)}, bf16[8,64,1536]{2,1,0:T(8,128)(2,1)}, bf16[8,512,384]{2,1,0:T(8,128)(2,1)}, f32[4,2,256,2048]{3,2,1,0:T(8,128)}) custom-call(bf16[8,384,2048]{2,1,0:T(8,128)(2,1)} %get-tuple-element.30.dy_ref, bf16[4,512,2048]{2,1,0:T(8,128)(2,1)} %bitcast.72, ...), custom_call_target="tpu_custom_call" | custom-call | flops 61203283968 | bytes 1000000 | tf_op jit(solution)/shard_map/backward_0/pallas_call | solution.py:678
  355.5 97.1 %backward_1.1 = (bf16[8,384,384]{2,1,0:T(8,128)(2,1)}, bf16[8,384,384]{2,1,0:T(8,128)(2,1)}, f32[4,2,192,2048]{3,2,1,0:T(8,128)}) custom-call(bf16[8,384,384]{2,1,0:T(8,128)(2,1)} %get-tuple-element.38.g2_ref.g_hbm, bf16[8,384,384]{2,1,0:T(8,128)(2,1)} %get-tuple-element.38.g2_ref.g_hbm, bf16[8,384,2048]{2,1,0:T(8,128)(2,1)} %get-tuple-element.39.r_ref, ...), custom_call_target="tpu_custom_call" | custom-call | flops 53150220288 | bytes 1000000 | tf_op jit(solution)/shard_map/backward_1/pallas_call | solution.py:694
  452.7 33.2 %weight_grad.1 = (f32[192,2048]{1,0:T(8,128)}, bf16[8,384,384]{2,1,0:T(8,128)(2,1)}) custom-call(bf16[8,384,384]{2,1,0:T(8,128)(2,1)} %get-tuple-element.42.g2_ref.g_hbm, bf16[8,384,384]{2,1,0:T(8,128)(2,1)} %get-tuple-element.42.g2_ref.g_hbm, bf16[8,384,2048]{2,1,0:T(8,128)(2,1)} %get-tuple-element.39.r_ref), custom_call_target="tpu_custom_call" | custom-call | flops 4831838208 | bytes 1000000 | tf_op jit(solution)/shard_map/weight_grad/pallas_call | solution.py:702
  485.8 0.1 all-gather.2.cloned.1.call-update
  485.9 9.7 %spread.2 = (f32[8,256,2048]{2,1,0:T(8,128)}, f32[8,64,2048]{2,1,0:T(8,128)}, f32[8,64,2048]{2,1,0:T(8,128)}) custom-call(f32[4,384,2048]{2,1,0:T(8,128)} %bitcast.79), custom_call_target="tpu_custom_call" | custom-call | flops 1000000 | bytes 1000000 | tf_op jit(solution)/shard_map/spread/pallas_call | solution.py:715
  495.6 0.7 fusion.10
  496.3 2.7 slice_bitcast_fusion.4
  499.0 4.2 slice_bitcast_fusion.1
  503.2 2.7 convolution_bitcast_fusion
  505.9 2.7 convolution_bitcast_fusion.1
  508.6 2.7 convolution_bitcast_fusion.2
  511.3 2.7 convolution_bitcast_fusion.3
  513.9 3.6 fusion.8
  517.5 12.5 %psum.7 = f32[2048]{0:T(1024)} all-reduce(f32[2048]{0:T(1024)S(1)} %get-tuple-element.53), channel_id=1, replica_groups=mesh['dp'=2,'sp'=8] {'sp'}, use_global_device_ids=true, to_apply=%region_3.0 | all-reduce | flops 2048 | bytes 16384 | tf_op jit(solution)/shard_map/psum | solution.py:729
  530.1 2.4 fusion.17
  532.4 6.0 %convolution_bitcast_fusion.4 = f32[1,384,2048]{2,1,0:T(8,128)S(1)} fusion(bf16[2048,384]{1,0:T(8,128)(2,1)S(1)} %bitcast.82, bf16[2048,2048]{1,0:T(8,128)(2,1)} %bitcast.73), kind=kOutput, calls=%fused_computation.25 | convolution fusion | flops 3221225472 | bytes 13107200 | tf_op jit(solution)/shard_map/dot_general | solution.py:26
  538.5 3.5 convolution_bitcast_fusion.5
  542.1 5.2 fusion.6
  547.2 3.3 all-gather.2.cloned.1.call-done
  550.5 9.3 %spread.3 = (f32[8,256,2048]{2,1,0:T(8,128)}, f32[8,64,2048]{2,1,0:T(8,128)}, f32[8,64,2048]{2,1,0:T(8,128)}) custom-call(f32[4,384,2048]{2,1,0:T(8,128)} %bitcast.80, f32[8,256,2048]{2,1,0:T(8,128)} %get-tuple-element.46.refs_1_, f32[8,64,2048]{2,1,0:T(8,128)} %get-tuple-element.47.refs_2_, ...), custom_call_target="tpu_custom_call", output_to_operand_aliasing={{0}: (1, {}), {1}: (2, {}), {2}: (3, {})} | custom-call | flops 1000000 | bytes 1000000 | tf_op jit(solution)/shard_map/spread/pallas_call | solution.py:715
  559.8 11.8 %copy.49 = f32[32,64,2048]{2,1,0:T(8,128)} copy(f32[32,64,2048]{2,1,0:T(8,128)} %bitcast.77) | data formatting | bytes 33554432
  (21 shorter events, 0.1 us)
Async XLA Ops:
  7.2 543.3 %all-gather.2.cloned.1.call-start = ((), (), s32[]{:S(2)}) async-start(), calls=%async_computation | async-start | bytes 14155776 | tf_op jit(solution)/shard_map/all_gather | solution.py:706
  485.9 9.7 %copy-start = (bf16[2,384,2048]{2,1,0:T(8,128)(2,1)S(1)}, bf16[2,384,2048]{2,1,0:T(8,128)(2,1)}, u32[]{:S(2)}) copy-start(bf16[2,384,2048]{2,1,0:T(8,128)(2,1)} %x_hbm.1) | copy-start | bytes 9437188
  499.0 4.2 copy-start.4
  505.9 2.7 copy-start.5
  511.3 2.7 copy-start.3
  530.1 8.4 %slice-start = ((s8[8388608]{0:T(1024)(128)(4,1)}), s8[4194304]{0:T(1024)(128)(4,1)S(1)}, s32[]{:S(2)}) async-start(s8[8388608]{0:T(1024)(128)(4,1)} %bitcast.74), calls=%async_computation.1 | async-start | bytes 8388608
  532.4 6.1 %slice-start.1 = ((s8[8388608]{0:T(1024)(128)(4,1)}), s8[4194304]{0:T(1024)(128)(4,1)S(1)}, s32[]{:S(2)}) async-start(s8[8388608]{0:T(1024)(128)(4,1)} %bitcast.74), calls=%async_computation.2 | async-start | bytes 8388608
  538.5 3.5 copy-start.1
  538.5 3.5 copy-start.2
Sparse Core Ops, SparseCore 0:
  486.0 64.4 all-gather.1
